TPU v7x, 256 devices: a whole 4x4x8 slice. The times are simulated.
256 devices in a mesh: trial: 4 (over z_lo), lat: 2 (over z_hi), lon: 4 (over x_hi, core), lev: 8 (over y, x_lo).
Axes of the slice: x: 4 (x_hi: 2, x_lo: 2; x = x_hi * 2 + x_lo), y: 4, z: 8 (z_hi: 2, z_lo: 4; z = z_hi * 4 + z_lo), core: 2. Of those that a mesh axis runs over, the one named last changes fastest.
Arguments:
- density: float32 [32, 64, 1024, 128], P(('trial', 'lat'), 'lon', 'lev'), parts along dimension 0, may hold values from 0.5 to 2
- crowding: float32 [32, 64, 1024, 128], P(('trial', 'lat'), 'lon', 'lev'), parts along dimension 0, may hold values from 0.5 to 2
Outputs:
- scaled_field: float32 [32, 64, 1024, 128], P(('trial', 'lat'), 'lon', 'lev'), parts along dimension 0
- density_end: float32 [32, 64, 1024, 128], P(('trial', 'lat'), 'lon', 'lev'), parts along dimension 0
There are 4 independent parts, one for each index of `trial`. A program takes and returns all parts, laid end to end along the dimension named above; each array names one. Nothing has to cross between parts.
All inputs are finite; a program needn't handle non-finite values.
Results may differ from a plain program's by a relative error of at most 0.000058.
Values sent between devices are 32-bit elements; how exact they have to be, the bound alone decides.
No kernel may reach another device: no remote copies, remote signals or barrier semaphores. Data moves between devices by JAX's collectives and lax.ppermute only.
A program may use at most 64 MiB of HBM per device.

v0:
```python
import jax
import jax.numpy as jnp
from jax import lax
from jax.sharding import PartitionSpec as P

STEPS = 4


def with_halo(array, sides, width):
    edges = {}
    for axis, dim in sides:
        devices, length = (lax.axis_size(axis), array.shape[dim])
        up = [(i, (i + 1) % devices) for i in range(devices - 1)]
        last = lax.slice_in_dim(array, length - width, length, axis=dim)
        first = lax.slice_in_dim(array, 0, width, axis=dim)
        edges[dim] = (
            lax.ppermute(last, axis, up),
            lax.ppermute(first, axis, [(b, a) for a, b in up]),
        )
    done = []
    for _, dim in sides:
        low, high = edges[dim]
        around = [(width, width) if d in done else (0, 0) for d in range(array.ndim)]
        array = jnp.concatenate([jnp.pad(low, around), array, jnp.pad(high, around)], axis=dim)
        done.append(dim)
    return array


def from_everyone(array, axis):
    devices = lax.axis_size(axis)
    return lax.all_to_all(
        jnp.broadcast_to(array[None], (devices, *array.shape)), axis, 0, 0, tiled=True
    )


def taken_together(array, axis):
    everything = from_everyone(array, axis)
    return jnp.sum(everything, axis=0)


def in_one(arrays, axis):
    line, at, done = (jnp.concatenate([a.reshape(-1) for a in arrays]), 0, [])
    so_far = taken_together(line, axis)
    for a in arrays:
        done.append(so_far[at : at + a.size].reshape(a.shape))
        at += a.size
    return tuple(done)


def inner_cells(values, dims):
    for dim in dims:
        values = lax.slice_in_dim(values, 1, values.shape[dim] - 1, axis=dim)
    return values


def side_cells(values, dim, start, dims):
    others = [other for other in dims if other != dim]
    values = inner_cells(values, others)
    return lax.slice_in_dim(values, start, start + values.shape[dim] - 2, axis=dim)


def advance(padded, crowding):
    middle = inner_cells(padded, (0, 1, 2))
    lower = [side_cells(padded, dim, 0, (0, 1, 2)) for dim in (0, 1, 2)]
    upper = [side_cells(padded, dim, 2, (0, 1, 2)) for dim in (0, 1, 2)]
    spread = lower[0] + upper[0] + lower[1] + upper[1] + lower[2] + upper[2] - 6.0 * middle
    return middle + 0.1 * spread + 0.2 * middle * (1.0 - middle * crowding)


def shards(density, crowding):
    for step in range(STEPS):
        padded = with_halo(density, (("lat", 0), ("lon", 1), ("lev", 2)), 1)
        density = advance(padded, crowding)
    count = density.shape[1] * lax.axis_size("lon")
    guess = 1.0
    moved = density - guess
    totals, squares = in_one(
        (jnp.sum(moved, axis=1, keepdims=True), jnp.sum(moved * moved, axis=1, keepdims=True)),
        "lon",
    )
    line_mean = guess + totals / count
    centred = density - line_mean
    line_variance = squares / count - totals / count * (totals / count)
    scaled_field = centred * lax.rsqrt(line_variance + 0.0001)
    return (scaled_field, density)


def solution(mesh):
    placed = (P(("trial", "lat"), "lon", "lev", None), P(("trial", "lat"), "lon", "lev", None))
    return jax.shard_map(
        shards,
        mesh=mesh,
        in_specs=placed,
        out_specs=(
            P(("trial", "lat"), "lon", "lev", None),
            P(("trial", "lat"), "lon", "lev", None),
        ),
        check_vma=False,
    )
```

profile of v0, /device:TPU:1, one launch (start us, length us, event | category | flops | bytes accessed | tf_op | source)
XLA Modules:
  0.0 274.8 jit_solution(10510386888826523579)
XLA Ops:
  0.6 1.8 fusion.60
  2.5 9.8 %collective-permute-start = (f32[1,16,128,128]{3,2,1,0:T(8,128)S(1)}, f32[1,16,128,128]{3,2,1,0:T(8,128)S(1)}, u32[]{:S(2)}, u32[]{:S(2)}) collective-permute-start(f32[1,16,128,128]{3,2,1,0:T(8,128)S(1)} %get-tuple-element.28), channel_id=1, source_target_pairs={{0,32},{1,33},{2,34},{3,35},{4,36},{5,37},{6,38},{7,39},{8,40},{9,... | collective-permute-start | bytes 3145736 | tf_op jit(solution)/shard_map/ppermute | solution.py:17
  12.3 1.3 collective-permute-start.1
  13.7 5.5 %collective-permute-start.2 = (f32[4,1,128,128]{3,2,1,0:T(8,128)S(1)}, f32[4,1,128,128]{3,2,1,0:T(8,128)S(1)}, u32[]{:S(2)}, u32[]{:S(2)}) collective-permute-start(f32[4,1,128,128]{3,2,1,0:T(8,128)S(1)} %get-tuple-element.25), channel_id=1, source_target_pairs={{0,8},{8,16},{16,24},{1,9},{9,17},{17,25},{2,10},{10,18},{18,26},{... | collective-permute-start | bytes 786440 | tf_op jit(solution)/shard_map/ppermute | solution.py:17
  19.2 1.9 collective-permute-start.3
  21.2 2.2 collective-permute-start.4
  23.4 0.0 collective-permute-done.2
  23.4 1.3 collective-permute-start.5
  24.7 3.9 %collective-permute-done.3 = f32[4,1,128,128]{3,2,1,0:T(8,128)S(1)} collective-permute-done((f32[4,1,128,128]{3,2,1,0:T(8,128)S(1)}, f32[4,1,128,128]{3,2,1,0:T(8,128)S(1)}, u32[]{:S(2)}, u32[]{:S(2)}) %collective-permute-start.3) | collective-permute-done | bytes 262176 | tf_op jit(solution)/shard_map/ppermute | solution.py:18
  28.7 10.0 %collective-permute-done = f32[1,16,128,128]{3,2,1,0:T(8,128)S(1)} collective-permute-done((f32[1,16,128,128]{3,2,1,0:T(8,128)S(1)}, f32[1,16,128,128]{3,2,1,0:T(8,128)S(1)}, u32[]{:S(2)}, u32[]{:S(2)}) %collective-permute-start) | collective-permute-done | bytes 1048608 | tf_op jit(solution)/shard_map/ppermute | solution.py:17
  38.7 1.0 constant_dynamic-update-slice_fusion.2
  39.8 2.4 constant_dynamic-update-slice_fusion.1
  42.2 21.4 %collective-permute-done.1 = f32[1,16,128,128]{3,2,1,0:T(8,128)S(1)} collective-permute-done((f32[1,16,128,128]{3,2,1,0:T(8,128)S(1)}, f32[1,16,128,128]{3,2,1,0:T(8,128)S(1)}, u32[]{:S(2)}, u32[]{:S(2)}) %collective-permute-start.1) | collective-permute-done | bytes 1048608 | tf_op jit(solution)/shard_map/ppermute | solution.py:18
  63.5 1.1 constant_dynamic-update-slice_fusion
  64.7 0.0 collective-permute-done.4
  64.7 0.2 copy-done.2
  64.8 0.0 collective-permute-done.5
  64.8 9.2 %fusion.38 = f32[4,16,128,128]{3,2,1,0:T(8,128)S(1)} fusion(f32[4,16,128,128]{3,2,1,0:T(8,128)S(1)} %copy-done.1, f32[4,16,1,128]{3,2,1,0:T(1,128)S(1)} %collective-permute-done.5, f32[6,1,128,128]{3,2,1,0:T(8,128)S(1)} %pad.51, f32[6,16,128,128]{3,2,1,0:T(8,128)} %constant_dynamic-update-slice_fusion, f32[6,1,128,128]{3,2,1,0:T(8,128)S(1)} %pad.50, ...), kind=kLoop, calls=%fused_computation.93 | loop fusion | flops 31457280 | bytes 21823488 | tf_op jit(solution)/shard_map/add | solution.py:67
  74.0 0.2 fusion.56
  74.2 1.4 collective-permute-start.6
  75.6 1.3 collective-permute-start.7
  76.9 6.5 %collective-permute-start.8 = (f32[4,1,128,128]{3,2,1,0:T(8,128)S(1)}, f32[4,1,128,128]{3,2,1,0:T(8,128)S(1)}, u32[]{:S(2)}, u32[]{:S(2)}) collective-permute-start(f32[4,1,128,128]{3,2,1,0:T(8,128)S(1)} %get-tuple-element.21), channel_id=1, source_target_pairs={{0,8},{8,16},{16,24},{1,9},{9,17},{17,25},{2,10},{10,18},{18,26},{... | collective-permute-start | bytes 786440 | tf_op jit(solution)/shard_map/ppermute | solution.py:17
  83.5 1.9 collective-permute-start.9
  85.4 2.2 collective-permute-start.10
  87.7 0.0 collective-permute-done.8
  87.7 1.3 collective-permute-start.11
  89.0 3.9 %collective-permute-done.9 = f32[4,1,128,128]{3,2,1,0:T(8,128)S(1)} collective-permute-done((f32[4,1,128,128]{3,2,1,0:T(8,128)S(1)}, f32[4,1,128,128]{3,2,1,0:T(8,128)S(1)}, u32[]{:S(2)}, u32[]{:S(2)}) %collective-permute-start.9) | collective-permute-done | bytes 262176 | tf_op jit(solution)/shard_map/ppermute | solution.py:18
  93.0 0.0 collective-permute-done.10
  93.0 0.4 collective-permute-done.11
  93.3 3.1 %collective-permute-done.6 = f32[1,16,128,128]{3,2,1,0:T(8,128)S(1)} collective-permute-done((f32[1,16,128,128]{3,2,1,0:T(8,128)S(1)}, f32[1,16,128,128]{3,2,1,0:T(8,128)S(1)}, u32[]{:S(2)}, u32[]{:S(2)}) %collective-permute-start.6) | collective-permute-done | bytes 1048608 | tf_op jit(solution)/shard_map/ppermute | solution.py:17
  96.4 7.9 %collective-permute-done.7 = f32[1,16,128,128]{3,2,1,0:T(8,128)S(1)} collective-permute-done((f32[1,16,128,128]{3,2,1,0:T(8,128)S(1)}, f32[1,16,128,128]{3,2,1,0:T(8,128)S(1)}, u32[]{:S(2)}, u32[]{:S(2)}) %collective-permute-start.7) | collective-permute-done | bytes 1048608 | tf_op jit(solution)/shard_map/ppermute | solution.py:18
  104.4 8.1 %fusion.27 = f32[4,16,128,128]{3,2,1,0:T(8,128)S(1)} fusion(f32[4,16,128,128]{3,2,1,0:T(8,128)S(1)} %fusion.38, f32[4,16,1,128]{3,2,1,0:T(1,128)S(1)} %collective-permute-done.11, f32[6,1,128,128]{3,2,1,0:T(8,128)S(1)} %pad.55, f32[6,1,128,128]{3,2,1,0:T(8,128)S(1)} %pad.54, f32[1,16,128,128]{3,2,1,0:T(8,128)S(1)} %collective-permute-done.7, ...), kind=kLoop, calls=%fused_computation.64 | loop fusion | flops 39845888 | bytes 15532032 | tf_op jit(solution)/shard_map/add | solution.py:67
  112.5 0.1 fusion.53
  112.6 1.4 collective-permute-start.12
  114.0 1.3 collective-permute-start.13
  115.3 31.9 %collective-permute-start.14 = (f32[4,1,128,128]{3,2,1,0:T(8,128)S(1)}, f32[4,1,128,128]{3,2,1,0:T(8,128)S(1)}, u32[]{:S(2)}, u32[]{:S(2)}) collective-permute-start(f32[4,1,128,128]{3,2,1,0:T(8,128)S(1)} %get-tuple-element.15), channel_id=1, source_target_pairs={{0,8},{8,16},{16,24},{1,9},{9,17},{17,25},{2,10},{10,18},{18,26},{... | collective-permute-start | bytes 786440 | tf_op jit(solution)/shard_map/ppermute | solution.py:17
  147.2 1.9 collective-permute-start.15
  149.2 2.2 collective-permute-start.16
  151.4 0.0 collective-permute-done.14
  151.4 1.3 collective-permute-start.17
  152.8 3.9 %collective-permute-done.15 = f32[4,1,128,128]{3,2,1,0:T(8,128)S(1)} collective-permute-done((f32[4,1,128,128]{3,2,1,0:T(8,128)S(1)}, f32[4,1,128,128]{3,2,1,0:T(8,128)S(1)}, u32[]{:S(2)}, u32[]{:S(2)}) %collective-permute-start.15) | collective-permute-done | bytes 262176 | tf_op jit(solution)/shard_map/ppermute | solution.py:18
  156.7 0.0 collective-permute-done.16
  156.8 0.4 collective-permute-done.17
  157.1 0.0 collective-permute-done.12
  157.1 8.1 %fusion.16 = f32[4,16,128,128]{3,2,1,0:T(8,128)S(1)} fusion(f32[4,16,128,128]{3,2,1,0:T(8,128)S(1)} %fusion.27, f32[4,16,1,128]{3,2,1,0:T(1,128)S(1)} %collective-permute-done.17, f32[6,1,128,128]{3,2,1,0:T(8,128)S(1)} %pad.59, f32[6,1,128,128]{3,2,1,0:T(8,128)S(1)} %pad.58, f32[1,16,128,128]{3,2,1,0:T(8,128)S(1)} %collective-permute-done.13, ...), kind=kLoop, calls=%fused_computation.35 | loop fusion | flops 39845888 | bytes 15532032 | tf_op jit(solution)/shard_map/add | solution.py:67
  165.2 0.2 fusion.51
  165.4 8.3 %collective-permute-start.18 = (f32[1,16,128,128]{3,2,1,0:T(8,128)S(1)}, f32[1,16,128,128]{3,2,1,0:T(8,128)S(1)}, u32[]{:S(2)}, u32[]{:S(2)}) collective-permute-start(f32[1,16,128,128]{3,2,1,0:T(8,128)S(1)} %get-tuple-element.9), channel_id=1, source_target_pairs={{0,32},{1,33},{2,34},{3,35},{4,36},{5,37},{6,38},{7,39},{8,40},{9,... | collective-permute-start | bytes 3145736 | tf_op jit(solution)/shard_map/ppermute | solution.py:17
  173.8 1.3 collective-permute-start.19
  175.1 27.3 %collective-permute-start.20 = (f32[4,1,128,128]{3,2,1,0:T(8,128)S(1)}, f32[4,1,128,128]{3,2,1,0:T(8,128)S(1)}, u32[]{:S(2)}, u32[]{:S(2)}) collective-permute-start(f32[4,1,128,128]{3,2,1,0:T(8,128)S(1)} %get-tuple-element.7), channel_id=1, source_target_pairs={{0,8},{8,16},{16,24},{1,9},{9,17},{17,25},{2,10},{10,18},{18,26},{... | collective-permute-start | bytes 786440 | tf_op jit(solution)/shard_map/ppermute | solution.py:17
  202.4 1.9 collective-permute-start.21
  204.4 1.3 collective-permute-start.22
  205.7 0.0 collective-permute-done.20
  205.7 1.3 collective-permute-start.23
  207.0 4.6 %collective-permute-done.21 = f32[4,1,128,128]{3,2,1,0:T(8,128)S(1)} collective-permute-done((f32[4,1,128,128]{3,2,1,0:T(8,128)S(1)}, f32[4,1,128,128]{3,2,1,0:T(8,128)S(1)}, u32[]{:S(2)}, u32[]{:S(2)}) %collective-permute-start.21) | collective-permute-done | bytes 262176 | tf_op jit(solution)/shard_map/ppermute | solution.py:18
  211.6 0.0 collective-permute-done.22
  211.6 0.4 collective-permute-done.23
  212.0 0.0 collective-permute-done.18
  212.0 4.6 %collective-permute-done.19 = f32[1,16,128,128]{3,2,1,0:T(8,128)S(1)} collective-permute-done((f32[1,16,128,128]{3,2,1,0:T(8,128)S(1)}, f32[1,16,128,128]{3,2,1,0:T(8,128)S(1)}, u32[]{:S(2)}, u32[]{:S(2)}) %collective-permute-start.19) | collective-permute-done | bytes 1048608 | tf_op jit(solution)/shard_map/ppermute | solution.py:18
  216.6 9.5 %add_reduce_fusion = (f32[4,128,128]{2,1,0:T(8,128)S(1)}, f32[4,128,128]{2,1,0:T(8,128)S(1)}, f32[4,16,128,128]{3,2,1,0:T(8,128)}) fusion(f32[4,16,128,128]{3,2,1,0:T(8,128)S(1)} %fusion.16, f32[4,16,128,128]{3,2,1,0:T(8,128)S(1)} %copy-done, f32[4,16,1,128]{3,2,1,0:T(1,128)S(1)} %collective-permute-done.23, f32[6,1,128,128]{3,2,1,0:T(8,128)S(1)} %pad.63, ...), kind=kLoop, calls=%fused_computation.112 | loop fusion | flops 43909120 | bytes 16056320 | tf_op jit(solution)/shard_map/reduce_sum | solution.py:78
  226.1 1.1 broadcast_in_dim.2
  227.2 40.6 %all_to_all.6 = f32[4,1,131072]{2,1,0:T(1,128)S(1)} all-to-all(f32[4,1,131072]{2,1,0:T(1,128)S(1)} %broadcast_in_dim.2), channel_id=1, replica_groups=mesh['trial'=4,'lat'=2,'lon'=4,'lev'=8] {'lon'}, dimensions={0} | all-to-all | bytes 4194304 | tf_op jit(solution)/shard_map/all_to_all | solution.py:31
  267.8 1.9 reduce_sum.29
  269.7 0.1 fusion.47
  269.8 5.0 %subtract_multiply_fusion = f32[4,16,128,128]{3,2,1,0:T(8,128)} fusion(f32[4,16,128,128]{3,2,1,0:T(8,128)} %get-tuple-element.4, f32[4,128,128]{2,1,0:T(8,128)S(1)} %bitcast.7, f32[4,128,128]{2,1,0:T(8,128)S(1)} %bitcast.6), kind=kLoop, calls=%fused_computation.110 | loop fusion | flops 2097152 | bytes 8912896 | tf_op jit(solution)/shard_map/mul | solution.py:84
  (23 shorter events, 0.6 us)
Async XLA Ops:
  0.6 13.0 %copy-start.1 = (f32[4,16,128,128]{3,2,1,0:T(8,128)S(1)}, f32[4,16,128,128]{3,2,1,0:T(8,128)}, u32[]{:S(2)}) copy-start(f32[4,16,128,128]{3,2,1,0:T(8,128)} %param.2) | copy-start | bytes 12582916
  2.5 36.2 %collective-permute-start = (f32[1,16,128,128]{3,2,1,0:T(8,128)S(1)}, f32[1,16,128,128]{3,2,1,0:T(8,128)S(1)}, u32[]{:S(2)}, u32[]{:S(2)}) collective-permute-start(f32[1,16,128,128]{3,2,1,0:T(8,128)S(1)} %get-tuple-element.28), channel_id=1, source_target_pairs={{0,32},{1,33},{2,34},{3,35},{4,36},{5,37},{6,38},{7,39},{8,40},{9,... | collective-permute-start | bytes 3145736 | tf_op jit(solution)/shard_map/ppermute | solution.py:17
  12.3 51.2 %collective-permute-start.1 = (f32[1,16,128,128]{3,2,1,0:T(8,128)S(1)}, f32[1,16,128,128]{3,2,1,0:T(8,128)S(1)}, u32[]{:S(2)}, u32[]{:S(2)}) collective-permute-start(f32[1,16,128,128]{3,2,1,0:T(8,128)S(1)} %get-tuple-element.27), channel_id=1, source_target_pairs={{32,0},{33,1},{34,2},{35,3},{36,4},{37,5},{38,6},{39,7},{40,8},{41... | collective-permute-start | bytes 3145736 | tf_op jit(solution)/shard_map/ppermute | solution.py:18
  13.7 9.7 %collective-permute-start.2 = (f32[4,1,128,128]{3,2,1,0:T(8,128)S(1)}, f32[4,1,128,128]{3,2,1,0:T(8,128)S(1)}, u32[]{:S(2)}, u32[]{:S(2)}) collective-permute-start(f32[4,1,128,128]{3,2,1,0:T(8,128)S(1)} %get-tuple-element.25), channel_id=1, source_target_pairs={{0,8},{8,16},{16,24},{1,9},{9,17},{17,25},{2,10},{10,18},{18,26},{... | collective-permute-start | bytes 786440 | tf_op jit(solution)/shard_map/ppermute | solution.py:17
  19.2 9.5 %collective-permute-start.3 = (f32[4,1,128,128]{3,2,1,0:T(8,128)S(1)}, f32[4,1,128,128]{3,2,1,0:T(8,128)S(1)}, u32[]{:S(2)}, u32[]{:S(2)}) collective-permute-start(f32[4,1,128,128]{3,2,1,0:T(8,128)S(1)} %get-tuple-element.26), channel_id=1, source_target_pairs={{8,0},{16,8},{24,16},{9,1},{17,9},{25,17},{10,2},{18,10},{26,18},{... | collective-permute-start | bytes 786440 | tf_op jit(solution)/shard_map/ppermute | solution.py:18
  21.2 43.5 %collective-permute-start.4 = (f32[4,16,1,128]{3,2,1,0:T(1,128)S(1)}, f32[4,16,1,128]{3,2,1,0:T(1,128)S(1)}, u32[]{:S(2)}, u32[]{:S(2)}) collective-permute-start(f32[4,16,1,128]{3,2,1,0:T(1,128)S(1)} %get-tuple-element.23), channel_id=1, source_target_pairs={{0,1},{1,2},{2,3},{3,4},{4,5},{5,6},{6,7},{8,9},{9,10},{10,11},{11... | collective-permute-start | bytes 98312 | tf_op jit(solution)/shard_map/ppermute | solution.py:17
  23.4 41.5 %collective-permute-start.5 = (f32[4,16,1,128]{3,2,1,0:T(1,128)S(1)}, f32[4,16,1,128]{3,2,1,0:T(1,128)S(1)}, u32[]{:S(2)}, u32[]{:S(2)}) collective-permute-start(f32[4,16,1,128]{3,2,1,0:T(1,128)S(1)} %get-tuple-element.24), channel_id=1, source_target_pairs={{1,0},{2,1},{3,2},{4,3},{5,4},{6,5},{7,6},{9,8},{10,9},{11,10},{12... | collective-permute-start | bytes 98312 | tf_op jit(solution)/shard_map/ppermute | solution.py:18
  39.8 25.1 %copy-start = (f32[4,16,128,128]{3,2,1,0:T(8,128)S(1)}, f32[4,16,128,128]{3,2,1,0:T(8,128)}, u32[]{:S(2)}) copy-start(f32[4,16,128,128]{3,2,1,0:T(8,128)} %param.3) | copy-start | bytes 12582916
  63.5 1.3 copy-start.2
  74.2 22.2 %collective-permute-start.6 = (f32[1,16,128,128]{3,2,1,0:T(8,128)S(1)}, f32[1,16,128,128]{3,2,1,0:T(8,128)S(1)}, u32[]{:S(2)}, u32[]{:S(2)}) collective-permute-start(f32[1,16,128,128]{3,2,1,0:T(8,128)S(1)} %get-tuple-element.19), channel_id=1, source_target_pairs={{0,32},{1,33},{2,34},{3,35},{4,36},{5,37},{6,38},{7,39},{8,40},{9,... | collective-permute-start | bytes 3145736 | tf_op jit(solution)/shard_map/ppermute | solution.py:17
  75.6 28.8 %collective-permute-start.7 = (f32[1,16,128,128]{3,2,1,0:T(8,128)S(1)}, f32[1,16,128,128]{3,2,1,0:T(8,128)S(1)}, u32[]{:S(2)}, u32[]{:S(2)}) collective-permute-start(f32[1,16,128,128]{3,2,1,0:T(8,128)S(1)} %get-tuple-element.20), channel_id=1, source_target_pairs={{32,0},{33,1},{34,2},{35,3},{36,4},{37,5},{38,6},{39,7},{40,8},{41... | collective-permute-start | bytes 3145736 | tf_op jit(solution)/shard_map/ppermute | solution.py:18
  76.9 10.7 %collective-permute-start.8 = (f32[4,1,128,128]{3,2,1,0:T(8,128)S(1)}, f32[4,1,128,128]{3,2,1,0:T(8,128)S(1)}, u32[]{:S(2)}, u32[]{:S(2)}) collective-permute-start(f32[4,1,128,128]{3,2,1,0:T(8,128)S(1)} %get-tuple-element.21), channel_id=1, source_target_pairs={{0,8},{8,16},{16,24},{1,9},{9,17},{17,25},{2,10},{10,18},{18,26},{... | collective-permute-start | bytes 786440 | tf_op jit(solution)/shard_map/ppermute | solution.py:17
  83.5 9.5 %collective-permute-start.9 = (f32[4,1,128,128]{3,2,1,0:T(8,128)S(1)}, f32[4,1,128,128]{3,2,1,0:T(8,128)S(1)}, u32[]{:S(2)}, u32[]{:S(2)}) collective-permute-start(f32[4,1,128,128]{3,2,1,0:T(8,128)S(1)} %get-tuple-element.22), channel_id=1, source_target_pairs={{8,0},{16,8},{24,16},{9,1},{17,9},{25,17},{10,2},{18,10},{26,18},{... | collective-permute-start | bytes 786440 | tf_op jit(solution)/shard_map/ppermute | solution.py:18
  85.4 7.5 %collective-permute-start.10 = (f32[4,16,1,128]{3,2,1,0:T(1,128)S(1)}, f32[4,16,1,128]{3,2,1,0:T(1,128)S(1)}, u32[]{:S(2)}, u32[]{:S(2)}) collective-permute-start(f32[4,16,1,128]{3,2,1,0:T(1,128)S(1)} %get-tuple-element.17), channel_id=1, source_target_pairs={{0,1},{1,2},{2,3},{3,4},{4,5},{5,6},{6,7},{8,9},{9,10},{10,11},{11... | collective-permute-start | bytes 98312 | tf_op jit(solution)/shard_map/ppermute | solution.py:17
  87.7 5.7 %collective-permute-start.11 = (f32[4,16,1,128]{3,2,1,0:T(1,128)S(1)}, f32[4,16,1,128]{3,2,1,0:T(1,128)S(1)}, u32[]{:S(2)}, u32[]{:S(2)}) collective-permute-start(f32[4,16,1,128]{3,2,1,0:T(1,128)S(1)} %get-tuple-element.18), channel_id=1, source_target_pairs={{1,0},{2,1},{3,2},{4,3},{5,4},{6,5},{7,6},{9,8},{10,9},{11,10},{12... | collective-permute-start | bytes 98312 | tf_op jit(solution)/shard_map/ppermute | solution.py:18
  112.6 44.5 %collective-permute-start.12 = (f32[1,16,128,128]{3,2,1,0:T(8,128)S(1)}, f32[1,16,128,128]{3,2,1,0:T(8,128)S(1)}, u32[]{:S(2)}, u32[]{:S(2)}) collective-permute-start(f32[1,16,128,128]{3,2,1,0:T(8,128)S(1)} %get-tuple-element.13), channel_id=1, source_target_pairs={{0,32},{1,33},{2,34},{3,35},{4,36},{5,37},{6,38},{7,39},{8,40},{9,... | collective-permute-start | bytes 3145736 | tf_op jit(solution)/shard_map/ppermute | solution.py:17
  114.0 43.1 %collective-permute-start.13 = (f32[1,16,128,128]{3,2,1,0:T(8,128)S(1)}, f32[1,16,128,128]{3,2,1,0:T(8,128)S(1)}, u32[]{:S(2)}, u32[]{:S(2)}) collective-permute-start(f32[1,16,128,128]{3,2,1,0:T(8,128)S(1)} %get-tuple-element.14), channel_id=1, source_target_pairs={{32,0},{33,1},{34,2},{35,3},{36,4},{37,5},{38,6},{39,7},{40,8},{41... | collective-permute-start | bytes 3145736 | tf_op jit(solution)/shard_map/ppermute | solution.py:18
  115.3 36.1 %collective-permute-start.14 = (f32[4,1,128,128]{3,2,1,0:T(8,128)S(1)}, f32[4,1,128,128]{3,2,1,0:T(8,128)S(1)}, u32[]{:S(2)}, u32[]{:S(2)}) collective-permute-start(f32[4,1,128,128]{3,2,1,0:T(8,128)S(1)} %get-tuple-element.15), channel_id=1, source_target_pairs={{0,8},{8,16},{16,24},{1,9},{9,17},{17,25},{2,10},{10,18},{18,26},{... | collective-permute-start | bytes 786440 | tf_op jit(solution)/shard_map/ppermute | solution.py:17
  147.2 9.5 %collective-permute-start.15 = (f32[4,1,128,128]{3,2,1,0:T(8,128)S(1)}, f32[4,1,128,128]{3,2,1,0:T(8,128)S(1)}, u32[]{:S(2)}, u32[]{:S(2)}) collective-permute-start(f32[4,1,128,128]{3,2,1,0:T(8,128)S(1)} %get-tuple-element.16), channel_id=1, source_target_pairs={{8,0},{16,8},{24,16},{9,1},{17,9},{25,17},{10,2},{18,10},{26,18},{... | collective-permute-start | bytes 786440 | tf_op jit(solution)/shard_map/ppermute | solution.py:18
  149.2 7.5 %collective-permute-start.16 = (f32[4,16,1,128]{3,2,1,0:T(1,128)S(1)}, f32[4,16,1,128]{3,2,1,0:T(1,128)S(1)}, u32[]{:S(2)}, u32[]{:S(2)}) collective-permute-start(f32[4,16,1,128]{3,2,1,0:T(1,128)S(1)} %get-tuple-element.11), channel_id=1, source_target_pairs={{0,1},{1,2},{2,3},{3,4},{4,5},{5,6},{6,7},{8,9},{9,10},{10,11},{11... | collective-permute-start | bytes 98312 | tf_op jit(solution)/shard_map/ppermute | solution.py:17
  151.4 5.7 %collective-permute-start.17 = (f32[4,16,1,128]{3,2,1,0:T(1,128)S(1)}, f32[4,16,1,128]{3,2,1,0:T(1,128)S(1)}, u32[]{:S(2)}, u32[]{:S(2)}) collective-permute-start(f32[4,16,1,128]{3,2,1,0:T(1,128)S(1)} %get-tuple-element.12), channel_id=1, source_target_pairs={{1,0},{2,1},{3,2},{4,3},{5,4},{6,5},{7,6},{9,8},{10,9},{11,10},{12... | collective-permute-start | bytes 98312 | tf_op jit(solution)/shard_map/ppermute | solution.py:18
  165.4 46.5 %collective-permute-start.18 = (f32[1,16,128,128]{3,2,1,0:T(8,128)S(1)}, f32[1,16,128,128]{3,2,1,0:T(8,128)S(1)}, u32[]{:S(2)}, u32[]{:S(2)}) collective-permute-start(f32[1,16,128,128]{3,2,1,0:T(8,128)S(1)} %get-tuple-element.9), channel_id=1, source_target_pairs={{0,32},{1,33},{2,34},{3,35},{4,36},{5,37},{6,38},{7,39},{8,40},{9,... | collective-permute-start | bytes 3145736 | tf_op jit(solution)/shard_map/ppermute | solution.py:17
  173.8 42.8 %collective-permute-start.19 = (f32[1,16,128,128]{3,2,1,0:T(8,128)S(1)}, f32[1,16,128,128]{3,2,1,0:T(8,128)S(1)}, u32[]{:S(2)}, u32[]{:S(2)}) collective-permute-start(f32[1,16,128,128]{3,2,1,0:T(8,128)S(1)} %get-tuple-element.10), channel_id=1, source_target_pairs={{32,0},{33,1},{34,2},{35,3},{36,4},{37,5},{38,6},{39,7},{40,8},{41... | collective-permute-start | bytes 3145736 | tf_op jit(solution)/shard_map/ppermute | solution.py:18
  175.1 30.6 %collective-permute-start.20 = (f32[4,1,128,128]{3,2,1,0:T(8,128)S(1)}, f32[4,1,128,128]{3,2,1,0:T(8,128)S(1)}, u32[]{:S(2)}, u32[]{:S(2)}) collective-permute-start(f32[4,1,128,128]{3,2,1,0:T(8,128)S(1)} %get-tuple-element.7), channel_id=1, source_target_pairs={{0,8},{8,16},{16,24},{1,9},{9,17},{17,25},{2,10},{10,18},{18,26},{... | collective-permute-start | bytes 786440 | tf_op jit(solution)/shard_map/ppermute | solution.py:17
  202.4 9.2 %collective-permute-start.21 = (f32[4,1,128,128]{3,2,1,0:T(8,128)S(1)}, f32[4,1,128,128]{3,2,1,0:T(8,128)S(1)}, u32[]{:S(2)}, u32[]{:S(2)}) collective-permute-start(f32[4,1,128,128]{3,2,1,0:T(8,128)S(1)} %get-tuple-element.8), channel_id=1, source_target_pairs={{8,0},{16,8},{24,16},{9,1},{17,9},{25,17},{10,2},{18,10},{26,18},{... | collective-permute-start | bytes 786440 | tf_op jit(solution)/shard_map/ppermute | solution.py:18
  204.4 7.2 %collective-permute-start.22 = (f32[4,16,1,128]{3,2,1,0:T(1,128)S(1)}, f32[4,16,1,128]{3,2,1,0:T(1,128)S(1)}, u32[]{:S(2)}, u32[]{:S(2)}) collective-permute-start(f32[4,16,1,128]{3,2,1,0:T(1,128)S(1)} %get-tuple-element.5), channel_id=1, source_target_pairs={{0,1},{1,2},{2,3},{3,4},{4,5},{5,6},{6,7},{8,9},{9,10},{10,11},{11... | collective-permute-start | bytes 98312 | tf_op jit(solution)/shard_map/ppermute | solution.py:17
  205.7 6.3 %collective-permute-start.23 = (f32[4,16,1,128]{3,2,1,0:T(1,128)S(1)}, f32[4,16,1,128]{3,2,1,0:T(1,128)S(1)}, u32[]{:S(2)}, u32[]{:S(2)}) collective-permute-start(f32[4,16,1,128]{3,2,1,0:T(1,128)S(1)} %get-tuple-element.6), channel_id=1, source_target_pairs={{1,0},{2,1},{3,2},{4,3},{5,4},{6,5},{7,6},{9,8},{10,9},{11,10},{12... | collective-permute-start | bytes 98312 | tf_op jit(solution)/shard_map/ppermute | solution.py:18
where the time goes:
time: 276 us; the launch traced here: 275 us
  starting transfers between devices  118 us (43%)
  waiting for transfers between devices  64.5 us (23%)
  other arithmetic  41.9 us (15%)
  blocking collectives  40.6 us (15%)
  local copies, waits for them, and re-layouts  8.81 us (3%)
    ppermute x12, starting transfers between devices, with_halo(): lax.ppermute(last, axis, up)  99.9 us
    ppermute x12, waiting for transfers between devices, with_halo(): lax.ppermute(first, axis, [(b, a) for a, b in up])  51.3 us
    all_to_all x1, blocking collectives, from_everyone(): lax.all_to_all(jnp.broadcast_to(array[None], (devices, *array.shape)), ax...  40.6 us
    add x3, other arithmetic, advance(): return middle + 0.1 * spread + 0.2 * middle * (1.0 - middle * crowding)  25.3 us
    ppermute x12, starting transfers between devices, with_halo(): lax.ppermute(first, axis, [(b, a) for a, b in up])  18 us
    ppermute x12, waiting for transfers between devices, with_halo(): lax.ppermute(last, axis, up)  13.2 us
    reduce_sum x1, other arithmetic, shards(): jnp.sum(moved, axis=1, keepdims=True)  9.51 us
  transfers between devices with their start and end apart: 24, of which 12 were waited for; matrix products, arithmetic and copies ran while one was open for 2% of the time, Pallas kernels for 0%

commit v1 on v0

v1 whole, which is shorter than its diff:
```python
import functools

import jax
import jax.numpy as jnp
from jax import lax
from jax.experimental import pallas as pl
from jax.experimental.pallas import tpu as pltpu
from jax.sharding import PartitionSpec as P

STEPS = 4
MIB = 1 << 20


def cells(a, low_x, high_x, near, far, low_z, high_z, crowding):
    length = a.shape[0]
    z = lax.broadcasted_iota(jnp.int32, a.shape, 0)
    down = jnp.where(z == 0, low_z, pltpu.roll(a, 1, 0))
    up = jnp.where(z == length - 1, high_z, pltpu.roll(a, length - 1, 0))
    spread = low_x + high_x + near + far + down + up - 6.0 * a
    return a + 0.1 * spread + 0.2 * a * (1.0 - a * crowding)


def over_x(n, visit):
    visit(0, None, 1)

    def inner(x, carry):
        visit(x, x - 1, x + 1)
        return carry

    lax.fori_loop(1, n - 1, inner, 0)
    visit(n - 1, n - 2, None)


def line_sums(column, n, mean_store, m2_store):
    total = lax.fori_loop(1, n, lambda x, s: s + column(x), column(0))
    mean = total / n
    mean_store(mean)

    def add(x, s):
        d = column(x) - mean
        return s + d * d

    m2_store(lax.fori_loop(0, n, add, jnp.zeros_like(mean)))


def row_kernel(first, last, stats, *refs):
    centre, near, far, crowding, x_low, x_high, z_low, z_high, out = refs[:9]
    n = centre.shape[0]

    def visit(x, before, after):
        low_x = x_low[0] if before is None else centre[before]
        high_x = x_high[0] if after is None else centre[after]
        low_z = z_low[0, pl.ds(x, 1), :] if first else z_low[x, 7:8, :]
        high_z = z_high[0, pl.ds(x, 1), :] if last else z_high[x, 0:1, :]
        out[x] = cells(centre[x], low_x, high_x, near[x], far[0, x], low_z, high_z, crowding[x])

    over_x(n, visit)
    if stats:
        sums = refs[9]

        def put(k, value):
            sums[k] = value

        line_sums(lambda x: out[x], n, functools.partial(put, 0), functools.partial(put, 1))


def row_step(c, chunks, received, rest, crowding, ghosts, stats):
    x_low, x_high, z_low, z_high = ghosts
    centre = chunks[c]
    n, depth, species = centre.shape
    count = len(chunks)
    first, last = c == 0, c == count - 1
    whole = pl.BlockSpec(memory_space=pltpu.VMEM)
    chunk = lambda: pl.BlockSpec((1, depth, species), lambda i: (0, c, 0))
    edge = lambda at: pl.BlockSpec((n, 8, species), lambda i: (0, at, 0))
    ghost = lambda: pl.BlockSpec((1, n, species), lambda i: (0, 0, 0))
    full = lambda: pl.BlockSpec((n, depth, species), lambda i: (0, 0, 0))
    out_shape = [jax.ShapeDtypeStruct(centre.shape, jnp.float32)]
    out_specs = [full()]
    if stats:
        out_shape.append(jax.ShapeDtypeStruct((2, depth, species), jnp.float32))
        out_specs.append(pl.BlockSpec((2, depth, species), lambda i: (0, 0, 0)))
    result = pl.pallas_call(
        functools.partial(row_kernel, first, last, stats),
        grid=(1,),
        out_shape=out_shape,
        in_specs=[
            full(),
            full(),
            pl.BlockSpec((1, n, depth, species), lambda i: (0, 0, c, 0)),
            full(),
            chunk(),
            chunk(),
            ghost() if first else edge(chunks[c - 1].shape[1] // 8 - 1),
            ghost() if last else edge(0),
        ],
        out_specs=out_specs,
        compiler_params=pltpu.CompilerParams(vmem_limit_bytes=16 * MIB),
        cost_estimate=pl.CostEstimate(
            flops=20 * centre.size, bytes_accessed=20 * centre.size, transcendentals=0
        ),
        name=f"row_chunk_{c}",
    )(
        centre,
        received,
        rest,
        crowding,
        x_low,
        x_high,
        z_low if first else chunks[c - 1],
        z_high if last else chunks[c + 1],
    )
    return result if stats else (result[0], None)


def rest_kernel(count, mapped, stats, *refs):
    order = refs[0]
    chunks, refs = refs[1 : 1 + count], refs[1 + count :]
    field, crowding, x_low, x_high, z_low, z_high, out = refs[:7]
    n, length = field.shape[1], field.shape[2]

    for row in range(3):
        at = order[row + 1] if mapped else row
        beyond = None if row == 2 else (order[row + 2] if mapped else row + 1)
        before_row = None if row == 0 else (order[row] if mapped else row - 1)
        crowd_at = order[row + 1]

        def visit(x, before, after):
            low_x = x_low[row + 1] if before is None else field[at, before]
            high_x = x_high[row + 1] if after is None else field[at, after]
            if row == 0:
                near = jnp.concatenate([part[x] for part in chunks], axis=0)
            else:
                near = field[before_row, x]
            far = 0.0 if beyond is None else field[beyond, x]
            low_z = z_low[row + 1, pl.ds(x, 1), :]
            high_z = z_high[row + 1, pl.ds(x, 1), :]
            out[row, x] = cells(
                field[at, x], low_x, high_x, near, far, low_z, high_z, crowding[crowd_at, x]
            )

        over_x(n, visit)
        if stats:
            sums = refs[7]

            def put(k, value):
                sums[k, row] = value

            line_sums(lambda x: out[row, x], n, functools.partial(put, 0), functools.partial(put, 1))


def rest_step(order, chunks, field, crowding, ghosts, mapped, stats):
    _, n, length, species = field.shape
    vmem = pl.BlockSpec(memory_space=pltpu.VMEM)
    out_shape = [jax.ShapeDtypeStruct((3, n, length, species), jnp.float32)]
    if stats:
        out_shape.append(jax.ShapeDtypeStruct((2, 3, length, species), jnp.float32))
    size = 3 * n * length * species
    result = pl.pallas_call(
        functools.partial(rest_kernel, len(chunks), mapped, stats),
        out_shape=out_shape,
        in_specs=[pl.BlockSpec(memory_space=pltpu.SMEM)] + [vmem] * (len(chunks) + 6),
        out_specs=[vmem] * len(out_shape),
        compiler_params=pltpu.CompilerParams(vmem_limit_bytes=24 * MIB),
        cost_estimate=pl.CostEstimate(
            flops=20 * size, bytes_accessed=16 * size, transcendentals=0
        ),
        name="rest",
    )(order, *chunks, field, crowding, *ghosts)
    return result if stats else (result[0], None)


def whole_lines(parts, n):
    mean = (parts[0][0] + parts[1][0] + parts[2][0] + parts[3][0]) / 4
    m2 = parts[0][1] + parts[1][1] + parts[2][1] + parts[3][1]
    between = jnp.zeros_like(mean)
    for part in parts:
        d = part[0] - mean
        between = between + d * d
    variance = (m2 + n * between) / (4 * n)
    return mean, lax.rsqrt(variance + 0.0001)


def place_kernel(order, field, s0, s1, s2, s3, scaled, density):
    n = field.shape[1]
    for row in range(3):
        at = order[row + 1]
        mean, factor = whole_lines([[s[0, row], s[1, row]] for s in (s0, s1, s2, s3)], n)

        def visit(x, carry):
            value = field[row, x]
            density[at, x] = value
            scaled[at, x] = (value - mean) * factor
            return carry

        lax.fori_loop(0, n, visit, 0)


def place_rest(order, field, parts):
    _, n, length, species = field.shape
    vmem = pl.BlockSpec(memory_space=pltpu.VMEM)
    whole = jax.ShapeDtypeStruct((4, n, length, species), jnp.float32)
    size = 3 * n * length * species
    return pl.pallas_call(
        place_kernel,
        out_shape=[whole, whole],
        in_specs=[pl.BlockSpec(memory_space=pltpu.SMEM)] + [vmem] * 5,
        out_specs=[vmem, vmem],
        compiler_params=pltpu.CompilerParams(vmem_limit_bytes=24 * MIB),
        cost_estimate=pl.CostEstimate(
            flops=10 * size, bytes_accessed=16 * size, transcendentals=0
        ),
        name="place_rest",
    )(order, field, *parts)


def place_row_kernel(order, field, s0, s1, s2, s3, scaled_in, density_in, scaled, density):
    n = field.shape[0]
    mean, factor = whole_lines([[s[0], s[1]] for s in (s0, s1, s2, s3)], n)

    def visit(x, carry):
        value = field[x]
        density[0, x] = value
        scaled[0, x] = (value - mean) * factor
        return carry

    lax.fori_loop(0, n, visit, 0)


def place_row(order, at, field, parts, scaled, density):
    n, depth, species = field.shape
    block = at // depth
    out = lambda: pl.BlockSpec((1, n, depth, species), lambda i, order: (order[0], 0, block, 0))
    return pl.pallas_call(
        place_row_kernel,
        grid_spec=pltpu.PrefetchScalarGridSpec(
            num_scalar_prefetch=1,
            grid=(1,),
            in_specs=[pl.BlockSpec((n, depth, species), lambda i, order: (0, 0, 0))]
            + [pl.BlockSpec((2, depth, species), lambda i, order: (0, 0, 0))] * 4
            + [pl.BlockSpec(memory_space=pl.ANY)] * 2,
            out_specs=[out(), out()],
        ),
        out_shape=[jax.ShapeDtypeStruct(scaled.shape, jnp.float32)] * 2,
        input_output_aliases={6: 0, 7: 1},
        compiler_params=pltpu.CompilerParams(vmem_limit_bytes=16 * MIB),
        cost_estimate=pl.CostEstimate(
            flops=10 * field.size, bytes_accessed=12 * field.size, transcendentals=0
        ),
        name="place_row",
    )(order, field, *parts, scaled, density)


def both_ways(low, high, axis):
    devices = lax.axis_size(axis)
    up = [(i, i + 1) for i in range(devices - 1)]
    return lax.ppermute(high, axis, up), lax.ppermute(low, axis, [(b, a) for a, b in up])


def everyones(array, axis):
    devices = lax.axis_size(axis)
    shifted = [
        lax.ppermute(array, axis, [(i, (i + k) % devices) for i in range(devices)])
        for k in range(1, devices)
    ]
    return [array, *shifted]


def shards(density, crowding):
    lat = lax.axis_index("lat")
    rows, n, length, species = density.shape
    cuts = (0, length // 2, length)
    order = jnp.where(lat == 0, jnp.arange(rows)[::-1], jnp.arange(rows)).astype(jnp.int32)

    def logical(edges):
        return jnp.where(lat == 0, edges[::-1], edges)

    def pieces(array):
        row = lax.dynamic_index_in_dim(array, order[0], 0, keepdims=False)
        return [row[:, a:b] for a, b in zip(cuts[:-1], cuts[1:])]

    swap = [(0, 1), (1, 0)]
    chunks = pieces(density)
    arriving = [lax.ppermute(c, "lat", swap) for c in chunks]
    x_edges = (logical(density[:, 0]), logical(density[:, n - 1]))
    z_edges = (logical(density[:, :, 0]), logical(density[:, :, length - 1]))
    crowd = pieces(crowding)
    rest = lax.dynamic_index_in_dim(density, order[1], 0)
    for step in range(STEPS):
        ghosts = (*both_ways(*x_edges, "lon"), *both_ways(*z_edges, "lev"))
        final = step == STEPS - 1
        new, sums = [], []
        rest_new, rest_sums = rest_step(
            order, chunks, density if step == 0 else rest, crowding, ghosts, step == 0, final
        )
        sent = []
        for c in range(len(chunks)):
            value, s = row_step(c, chunks, arriving[c], rest, crowd[c], ghosts, final)
            new.append(value)
            sums.append(s)
            if not final:
                sent.append(lax.ppermute(value, "lat", swap))
        chunks, rest, arriving = new, rest_new, sent
        if not final:
            row_x = [jnp.concatenate([c[at] for c in chunks], axis=0)[None] for at in (0, n - 1)]
            x_edges = [
                jnp.concatenate([row_x[k], rest[:, at]], axis=0) for k, at in enumerate((0, n - 1))
            ]
            z_edges = (
                jnp.concatenate([chunks[0][None, :, 0], rest[:, :, 0]], axis=0),
                jnp.concatenate([chunks[-1][None, :, -1], rest[:, :, length - 1]], axis=0),
            )
    scaled, ended = place_rest(order, rest, everyones(rest_sums, "lon"))
    for c, value in enumerate(chunks):
        scaled, ended = place_row(order, cuts[c], value, everyones(sums[c], "lon"), scaled, ended)
    return scaled, ended


def solution(mesh):
    placed = P(("trial", "lat"), "lon", "lev", None)
    return jax.shard_map(
        shards,
        mesh=mesh,
        in_specs=(placed, placed),
        out_specs=(placed, placed),
        check_vma=False,
    )
```

time: 276 us -> 240 us (0.87)
  other arithmetic: 41.9 us -> 0.26 us
  blocking collectives: 40.6 us -> 0 us
  waiting for transfers between devices: 64.5 us -> 100 us
  Pallas kernels: 0 us -> 23.8 us
  starting transfers between devices: 118 us -> 104 us
  between operations: 1.08 us -> 5.15 us
  local copies, waits for them, and re-layouts: 8.81 us -> 5.35 us
    all_to_all x1 -> x0, blocking collectives: 40.6 us -> none  [from_everyone(): lax.all_to_all(jnp.broadcast_to(array[None], (devices, *array.shape)), ax...]
    ppermute x24 -> x33, waiting for transfers between devices: 64.5 us -> 100 us  [the longest x6 57 us: shards(): sent.append(lax.ppermute(value, 'lat', swap))]
    add x4 -> x0, other arithmetic: 25.4 us -> none  [the longest x3 25.3 us: advance(): return middle + 0.1 * spread + 0.2 * middle * (1.0 - middle * crowding)]
    pallas_call x0 -> x15, Pallas kernels: none -> 23.8 us  [the longest x4 11.8 us: rest_step(): pl.pallas_call(functools.partial(rest_kernel, len(chunks), mapped, stats)...]
    ppermute x24 -> x33, starting transfers between devices: 118 us -> 104 us  [the longest x8 40.3 us: both_ways(): lax.ppermute(high, axis, up)]
    reduce_sum x2 -> x0, other arithmetic: 11.4 us -> none  [the longest x1 9.51 us: shards(): jnp.sum(moved, axis=1, keepdims=True)]
    mul x1 -> x0, other arithmetic: 5.01 us -> none  [shards(): scaled_field = centred * lax.rsqrt(line_variance + 0.0001)]
    unnamed x8 -> x4, local copies, waits for them, and re-layouts: 3.64 us -> 0.01 us
  transfers between devices with their start and end apart: 24 -> 33, of which waited for: 12 -> 13; matrix products, arithmetic and copies ran while one was open for 2% -> 2% of each run, Pallas kernels for 0% -> 9%
where the time goes in v1:
time: 240 us; the launch traced here: 239 us
  starting transfers between devices  104 us (43%)
  waiting for transfers between devices  100 us (42%)
  Pallas kernels  23.8 us (10%)
  local copies, waits for them, and re-layouts  5.35 us (2%)
  between operations  5.15 us (2%)
    ppermute x6, waiting for transfers between devices, shards(): sent.append(lax.ppermute(value, 'lat', swap))  57 us
    ppermute x8, starting transfers between devices, both_ways(): lax.ppermute(high, axis, up)  40.3 us
    ppermute x6, starting transfers between devices, shards(): sent.append(lax.ppermute(value, 'lat', swap))  25.1 us
    ppermute x2, waiting for transfers between devices, shards(): arriving = [lax.ppermute(c, 'lat', swap) for c in chunks]  21.4 us
    ppermute x9, starting transfers between devices, everyones(): lax.ppermute(array, axis, [(i, (i + k) % devices) for i in range(devices)])  18.3 us
    ppermute x8, waiting for transfers between devices, both_ways(): lax.ppermute(low, axis, [(b, a) for a, b in up])  16.3 us
    ppermute x8, starting transfers between devices, both_ways(): lax.ppermute(low, axis, [(b, a) for a, b in up])  12.8 us
    pallas_call x4, Pallas kernels, rest_step(): pl.pallas_call(functools.partial(rest_kernel, len(chunks), mapped, stats)...  11.8 us
  transfers between devices with their start and end apart: 33, of which 13 were waited for; matrix products, arithmetic and copies ran while one was open for 2% of the time, Pallas kernels for 9%

profile of v1, /device:TPU:1, one launch (start us, length us, event | category | flops | bytes accessed | tf_op | source)
XLA Modules:
  0.0 238.9 jit_solution(17726725568285058047)
XLA Ops:
  0.6 1.1 fusion
  1.7 1.3 collective-permute-start.3
  3.1 4.6 %collective-permute-start.5 = (f32[4,16,128]{2,1,0:T(8,128)S(1)}, f32[4,16,128]{2,1,0:T(8,128)S(1)}, u32[]{:S(2)}, u32[]{:S(2)}) collective-permute-start(f32[4,16,128]{2,1,0:T(8,128)S(1)} %reverse_select_fusion.2), channel_id=1, source_target_pairs={{0,1},{1,2},{2,3},{3,4},{4,5},{5,6},{6,7},{8,9},{9,10},{10,11},{11... | collective-permute-start | bytes 98312 | tf_op jit(solution)/shard_map/ppermute | solution.py:257
  7.6 1.1 slice_bitcast_fusion
  8.7 6.0 %collective-permute-start.1 = (f32[4,128,128]{2,1,0:T(8,128)S(1)}, f32[4,128,128]{2,1,0:T(8,128)S(1)}, u32[]{:S(2)}, u32[]{:S(2)}) collective-permute-start(f32[4,128,128]{2,1,0:T(8,128)S(1)} %reverse_select_fusion.1), channel_id=1, source_target_pairs={{0,8},{8,16},{16,24},{1,9},{9,17},{17,25},{2,10},{10,18},{18,26},{... | collective-permute-start | bytes 786440 | tf_op jit(solution)/shard_map/ppermute | solution.py:257
  14.8 1.9 collective-permute-start.2
  16.8 0.6 fusion.6
  21.3 1.9 constant_dynamic-slice_fusion
  23.2 0.1 fusion.5
  23.4 7.0 %collective-permute-start = (f32[16,64,128]{2,1,0:T(8,128)S(1)}, f32[16,64,128]{2,1,0:T(8,128)S(1)}, u32[]{:S(2)}, u32[]{:S(2)}) collective-permute-start(f32[16,64,128]{2,1,0:T(8,128)S(1)} %get-tuple-element.43.refs_0_.refs_2_.refs_7_), channel_id=1, source_target_pairs={{0,32},{32,0},{1,33},{33,1},{2,34},{34,2},{3,35},{35,3},{4,36},{36... | collective-permute-start | bytes 1572872 | tf_op jit(solution)/shard_map/ppermute | solution.py:284
  30.5 0.8 collective-permute-start.6
  31.2 0.1 fusion.4
  31.4 2.7 %rest.4.refs_2_.refs_3_ = f32[3,16,128,128]{3,2,1,0:T(8,128)S(1)} custom-call(s32[4]{0:T(128)S(1)} %broadcast_select_fusion.refs_0_.order, f32[16,64,128]{2,1,0:T(8,128)S(1)} %get-tuple-element.42.refs_6_.refs_1_.refs_0_, f32[16,64,128]{2,1,0:T(8,128)S(1)} %get-tuple-element.43.refs_0_.refs_2_.refs_7_, f32[4,16,128,128]{3,2,1,0:T(8,128)S(1)} %copy-done.1, ...), custom_call_target="tpu_custom_call" | custom-call | flops 15728640 | bytes 12582912 | tf_op jit(solution)/shard_map/rest/pallas_call | solution.py:159
  34.1 12.1 %collective-permute-done.refs_1_ = f32[16,64,128]{2,1,0:T(8,128)S(1)} collective-permute-done((f32[16,64,128]{2,1,0:T(8,128)S(1)}, f32[16,64,128]{2,1,0:T(8,128)S(1)}, u32[]{:S(2)}, u32[]{:S(2)}) %collective-permute-start) | collective-permute-done | bytes 524320 | tf_op jit(solution)/shard_map/ppermute | solution.py:284
  46.2 0.5 row_chunk_1.4.refs_0_.refs_2_.refs_7_
  46.7 5.6 %collective-permute-start.4 = (f32[16,64,128]{2,1,0:T(8,128)S(1)}, f32[16,64,128]{2,1,0:T(8,128)S(1)}, u32[]{:S(2)}, u32[]{:S(2)}) collective-permute-start(f32[16,64,128]{2,1,0:T(8,128)S(1)} %row_chunk_1.4.refs_0_.refs_2_.refs_7_), channel_id=1, source_target_pairs={{0,32},{32,0},{1,33},{33,1},{2,34},{34,2},{3,35},{35,3},{4,36},{36... | collective-permute-start | bytes 1572872 | tf_op jit(solution)/shard_map/ppermute | solution.py:302
  52.3 9.3 %collective-permute-done.6.refs_1_ = f32[16,64,128]{2,1,0:T(8,128)S(1)} collective-permute-done((f32[16,64,128]{2,1,0:T(8,128)S(1)}, f32[16,64,128]{2,1,0:T(8,128)S(1)}, u32[]{:S(2)}, u32[]{:S(2)}) %collective-permute-start.6) | collective-permute-done | bytes 524320 | tf_op jit(solution)/shard_map/ppermute | solution.py:284
  61.5 0.5 row_chunk_0.4.refs_6_.refs_1_.refs_0_
  62.1 5.8 %collective-permute-start.7 = (f32[4,128,128]{2,1,0:T(8,128)S(1)}, f32[4,128,128]{2,1,0:T(8,128)S(1)}, u32[]{:S(2)}, u32[]{:S(2)}) collective-permute-start(f32[4,128,128]{2,1,0:T(8,128)S(1)} %pad_maximum_fusion), channel_id=1, source_target_pairs={{0,8},{8,16},{16,24},{1,9},{9,17},{17,25},{2,10},{10,18},{18,26},{... | collective-permute-start | bytes 786440 | tf_op jit(solution)/shard_map/ppermute | solution.py:257
  68.0 1.9 collective-permute-start.8
  69.9 6.0 %collective-permute-start.12 = (f32[16,64,128]{2,1,0:T(8,128)S(1)}, f32[16,64,128]{2,1,0:T(8,128)S(1)}, u32[]{:S(2)}, u32[]{:S(2)}) collective-permute-start(f32[16,64,128]{2,1,0:T(8,128)S(1)} %row_chunk_0.4.refs_6_.refs_1_.refs_0_), channel_id=1, source_target_pairs={{0,32},{32,0},{1,33},{33,1},{2,34},{34,2},{3,35},{35,3},{4,36},{36... | collective-permute-start | bytes 1572872 | tf_op jit(solution)/shard_map/ppermute | solution.py:302
  76.0 1.3 collective-permute-start.9
  77.3 3.6 %collective-permute-done.9.refs_7_.refs_8_ = f32[4,16,128]{2,1,0:T(8,128)S(1)} collective-permute-done((f32[4,16,128]{2,1,0:T(8,128)S(1)}, f32[4,16,128]{2,1,0:T(8,128)S(1)}, u32[]{:S(2)}, u32[]{:S(2)}) %collective-permute-start.9) | collective-permute-done | bytes 32800 | tf_op jit(solution)/shard_map/ppermute | solution.py:257
  80.9 4.0 %collective-permute-start.11 = (f32[4,16,128]{2,1,0:T(8,128)S(1)}, f32[4,16,128]{2,1,0:T(8,128)S(1)}, u32[]{:S(2)}, u32[]{:S(2)}) collective-permute-start(f32[4,16,128]{2,1,0:T(8,128)S(1)} %pad_maximum_fusion.7), channel_id=1, source_target_pairs={{0,1},{1,2},{2,3},{3,4},{4,5},{5,6},{6,7},{8,9},{9,10},{10,11},{11... | collective-permute-start | bytes 98312 | tf_op jit(solution)/shard_map/ppermute | solution.py:257
  84.9 1.0 collective-permute-done.11.refs_7_.refs_6_
  85.9 2.7 %rest.5.refs_2_.refs_3_ = f32[3,16,128,128]{3,2,1,0:T(8,128)S(1)} custom-call(s32[4]{0:T(128)S(1)} %broadcast_select_fusion.refs_0_.order, f32[16,64,128]{2,1,0:T(8,128)S(1)} %row_chunk_0.4.refs_6_.refs_1_.refs_0_, f32[16,64,128]{2,1,0:T(8,128)S(1)} %row_chunk_1.4.refs_0_.refs_2_.refs_7_, f32[3,16,128,128]{3,2,1,0:T(8,128)S(1)} %rest.4.refs_2_.refs_3_, ...), custom_call_target="tpu_custom_call" | custom-call | flops 15728640 | bytes 12582912 | tf_op jit(solution)/shard_map/rest/pallas_call | solution.py:159
  88.7 0.5 row_chunk_1.5.refs_0_.refs_2_.refs_7_
  89.1 0.1 collective-permute-start.10
  89.3 11.3 %collective-permute-done.12.refs_1_ = f32[16,64,128]{2,1,0:T(8,128)S(1)} collective-permute-done((f32[16,64,128]{2,1,0:T(8,128)S(1)}, f32[16,64,128]{2,1,0:T(8,128)S(1)}, u32[]{:S(2)}, u32[]{:S(2)}) %collective-permute-start.12) | collective-permute-done | bytes 524320 | tf_op jit(solution)/shard_map/ppermute | solution.py:302
  100.5 0.5 row_chunk_0.5.refs_6_.refs_1_.refs_0_
  101.1 7.5 %collective-permute-start.13 = (f32[4,128,128]{2,1,0:T(8,128)S(1)}, f32[4,128,128]{2,1,0:T(8,128)S(1)}, u32[]{:S(2)}, u32[]{:S(2)}) collective-permute-start(f32[4,128,128]{2,1,0:T(8,128)S(1)} %pad_maximum_fusion.2), channel_id=1, source_target_pairs={{0,8},{8,16},{16,24},{1,9},{9,17},{17,25},{2,10},{10,18},{18,26},{... | collective-permute-start | bytes 786440 | tf_op jit(solution)/shard_map/ppermute | solution.py:257
  108.6 1.9 collective-permute-start.14
  110.6 7.1 %collective-permute-start.18 = (f32[16,64,128]{2,1,0:T(8,128)S(1)}, f32[16,64,128]{2,1,0:T(8,128)S(1)}, u32[]{:S(2)}, u32[]{:S(2)}) collective-permute-start(f32[16,64,128]{2,1,0:T(8,128)S(1)} %row_chunk_0.5.refs_6_.refs_1_.refs_0_), channel_id=1, source_target_pairs={{0,32},{32,0},{1,33},{33,1},{2,34},{34,2},{3,35},{35,3},{4,36},{36... | collective-permute-start | bytes 1572872 | tf_op jit(solution)/shard_map/ppermute | solution.py:302
  117.6 1.3 collective-permute-start.15
  118.9 9.0 %collective-permute-done.15.refs_7_.refs_8_ = f32[4,16,128]{2,1,0:T(8,128)S(1)} collective-permute-done((f32[4,16,128]{2,1,0:T(8,128)S(1)}, f32[4,16,128]{2,1,0:T(8,128)S(1)}, u32[]{:S(2)}, u32[]{:S(2)}) %collective-permute-start.15) | collective-permute-done | bytes 32800 | tf_op jit(solution)/shard_map/ppermute | solution.py:257
  127.9 4.3 %collective-permute-start.17 = (f32[4,16,128]{2,1,0:T(8,128)S(1)}, f32[4,16,128]{2,1,0:T(8,128)S(1)}, u32[]{:S(2)}, u32[]{:S(2)}) collective-permute-start(f32[4,16,128]{2,1,0:T(8,128)S(1)} %pad_maximum_fusion.9), channel_id=1, source_target_pairs={{0,1},{1,2},{2,3},{3,4},{4,5},{5,6},{6,7},{8,9},{9,10},{10,11},{11... | collective-permute-start | bytes 98312 | tf_op jit(solution)/shard_map/ppermute | solution.py:257
  132.2 1.0 collective-permute-done.17.refs_7_.refs_6_
  133.2 2.7 %rest.6.refs_2_.refs_3_ = f32[3,16,128,128]{3,2,1,0:T(8,128)S(1)} custom-call(s32[4]{0:T(128)S(1)} %broadcast_select_fusion.refs_0_.order, f32[16,64,128]{2,1,0:T(8,128)S(1)} %row_chunk_0.5.refs_6_.refs_1_.refs_0_, f32[16,64,128]{2,1,0:T(8,128)S(1)} %row_chunk_1.5.refs_0_.refs_2_.refs_7_, f32[3,16,128,128]{3,2,1,0:T(8,128)S(1)} %rest.5.refs_2_.refs_3_, ...), custom_call_target="tpu_custom_call" | custom-call | flops 15728640 | bytes 12582912 | tf_op jit(solution)/shard_map/rest/pallas_call | solution.py:159
  135.9 0.8 collective-permute-done.10.refs_1_
  136.7 0.5 row_chunk_1.6.refs_0_.refs_7_.refs_2_
  137.2 26.4 %collective-permute-done.18.refs_1_ = f32[16,64,128]{2,1,0:T(8,128)S(1)} collective-permute-done((f32[16,64,128]{2,1,0:T(8,128)S(1)}, f32[16,64,128]{2,1,0:T(8,128)S(1)}, u32[]{:S(2)}, u32[]{:S(2)}) %collective-permute-start.18) | collective-permute-done | bytes 524320 | tf_op jit(solution)/shard_map/ppermute | solution.py:302
  163.5 0.5 row_chunk_0.6.refs_6_.refs_0_.refs_1_
  164.1 4.1 %collective-permute-start.19 = (f32[4,128,128]{2,1,0:T(8,128)S(1)}, f32[4,128,128]{2,1,0:T(8,128)S(1)}, u32[]{:S(2)}, u32[]{:S(2)}) collective-permute-start(f32[4,128,128]{2,1,0:T(8,128)S(1)} %pad_maximum_fusion.4), channel_id=1, source_target_pairs={{0,8},{8,16},{16,24},{1,9},{9,17},{17,25},{2,10},{10,18},{18,26},{... | collective-permute-start | bytes 786440 | tf_op jit(solution)/shard_map/ppermute | solution.py:257
  168.2 1.9 collective-permute-start.20
  170.2 6.2 %collective-permute-start.16 = (f32[16,64,128]{2,1,0:T(8,128)S(1)}, f32[16,64,128]{2,1,0:T(8,128)S(1)}, u32[]{:S(2)}, u32[]{:S(2)}) collective-permute-start(f32[16,64,128]{2,1,0:T(8,128)S(1)} %row_chunk_1.6.refs_0_.refs_7_.refs_2_), channel_id=1, source_target_pairs={{0,32},{32,0},{1,33},{33,1},{2,34},{34,2},{3,35},{35,3},{4,36},{36... | collective-permute-start | bytes 1572872 | tf_op jit(solution)/shard_map/ppermute | solution.py:302
  176.4 0.1 collective-permute-start.25
  176.6 1.3 collective-permute-start.21
  177.9 3.6 %collective-permute-done.21.refs_7_.refs_8_ = f32[4,16,128]{2,1,0:T(8,128)S(1)} collective-permute-done((f32[4,16,128]{2,1,0:T(8,128)S(1)}, f32[4,16,128]{2,1,0:T(8,128)S(1)}, u32[]{:S(2)}, u32[]{:S(2)}) %collective-permute-start.21) | collective-permute-done | bytes 32800 | tf_op jit(solution)/shard_map/ppermute | solution.py:257
  181.5 4.0 %collective-permute-start.26 = (f32[4,16,128]{2,1,0:T(8,128)S(1)}, f32[4,16,128]{2,1,0:T(8,128)S(1)}, u32[]{:S(2)}, u32[]{:S(2)}) collective-permute-start(f32[4,16,128]{2,1,0:T(8,128)S(1)} %pad_maximum_fusion.11), channel_id=1, source_target_pairs={{0,1},{1,2},{2,3},{3,4},{4,5},{5,6},{6,7},{8,9},{9,10},{10,11},{11... | collective-permute-start | bytes 98312 | tf_op jit(solution)/shard_map/ppermute | solution.py:257
  185.5 1.0 collective-permute-done.26.refs_6_.refs_7_
  186.5 3.7 %rest.7 = (f32[3,16,128,128]{3,2,1,0:T(8,128)S(1)}, f32[2,3,128,128]{3,2,1,0:T(8,128)S(1)}) custom-call(s32[4]{0:T(128)S(1)} %broadcast_select_fusion.refs_0_.order, f32[16,64,128]{2,1,0:T(8,128)S(1)} %row_chunk_0.6.refs_6_.refs_0_.refs_1_, f32[16,64,128]{2,1,0:T(8,128)S(1)} %row_chunk_1.6.refs_0_.refs_7_.refs_2_, ...), custom_call_target="tpu_custom_call" | custom-call | flops 15728640 | bytes 12582912 | tf_op jit(solution)/shard_map/rest/pallas_call | solution.py:159
  190.4 5.9 %collective-permute-start.31 = (f32[2,3,128,128]{3,2,1,0:T(8,128)S(1)}, f32[2,3,128,128]{3,2,1,0:T(8,128)S(1)}, u32[]{:S(2)}, u32[]{:S(2)}) collective-permute-start(f32[2,3,128,128]{3,2,1,0:T(8,128)S(1)} %get-tuple-element.17.s0), channel_id=1, source_target_pairs={{0,16},{8,24},{16,0},{24,8},{1,17},{9,25},{17,1},{25,9},{2,18},{10... | collective-permute-start | bytes 1179656 | tf_op jit(solution)/shard_map/ppermute | solution.py:263
  196.4 18.5 %collective-permute-done.25.refs_1_ = f32[16,64,128]{2,1,0:T(8,128)S(1)} collective-permute-done((f32[16,64,128]{2,1,0:T(8,128)S(1)}, f32[16,64,128]{2,1,0:T(8,128)S(1)}, u32[]{:S(2)}, u32[]{:S(2)}) %collective-permute-start.25) | collective-permute-done | bytes 524320 | tf_op jit(solution)/shard_map/ppermute | solution.py:302
  214.9 0.7 row_chunk_0.7
  215.6 0.3 collective-permute-start.29
  215.8 7.5 %collective-permute-start.28 = (f32[2,64,128]{2,1,0:T(8,128)S(1)}, f32[2,64,128]{2,1,0:T(8,128)S(1)}, u32[]{:S(2)}, u32[]{:S(2)}) collective-permute-start(f32[2,64,128]{2,1,0:T(8,128)S(1)} %get-tuple-element.15.s0), channel_id=1, source_target_pairs={{0,16},{8,24},{16,0},{24,8},{1,17},{9,25},{17,1},{25,9},{2,18},{10... | collective-permute-start | bytes 196616 | tf_op jit(solution)/shard_map/ppermute | solution.py:263
  223.3 2.4 collective-permute-done.29.s3
  225.7 0.7 row_chunk_1.7
  226.4 0.6 collective-permute-start.24
  227.0 0.5 collective-permute-start.23
  227.4 3.4 %collective-permute-start.22 = (f32[2,64,128]{2,1,0:T(8,128)S(1)}, f32[2,64,128]{2,1,0:T(8,128)S(1)}, u32[]{:S(2)}, u32[]{:S(2)}) collective-permute-start(f32[2,64,128]{2,1,0:T(8,128)S(1)} %get-tuple-element.13.s0), channel_id=1, source_target_pairs={{0,8},{8,16},{16,24},{24,0},{1,9},{9,17},{17,25},{25,1},{2,10},{10... | collective-permute-start | bytes 196616 | tf_op jit(solution)/shard_map/ppermute | solution.py:263
  230.9 4.7 %place_rest.1 = (f32[4,16,128,128]{3,2,1,0:T(8,128)}, f32[4,16,128,128]{3,2,1,0:T(8,128)}) custom-call(s32[4]{0:T(128)S(1)} %broadcast_select_fusion.refs_0_.order, f32[3,16,128,128]{3,2,1,0:T(8,128)S(1)} %get-tuple-element.16.field, f32[2,3,128,128]{3,2,1,0:T(8,128)S(1)} %get-tuple-element.17.s0, f32[2,3,128,128]{3,2,1,0:T(8,128)S(1)} %collective-permute-done.30.s1, ...), custom_call_target="tpu_custom_call" | custom-call | flops 7864320 | bytes 12582912 | tf_op jit(solution)/shard_map/place_rest/pallas_call | solution.py:204
  235.6 1.7 place_row.2
  237.2 1.7 place_row.3
  (71 shorter events, 1.0 us)
Async XLA Ops:
  1.7 28.7 %collective-permute-start.3 = (f32[4,16,128]{2,1,0:T(8,128)S(1)}, f32[4,16,128]{2,1,0:T(8,128)S(1)}, u32[]{:S(2)}, u32[]{:S(2)}) collective-permute-start(f32[4,16,128]{2,1,0:T(8,128)S(1)} %reverse_select_fusion.3), channel_id=1, source_target_pairs={{1,0},{2,1},{3,2},{4,3},{5,4},{6,5},{7,6},{9,8},{10,9},{11,10},{12... | collective-permute-start | bytes 98312 | tf_op jit(solution)/shard_map/ppermute | solution.py:257
  3.1 28.3 %collective-permute-start.5 = (f32[4,16,128]{2,1,0:T(8,128)S(1)}, f32[4,16,128]{2,1,0:T(8,128)S(1)}, u32[]{:S(2)}, u32[]{:S(2)}) collective-permute-start(f32[4,16,128]{2,1,0:T(8,128)S(1)} %reverse_select_fusion.2), channel_id=1, source_target_pairs={{0,1},{1,2},{2,3},{3,4},{4,5},{5,6},{6,7},{8,9},{9,10},{10,11},{11... | collective-permute-start | bytes 98312 | tf_op jit(solution)/shard_map/ppermute | solution.py:257
  8.7 22.6 %collective-permute-start.1 = (f32[4,128,128]{2,1,0:T(8,128)S(1)}, f32[4,128,128]{2,1,0:T(8,128)S(1)}, u32[]{:S(2)}, u32[]{:S(2)}) collective-permute-start(f32[4,128,128]{2,1,0:T(8,128)S(1)} %reverse_select_fusion.1), channel_id=1, source_target_pairs={{0,8},{8,16},{16,24},{1,9},{9,17},{17,25},{2,10},{10,18},{18,26},{... | collective-permute-start | bytes 786440 | tf_op jit(solution)/shard_map/ppermute | solution.py:257
  14.8 16.6 %collective-permute-start.2 = (f32[4,128,128]{2,1,0:T(8,128)S(1)}, f32[4,128,128]{2,1,0:T(8,128)S(1)}, u32[]{:S(2)}, u32[]{:S(2)}) collective-permute-start(f32[4,128,128]{2,1,0:T(8,128)S(1)} %reverse_select_fusion), channel_id=1, source_target_pairs={{8,0},{16,8},{24,16},{9,1},{17,9},{25,17},{10,2},{18,10},{26,18},{... | collective-permute-start | bytes 786440 | tf_op jit(solution)/shard_map/ppermute | solution.py:257
  21.3 9.1 %copy-start = (f32[4,16,128,128]{3,2,1,0:T(8,128)S(1)}, f32[4,16,128,128]{3,2,1,0:T(8,128)}, u32[]{:S(2)}) copy-start(f32[4,16,128,128]{3,2,1,0:T(8,128)} %refs_4_.7) | copy-start | bytes 12582916
  23.2 8.1 %copy-start.1 = (f32[4,16,128,128]{3,2,1,0:T(8,128)S(1)}, f32[4,16,128,128]{3,2,1,0:T(8,128)}, u32[]{:S(2)}) copy-start(f32[4,16,128,128]{3,2,1,0:T(8,128)} %refs_3_.1) | copy-start | bytes 12582916
  23.4 22.8 %collective-permute-start = (f32[16,64,128]{2,1,0:T(8,128)S(1)}, f32[16,64,128]{2,1,0:T(8,128)S(1)}, u32[]{:S(2)}, u32[]{:S(2)}) collective-permute-start(f32[16,64,128]{2,1,0:T(8,128)S(1)} %get-tuple-element.43.refs_0_.refs_2_.refs_7_), channel_id=1, source_target_pairs={{0,32},{32,0},{1,33},{33,1},{2,34},{34,2},{3,35},{35,3},{4,36},{36... | collective-permute-start | bytes 1572872 | tf_op jit(solution)/shard_map/ppermute | solution.py:284
  30.5 31.1 %collective-permute-start.6 = (f32[16,64,128]{2,1,0:T(8,128)S(1)}, f32[16,64,128]{2,1,0:T(8,128)S(1)}, u32[]{:S(2)}, u32[]{:S(2)}) collective-permute-start(f32[16,64,128]{2,1,0:T(8,128)S(1)} %get-tuple-element.42.refs_6_.refs_1_.refs_0_), channel_id=1, source_target_pairs={{0,32},{32,0},{1,33},{33,1},{2,34},{34,2},{3,35},{35,3},{4,36},{36... | collective-permute-start | bytes 1572872 | tf_op jit(solution)/shard_map/ppermute | solution.py:284
  46.7 42.0 %collective-permute-start.4 = (f32[16,64,128]{2,1,0:T(8,128)S(1)}, f32[16,64,128]{2,1,0:T(8,128)S(1)}, u32[]{:S(2)}, u32[]{:S(2)}) collective-permute-start(f32[16,64,128]{2,1,0:T(8,128)S(1)} %row_chunk_1.4.refs_0_.refs_2_.refs_7_), channel_id=1, source_target_pairs={{0,32},{32,0},{1,33},{33,1},{2,34},{34,2},{3,35},{35,3},{4,36},{36... | collective-permute-start | bytes 1572872 | tf_op jit(solution)/shard_map/ppermute | solution.py:302
  62.1 23.9 %collective-permute-start.7 = (f32[4,128,128]{2,1,0:T(8,128)S(1)}, f32[4,128,128]{2,1,0:T(8,128)S(1)}, u32[]{:S(2)}, u32[]{:S(2)}) collective-permute-start(f32[4,128,128]{2,1,0:T(8,128)S(1)} %pad_maximum_fusion), channel_id=1, source_target_pairs={{0,8},{8,16},{16,24},{1,9},{9,17},{17,25},{2,10},{10,18},{18,26},{... | collective-permute-start | bytes 786440 | tf_op jit(solution)/shard_map/ppermute | solution.py:257
  68.0 18.0 %collective-permute-start.8 = (f32[4,128,128]{2,1,0:T(8,128)S(1)}, f32[4,128,128]{2,1,0:T(8,128)S(1)}, u32[]{:S(2)}, u32[]{:S(2)}) collective-permute-start(f32[4,128,128]{2,1,0:T(8,128)S(1)} %pad_maximum_fusion.1), channel_id=1, source_target_pairs={{8,0},{16,8},{24,16},{9,1},{17,9},{25,17},{10,2},{18,10},{26,18},{... | collective-permute-start | bytes 786440 | tf_op jit(solution)/shard_map/ppermute | solution.py:257
  69.9 30.6 %collective-permute-start.12 = (f32[16,64,128]{2,1,0:T(8,128)S(1)}, f32[16,64,128]{2,1,0:T(8,128)S(1)}, u32[]{:S(2)}, u32[]{:S(2)}) collective-permute-start(f32[16,64,128]{2,1,0:T(8,128)S(1)} %row_chunk_0.4.refs_6_.refs_1_.refs_0_), channel_id=1, source_target_pairs={{0,32},{32,0},{1,33},{33,1},{2,34},{34,2},{3,35},{35,3},{4,36},{36... | collective-permute-start | bytes 1572872 | tf_op jit(solution)/shard_map/ppermute | solution.py:302
  76.0 5.0 %collective-permute-start.9 = (f32[4,16,128]{2,1,0:T(8,128)S(1)}, f32[4,16,128]{2,1,0:T(8,128)S(1)}, u32[]{:S(2)}, u32[]{:S(2)}) collective-permute-start(f32[4,16,128]{2,1,0:T(8,128)S(1)} %pad_maximum_fusion.6), channel_id=1, source_target_pairs={{1,0},{2,1},{3,2},{4,3},{5,4},{6,5},{7,6},{9,8},{10,9},{11,10},{12... | collective-permute-start | bytes 98312 | tf_op jit(solution)/shard_map/ppermute | solution.py:257
  80.9 5.0 %collective-permute-start.11 = (f32[4,16,128]{2,1,0:T(8,128)S(1)}, f32[4,16,128]{2,1,0:T(8,128)S(1)}, u32[]{:S(2)}, u32[]{:S(2)}) collective-permute-start(f32[4,16,128]{2,1,0:T(8,128)S(1)} %pad_maximum_fusion.7), channel_id=1, source_target_pairs={{0,1},{1,2},{2,3},{3,4},{4,5},{5,6},{6,7},{8,9},{9,10},{10,11},{11... | collective-permute-start | bytes 98312 | tf_op jit(solution)/shard_map/ppermute | solution.py:257
  89.1 47.6 %collective-permute-start.10 = (f32[16,64,128]{2,1,0:T(8,128)S(1)}, f32[16,64,128]{2,1,0:T(8,128)S(1)}, u32[]{:S(2)}, u32[]{:S(2)}) collective-permute-start(f32[16,64,128]{2,1,0:T(8,128)S(1)} %row_chunk_1.5.refs_0_.refs_2_.refs_7_), channel_id=1, source_target_pairs={{0,32},{32,0},{1,33},{33,1},{2,34},{34,2},{3,35},{35,3},{4,36},{36... | collective-permute-start | bytes 1572872 | tf_op jit(solution)/shard_map/ppermute | solution.py:302
  101.1 32.2 %collective-permute-start.13 = (f32[4,128,128]{2,1,0:T(8,128)S(1)}, f32[4,128,128]{2,1,0:T(8,128)S(1)}, u32[]{:S(2)}, u32[]{:S(2)}) collective-permute-start(f32[4,128,128]{2,1,0:T(8,128)S(1)} %pad_maximum_fusion.2), channel_id=1, source_target_pairs={{0,8},{8,16},{16,24},{1,9},{9,17},{17,25},{2,10},{10,18},{18,26},{... | collective-permute-start | bytes 786440 | tf_op jit(solution)/shard_map/ppermute | solution.py:257
  108.6 24.6 %collective-permute-start.14 = (f32[4,128,128]{2,1,0:T(8,128)S(1)}, f32[4,128,128]{2,1,0:T(8,128)S(1)}, u32[]{:S(2)}, u32[]{:S(2)}) collective-permute-start(f32[4,128,128]{2,1,0:T(8,128)S(1)} %pad_maximum_fusion.3), channel_id=1, source_target_pairs={{8,0},{16,8},{24,16},{9,1},{17,9},{25,17},{10,2},{18,10},{26,18},{... | collective-permute-start | bytes 786440 | tf_op jit(solution)/shard_map/ppermute | solution.py:257
  110.6 52.9 %collective-permute-start.18 = (f32[16,64,128]{2,1,0:T(8,128)S(1)}, f32[16,64,128]{2,1,0:T(8,128)S(1)}, u32[]{:S(2)}, u32[]{:S(2)}) collective-permute-start(f32[16,64,128]{2,1,0:T(8,128)S(1)} %row_chunk_0.5.refs_6_.refs_1_.refs_0_), channel_id=1, source_target_pairs={{0,32},{32,0},{1,33},{33,1},{2,34},{34,2},{3,35},{35,3},{4,36},{36... | collective-permute-start | bytes 1572872 | tf_op jit(solution)/shard_map/ppermute | solution.py:302
  117.6 10.3 %collective-permute-start.15 = (f32[4,16,128]{2,1,0:T(8,128)S(1)}, f32[4,16,128]{2,1,0:T(8,128)S(1)}, u32[]{:S(2)}, u32[]{:S(2)}) collective-permute-start(f32[4,16,128]{2,1,0:T(8,128)S(1)} %pad_maximum_fusion.8), channel_id=1, source_target_pairs={{1,0},{2,1},{3,2},{4,3},{5,4},{6,5},{7,6},{9,8},{10,9},{11,10},{12... | collective-permute-start | bytes 98312 | tf_op jit(solution)/shard_map/ppermute | solution.py:257
  127.9 5.3 %collective-permute-start.17 = (f32[4,16,128]{2,1,0:T(8,128)S(1)}, f32[4,16,128]{2,1,0:T(8,128)S(1)}, u32[]{:S(2)}, u32[]{:S(2)}) collective-permute-start(f32[4,16,128]{2,1,0:T(8,128)S(1)} %pad_maximum_fusion.9), channel_id=1, source_target_pairs={{0,1},{1,2},{2,3},{3,4},{4,5},{5,6},{6,7},{8,9},{9,10},{10,11},{11... | collective-permute-start | bytes 98312 | tf_op jit(solution)/shard_map/ppermute | solution.py:257
  164.1 22.5 %collective-permute-start.19 = (f32[4,128,128]{2,1,0:T(8,128)S(1)}, f32[4,128,128]{2,1,0:T(8,128)S(1)}, u32[]{:S(2)}, u32[]{:S(2)}) collective-permute-start(f32[4,128,128]{2,1,0:T(8,128)S(1)} %pad_maximum_fusion.4), channel_id=1, source_target_pairs={{0,8},{8,16},{16,24},{1,9},{9,17},{17,25},{2,10},{10,18},{18,26},{... | collective-permute-start | bytes 786440 | tf_op jit(solution)/shard_map/ppermute | solution.py:257
  168.2 18.3 %collective-permute-start.20 = (f32[4,128,128]{2,1,0:T(8,128)S(1)}, f32[4,128,128]{2,1,0:T(8,128)S(1)}, u32[]{:S(2)}, u32[]{:S(2)}) collective-permute-start(f32[4,128,128]{2,1,0:T(8,128)S(1)} %pad_maximum_fusion.5), channel_id=1, source_target_pairs={{8,0},{16,8},{24,16},{9,1},{17,9},{25,17},{10,2},{18,10},{26,18},{... | collective-permute-start | bytes 786440 | tf_op jit(solution)/shard_map/ppermute | solution.py:257
  170.2 45.6 %collective-permute-start.16 = (f32[16,64,128]{2,1,0:T(8,128)S(1)}, f32[16,64,128]{2,1,0:T(8,128)S(1)}, u32[]{:S(2)}, u32[]{:S(2)}) collective-permute-start(f32[16,64,128]{2,1,0:T(8,128)S(1)} %row_chunk_1.6.refs_0_.refs_7_.refs_2_), channel_id=1, source_target_pairs={{0,32},{32,0},{1,33},{33,1},{2,34},{34,2},{3,35},{35,3},{4,36},{36... | collective-permute-start | bytes 1572872 | tf_op jit(solution)/shard_map/ppermute | solution.py:302
  176.4 38.5 %collective-permute-start.25 = (f32[16,64,128]{2,1,0:T(8,128)S(1)}, f32[16,64,128]{2,1,0:T(8,128)S(1)}, u32[]{:S(2)}, u32[]{:S(2)}) collective-permute-start(f32[16,64,128]{2,1,0:T(8,128)S(1)} %row_chunk_0.6.refs_6_.refs_0_.refs_1_), channel_id=1, source_target_pairs={{0,32},{32,0},{1,33},{33,1},{2,34},{34,2},{3,35},{35,3},{4,36},{36... | collective-permute-start | bytes 1572872 | tf_op jit(solution)/shard_map/ppermute | solution.py:302
  176.6 5.0 %collective-permute-start.21 = (f32[4,16,128]{2,1,0:T(8,128)S(1)}, f32[4,16,128]{2,1,0:T(8,128)S(1)}, u32[]{:S(2)}, u32[]{:S(2)}) collective-permute-start(f32[4,16,128]{2,1,0:T(8,128)S(1)} %pad_maximum_fusion.10), channel_id=1, source_target_pairs={{1,0},{2,1},{3,2},{4,3},{5,4},{6,5},{7,6},{9,8},{10,9},{11,10},{12... | collective-permute-start | bytes 98312 | tf_op jit(solution)/shard_map/ppermute | solution.py:257
  181.5 5.0 %collective-permute-start.26 = (f32[4,16,128]{2,1,0:T(8,128)S(1)}, f32[4,16,128]{2,1,0:T(8,128)S(1)}, u32[]{:S(2)}, u32[]{:S(2)}) collective-permute-start(f32[4,16,128]{2,1,0:T(8,128)S(1)} %pad_maximum_fusion.11), channel_id=1, source_target_pairs={{0,1},{1,2},{2,3},{3,4},{4,5},{5,6},{6,7},{8,9},{9,10},{10,11},{11... | collective-permute-start | bytes 98312 | tf_op jit(solution)/shard_map/ppermute | solution.py:257
  190.3 36.1 %collective-permute-start.32 = (f32[2,3,128,128]{3,2,1,0:T(8,128)S(1)}, f32[2,3,128,128]{3,2,1,0:T(8,128)S(1)}, u32[]{:S(2)}, u32[]{:S(2)}) collective-permute-start(f32[2,3,128,128]{3,2,1,0:T(8,128)S(1)} %get-tuple-element.17.s0), channel_id=1, source_target_pairs={{0,24},{8,0},{16,8},{24,16},{1,25},{9,1},{17,9},{25,17},{2,26},{10... | collective-permute-start | bytes 1179656 | tf_op jit(solution)/shard_map/ppermute | solution.py:263
  190.4 36.6 %collective-permute-start.31 = (f32[2,3,128,128]{3,2,1,0:T(8,128)S(1)}, f32[2,3,128,128]{3,2,1,0:T(8,128)S(1)}, u32[]{:S(2)}, u32[]{:S(2)}) collective-permute-start(f32[2,3,128,128]{3,2,1,0:T(8,128)S(1)} %get-tuple-element.17.s0), channel_id=1, source_target_pairs={{0,16},{8,24},{16,0},{24,8},{1,17},{9,25},{17,1},{25,9},{2,18},{10... | collective-permute-start | bytes 1179656 | tf_op jit(solution)/shard_map/ppermute | solution.py:263
  196.3 31.2 %collective-permute-start.30 = (f32[2,3,128,128]{3,2,1,0:T(8,128)S(1)}, f32[2,3,128,128]{3,2,1,0:T(8,128)S(1)}, u32[]{:S(2)}, u32[]{:S(2)}) collective-permute-start(f32[2,3,128,128]{3,2,1,0:T(8,128)S(1)} %get-tuple-element.17.s0), channel_id=1, source_target_pairs={{0,8},{8,16},{16,24},{24,0},{1,9},{9,17},{17,25},{25,1},{2,10},{10... | collective-permute-start | bytes 1179656 | tf_op jit(solution)/shard_map/ppermute | solution.py:263
  215.6 10.1 %collective-permute-start.29 = (f32[2,64,128]{2,1,0:T(8,128)S(1)}, f32[2,64,128]{2,1,0:T(8,128)S(1)}, u32[]{:S(2)}, u32[]{:S(2)}) collective-permute-start(f32[2,64,128]{2,1,0:T(8,128)S(1)} %get-tuple-element.15.s0), channel_id=1, source_target_pairs={{0,24},{8,0},{16,8},{24,16},{1,25},{9,1},{17,9},{25,17},{2,26},{10... | collective-permute-start | bytes 196616 | tf_op jit(solution)/shard_map/ppermute | solution.py:263
  215.8 19.7 %collective-permute-start.28 = (f32[2,64,128]{2,1,0:T(8,128)S(1)}, f32[2,64,128]{2,1,0:T(8,128)S(1)}, u32[]{:S(2)}, u32[]{:S(2)}) collective-permute-start(f32[2,64,128]{2,1,0:T(8,128)S(1)} %get-tuple-element.15.s0), channel_id=1, source_target_pairs={{0,16},{8,24},{16,0},{24,8},{1,17},{9,25},{17,1},{25,9},{2,18},{10... | collective-permute-start | bytes 196616 | tf_op jit(solution)/shard_map/ppermute | solution.py:263
  225.7 9.9 %collective-permute-start.27 = (f32[2,64,128]{2,1,0:T(8,128)S(1)}, f32[2,64,128]{2,1,0:T(8,128)S(1)}, u32[]{:S(2)}, u32[]{:S(2)}) collective-permute-start(f32[2,64,128]{2,1,0:T(8,128)S(1)} %get-tuple-element.15.s0), channel_id=1, source_target_pairs={{0,8},{8,16},{16,24},{24,0},{1,9},{9,17},{17,25},{25,1},{2,10},{10... | collective-permute-start | bytes 196616 | tf_op jit(solution)/shard_map/ppermute | solution.py:263
  226.4 10.9 %collective-permute-start.24 = (f32[2,64,128]{2,1,0:T(8,128)S(1)}, f32[2,64,128]{2,1,0:T(8,128)S(1)}, u32[]{:S(2)}, u32[]{:S(2)}) collective-permute-start(f32[2,64,128]{2,1,0:T(8,128)S(1)} %get-tuple-element.13.s0), channel_id=1, source_target_pairs={{0,24},{8,0},{16,8},{24,16},{1,25},{9,1},{17,9},{25,17},{2,26},{10... | collective-permute-start | bytes 196616 | tf_op jit(solution)/shard_map/ppermute | solution.py:263
  227.0 10.3 %collective-permute-start.23 = (f32[2,64,128]{2,1,0:T(8,128)S(1)}, f32[2,64,128]{2,1,0:T(8,128)S(1)}, u32[]{:S(2)}, u32[]{:S(2)}) collective-permute-start(f32[2,64,128]{2,1,0:T(8,128)S(1)} %get-tuple-element.13.s0), channel_id=1, source_target_pairs={{0,16},{8,24},{16,0},{24,8},{1,17},{9,25},{17,1},{25,9},{2,18},{10... | collective-permute-start | bytes 196616 | tf_op jit(solution)/shard_map/ppermute | solution.py:263
  227.4 9.8 %collective-permute-start.22 = (f32[2,64,128]{2,1,0:T(8,128)S(1)}, f32[2,64,128]{2,1,0:T(8,128)S(1)}, u32[]{:S(2)}, u32[]{:S(2)}) collective-permute-start(f32[2,64,128]{2,1,0:T(8,128)S(1)} %get-tuple-element.13.s0), channel_id=1, source_target_pairs={{0,8},{8,16},{16,24},{24,0},{1,9},{9,17},{17,25},{25,1},{2,10},{10... | collective-permute-start | bytes 196616 | tf_op jit(solution)/shard_map/ppermute | solution.py:263

commit v2 on v0

v2 whole, which is shorter than its diff:
```python
import functools

import jax
import jax.numpy as jnp
from jax import lax
from jax.experimental import pallas as pl
from jax.experimental.pallas import tpu as pltpu
from jax.sharding import PartitionSpec as P


STEPS = 4
MIB = 1 << 20
EVEN_X, EVEN_Z = 4, 5
VMEM = pl.BlockSpec(memory_space=pltpu.VMEM)
SMEM = pl.BlockSpec(memory_space=pltpu.SMEM)
ANY = pl.BlockSpec(memory_space=pl.ANY)


def cost(size, flops, reads):
    return pl.CostEstimate(flops=flops * size, bytes_accessed=4 * reads * size, transcendentals=0)


def cells(a, low_x, high_x, near, far, low_z, high_z, crowding):
    length = a.shape[0]
    z = lax.broadcasted_iota(jnp.int32, a.shape, 0)
    down = jnp.where(z == 0, low_z, pltpu.roll(a, 1, 0))
    up = jnp.where(z == length - 1, high_z, pltpu.roll(a, length - 1, 0))
    spread = low_x + high_x + near + far + down + up - 6.0 * a
    return a + 0.1 * spread + 0.2 * a * (1.0 - a * crowding)


def over_x(n, visit):
    visit(0, None, 1)

    def inner(x, carry):
        visit(x, x - 1, x + 1)
        return carry

    lax.fori_loop(1, n - 1, inner, 0)
    visit(n - 1, n - 2, None)


def line_sums(column, n):
    mean = lax.fori_loop(1, n, lambda x, s: s + column(x), column(0)) / n

    def add(x, s):
        d = column(x) - mean
        return s + d * d

    return mean, lax.fori_loop(0, n, add, jnp.zeros_like(mean))


def sides(info, row, ghosts):
    lon_a, lon_b, lev_a, lev_b = ghosts
    even_x, even_z = info[EVEN_X] == 1, info[EVEN_Z] == 1
    low_x = lambda: jnp.where(even_x, lon_b[row], lon_a[row])
    high_x = lambda: jnp.where(even_x, lon_a[row], lon_b[row])

    def ends_z(x):
        a, b = lev_a[row, pl.ds(x, 1), :], lev_b[row, pl.ds(x, 1), :]
        return jnp.where(even_z, b, a), jnp.where(even_z, a, b)

    return low_x, high_x, ends_z


def edge_kernel(mapped, info, *refs):
    if mapped:
        field, lon_a, lon_b, lev_a, lev_b = refs
        rows = [field.at[info[row]] for row in range(4)]
    else:
        first, field, lon_a, lon_b, lev_a, lev_b = refs
        rows = [first, *(field.at[row] for row in range(3))]
    n, length = rows[0].shape[0], rows[0].shape[1]
    for row, values in enumerate(rows):
        at = info[EVEN_X] * (n - 1)
        lon_a[row] = values[at]
        lon_b[row] = values[n - 1 - at]
        at = info[EVEN_Z] * (length - 1)
        for x in range(n):
            lev_a[row, x : x + 1, :] = values[x, pl.ds(at, 1), :]
            lev_b[row, x : x + 1, :] = values[x, pl.ds(length - 1 - at, 1), :]


def edges(info, first, field):
    mapped = first is None
    _, n, length, species = field.shape
    lon = jax.ShapeDtypeStruct((4, length, species), jnp.float32)
    lev = jax.ShapeDtypeStruct((4, n, species), jnp.float32)
    args = [field] if mapped else [first, field]
    return pl.pallas_call(
        functools.partial(edge_kernel, mapped),
        out_shape=[lon, lon, lev, lev],
        in_specs=[SMEM] + [VMEM] * len(args),
        out_specs=[VMEM] * 4,
        compiler_params=pltpu.CompilerParams(vmem_limit_bytes=16 * MIB),
        cost_estimate=cost(8 * (length + n) * species, 1, 2),
        name="edges",
    )(info, *args)


def row_kernel(info, centre, near, far, crowding, lon_a, lon_b, lev_a, lev_b, *out):
    new = out[0]
    n = centre.shape[0]
    low, high, ends_z = sides(info, 0, (lon_a, lon_b, lev_a, lev_b))

    def visit(x, before, after):
        low_x = low() if before is None else centre[before]
        high_x = high() if after is None else centre[after]
        low_z, high_z = ends_z(x)
        new[x] = cells(
            centre[x], low_x, high_x, near[x], far[0, x], low_z, high_z, crowding[0, x]
        )

    over_x(n, visit)


def row_end_kernel(info, centre, near, far, crowding, lon_a, lon_b, lev_a, lev_b, _, new, sums, ended, sem):
    row_kernel(info, centre, near, far, crowding, lon_a, lon_b, lev_a, lev_b, new)
    copy = pltpu.make_async_copy(new, ended.at[info[0]], sem)
    copy.start()
    sums[0], sums[1] = line_sums(lambda x: new[x], centre.shape[0])
    copy.wait()


def row_step(info, centre, received, field, crowding, ghosts, mapped, ended=None):
    n, length, species = centre.shape
    full = lambda a: pl.BlockSpec(a.shape, lambda i, info: (0,) * a.ndim)
    one = (1, n, length, species)
    out_shape = [jax.ShapeDtypeStruct(centre.shape, jnp.float32)]
    out_specs = [full(centre)]
    extra, more = [], {}
    if ended is not None:
        out_shape += [
            jax.ShapeDtypeStruct((2, length, species), jnp.float32),
            jax.ShapeDtypeStruct(ended.shape, jnp.float32),
        ]
        out_specs += [full(out_shape[1]), ANY]
        extra, more = [ended], {"input_output_aliases": {9: 2}}
    return pl.pallas_call(
        row_kernel if ended is None else row_end_kernel,
        grid_spec=pltpu.PrefetchScalarGridSpec(
            num_scalar_prefetch=1,
            grid=(1,),
            in_specs=[
                full(centre),
                full(received),
                pl.BlockSpec(one, lambda i, info: (info[1] if mapped else 0, 0, 0, 0)),
                pl.BlockSpec(one, lambda i, info: (info[0], 0, 0, 0)),
                *map(full, ghosts),
                *([ANY] * len(extra)),
            ],
            out_specs=out_specs,
            scratch_shapes=[pltpu.SemaphoreType.DMA] * len(extra),
        ),
        out_shape=out_shape,
        compiler_params=pltpu.CompilerParams(vmem_limit_bytes=20 * MIB),
        cost_estimate=cost(centre.size, 20, 5),
        name="row",
        **more,
    )(info, centre, received, field, crowding, *ghosts, *extra)


def rest_kernel(mapped, final, info, *refs):
    if mapped:
        first, refs = None, refs
    else:
        first, refs = refs[0], refs[1:]
    field, crowding, lon_a, lon_b, lev_a, lev_b, out = refs[:7]
    n = field.shape[1]
    copies = []
    for row in range(3):
        at = info[row + 1] if mapped else row
        beyond = info[row + 2] if mapped and row < 2 else row + 1
        crowd_at = info[row + 1]
        low, high, ends_z = sides(info, row + 1, (lon_a, lon_b, lev_a, lev_b))

        def visit(x, before, after):
            low_x = low() if before is None else field[at, before]
            high_x = high() if after is None else field[at, after]
            if mapped:
                near = field[info[row], x]
            else:
                near = first[x] if row == 0 else field[row - 1, x]
            far = 0.0 if row == 2 else field[beyond, x]
            low_z, high_z = ends_z(x)
            out[row, x] = cells(
                field[at, x], low_x, high_x, near, far, low_z, high_z, crowding[crowd_at, x]
            )

        over_x(n, visit)
        if final:
            sums, ended, sem = refs[7:]
            copies.append(pltpu.make_async_copy(out.at[row], ended.at[info[row + 1]], sem.at[row]))
            copies[-1].start()
            sums[0, row], sums[1, row] = line_sums(lambda x: out[row, x], n)
    for copy in copies:
        copy.wait()


def rest_step(info, first, field, crowding, ghosts, final):
    mapped = first is None
    _, n, length, species = field.shape
    out_shape = [jax.ShapeDtypeStruct((3, n, length, species), jnp.float32)]
    out_specs, scratch = [VMEM], []
    if final:
        out_shape += [
            jax.ShapeDtypeStruct((2, 3, length, species), jnp.float32),
            jax.ShapeDtypeStruct((4, n, length, species), jnp.float32),
        ]
        out_specs += [VMEM, ANY]
        scratch = [pltpu.SemaphoreType.DMA((3,))]
    args = [*([] if mapped else [first]), field, crowding, *ghosts]
    return pl.pallas_call(
        functools.partial(rest_kernel, mapped, final),
        out_shape=out_shape,
        in_specs=[SMEM] + [VMEM] * len(args),
        out_specs=out_specs,
        scratch_shapes=scratch,
        compiler_params=pltpu.CompilerParams(vmem_limit_bytes=24 * MIB),
        cost_estimate=cost(3 * n * length * species, 20, 4),
        name="rest",
    )(info, *args)


def merged(a, b, n):
    d = a[0] - b[0]
    return jnp.stack([0.5 * (a[0] + b[0]), a[1] + b[1] + (0.5 * n) * d * d])


def line_factors(a, b, n):
    d = a[0] - b[0]
    variance = (a[1] + b[1] + (0.5 * n) * d * d) / (2 * n)
    return 0.5 * (a[0] + b[0]), lax.rsqrt(variance + 0.0001)


def scale_kernel(rows, info, field, one, two, *refs):
    scaled, buffer, sem = refs[-3:]
    n = buffer.shape[1]
    copies = []
    for k, row in enumerate(rows):
        values = field if len(rows) == 1 else field.at[k]
        mean, factor = line_factors(*([s[0, k], s[1, k]] for s in (one, two)), 2 * n)

        def visit(x, carry):
            buffer[k, x] = (values[x] - mean) * factor
            return carry

        lax.fori_loop(0, n, visit, 0)
        copies.append(pltpu.make_async_copy(buffer.at[k], scaled.at[info[row]], sem.at[k]))
        copies[-1].start()
    for copy in copies:
        copy.wait()


def scale(info, rows, field, one, two, scaled=None):
    n, length, species = field.shape[-3:]
    count = len(rows)
    whole = jax.ShapeDtypeStruct((4, n, length, species), jnp.float32)
    extra, more = ([], {}) if scaled is None else ([scaled], {"input_output_aliases": {4: 0}})
    return pl.pallas_call(
        functools.partial(scale_kernel, rows),
        out_shape=whole,
        in_specs=[SMEM] + [VMEM] * 3 + [ANY] * len(extra),
        out_specs=ANY,
        scratch_shapes=[
            pltpu.VMEM((count, n, length, species), jnp.float32),
            pltpu.SemaphoreType.DMA((count,)),
        ],
        compiler_params=pltpu.CompilerParams(vmem_limit_bytes=16 * MIB),
        cost_estimate=cost(field.size, 3, 2),
        name="scale",
        **more,
    )(info, field, one, two, *extra)


def paired(array, axis, pairs):
    return lax.ppermute(array, axis, [*pairs, *((b, a) for a, b in pairs)])


def exchanged(sent):
    lon_a, lon_b, lev_a, lev_b = sent
    return (
        paired(lon_a, "lon", [(0, 1), (2, 3)]),
        paired(lon_b, "lon", [(1, 2)]),
        paired(lev_a, "lev", [(0, 1), (2, 3), (4, 5), (6, 7)]),
        paired(lev_b, "lev", [(1, 2), (3, 4), (5, 6)]),
    )


def halves_of_lines(sums, n):
    half = merged(sums, paired(sums, "lon", [(0, 1), (2, 3)]), n)
    return half, paired(half, "lon", [(0, 2), (1, 3)])


def steps(density, crowding):
    rows, n, _, _ = density.shape
    flipped = lax.axis_index("lat") == 0
    order = [jnp.where(flipped, rows - 1 - row, row) for row in range(rows)]
    row = lax.dynamic_index_in_dim(density, order[0], 0, keepdims=False)
    arriving = paired(row, "lat", [(0, 1)])
    even = [1 - lax.axis_index(axis) % 2 for axis in ("lon", "lev")]
    info = jnp.stack([*order, *even]).astype(jnp.int32)
    rest = None
    for step in range(STEPS):
        start, final = step == 0, step == STEPS - 1
        field = density if start else rest
        first = None if start else row
        sent = edges(info, first, field)
        ghosts = exchanged(sent)
        done = rest_step(info, first, field, crowding, ghosts, final)
        rest = done[0]
        ended = done[2] if final else None
        row_done = row_step(info, row, arriving, field, crowding, ghosts, start, ended)
        row = row_done[0]
        if not final:
            arriving = paired(row, "lat", [(0, 1)])
    halves = halves_of_lines(done[1], n)
    row_halves = halves_of_lines(row_done[1][:, None], n)
    scaled = scale(info, (1, 2, 3), rest, *halves)
    scaled = scale(info, (0,), row, *row_halves, scaled)
    return scaled, row_done[2]


def solution(mesh):
    placed = P(("trial", "lat"), "lon", "lev", None)
    return jax.shard_map(
        steps,
        mesh=mesh,
        in_specs=(placed, placed),
        out_specs=(placed, placed),
        check_vma=False,
    )
```

time: 276 us -> 223 us (0.81)
  the two profiles are of different devices: /device:TPU:1 before, /device:TPU:92 now
where the time goes in v2:
time: 223 us; the launch traced here: 222 us
  waiting for transfers between devices  126 us (57%)
  starting transfers between devices  64.7 us (29%)
  Pallas kernels  25.4 us (11%)
  local copies, waits for them, and re-layouts  5.77 us (3%)
    ppermute x24, waiting for transfers between devices, paired(): return lax.ppermute(array, axis, [*pairs, *((b, a) for a, b in pairs)])  126 us
    ppermute x24, starting transfers between devices, paired(): return lax.ppermute(array, axis, [*pairs, *((b, a) for a, b in pairs)])  64.7 us
    pallas_call x4, Pallas kernels, rest_step(): pl.pallas_call(functools.partial(rest_kernel, mapped, final), out_shape=o...  12.7 us
    pallas_call x4, Pallas kernels, row_step(): pl.pallas_call(row_kernel if ended is None else row_end_kernel, grid_spec...  6.08 us
  transfers between devices with their start and end apart: 24, of which 15 were waited for; matrix products, arithmetic and copies ran while one was open for 0% of the time, Pallas kernels for 9%

profile of v2, /device:TPU:92, one launch (start us, length us, event | category | flops | bytes accessed | tf_op | source)
XLA Modules:
  0.0 222.5 jit_solution(6368716436460703086)
XLA Ops:
  0.6 1.3 dynamic-slice_bitcast_fusion.centre
  1.9 5.5 %collective-permute-start = (f32[16,128,128]{2,1,0:T(8,128)S(1)}, f32[16,128,128]{2,1,0:T(8,128)S(1)}, u32[]{:S(2)}, u32[]{:S(2)}) collective-permute-start(f32[16,128,128]{2,1,0:T(8,128)S(1)} %dynamic-slice_bitcast_fusion.centre), channel_id=1, source_target_pairs={{0,32},{32,0},{1,33},{33,1},{2,34},{34,2},{3,35},{35,3},{4,36},{36... | collective-permute-start | bytes 3145736 | tf_op jit(solution)/shard_map/ppermute | solution.py:277
  7.4 0.1 stack.41.info
  7.5 2.2 copy-done.1
  9.7 0.6 edges.4
  10.3 0.1 collective-permute-start.1
  10.4 2.5 %collective-permute-start.2 = (f32[4,128,128]{2,1,0:T(8,128)S(1)}, f32[4,128,128]{2,1,0:T(8,128)S(1)}, u32[]{:S(2)}, u32[]{:S(2)}) collective-permute-start(f32[4,128,128]{2,1,0:T(8,128)S(1)} %get-tuple-element.25), channel_id=1, source_target_pairs={{8,16},{16,8},{9,17},{17,9},{10,18},{18,10},{11,19},{19,11},{12,20... | collective-permute-start | bytes 786440 | tf_op jit(solution)/shard_map/ppermute | solution.py:277
  13.0 2.2 collective-permute-start.3
  15.1 2.1 collective-permute-start.4
  17.2 2.5 %collective-permute-done.3.lev_a.refs_4_ = f32[4,16,128]{2,1,0:T(8,128)S(1)} collective-permute-done((f32[4,16,128]{2,1,0:T(8,128)S(1)}, f32[4,16,128]{2,1,0:T(8,128)S(1)}, u32[]{:S(2)}, u32[]{:S(2)}) %collective-permute-start.3) | collective-permute-done | bytes 32800 | tf_op jit(solution)/shard_map/ppermute | solution.py:277
  19.7 2.1 collective-permute-done.4.lev_b.refs_5_
  21.8 0.0 collective-permute-done.1.lon_a.refs_2_
  21.8 0.0 collective-permute-done.2.lon_b.refs_3_
  21.8 31.7 %collective-permute-done.near = f32[16,128,128]{2,1,0:T(8,128)S(1)} collective-permute-done((f32[16,128,128]{2,1,0:T(8,128)S(1)}, f32[16,128,128]{2,1,0:T(8,128)S(1)}, u32[]{:S(2)}, u32[]{:S(2)}) %collective-permute-start) | collective-permute-done | bytes 1048608 | tf_op jit(solution)/shard_map/ppermute | solution.py:277
  53.6 2.2 copy-done.2
  55.7 1.3 row.4.refs_0_.centre
  57.0 5.1 %collective-permute-start.5 = (f32[16,128,128]{2,1,0:T(8,128)S(1)}, f32[16,128,128]{2,1,0:T(8,128)S(1)}, u32[]{:S(2)}, u32[]{:S(2)}) collective-permute-start(f32[16,128,128]{2,1,0:T(8,128)S(1)} %row.4.refs_0_.centre), channel_id=1, source_target_pairs={{0,32},{32,0},{1,33},{33,1},{2,34},{34,2},{3,35},{35,3},{4,36},{36... | collective-permute-start | bytes 3145736 | tf_op jit(solution)/shard_map/ppermute | solution.py:277
  62.1 2.8 %rest.4.refs_1_.far = f32[3,16,128,128]{3,2,1,0:T(8,128)S(1)} custom-call(s32[6]{0:T(128)S(1)} %stack.41.info, f32[4,16,128,128]{3,2,1,0:T(8,128)S(1)} %copy-done.3, f32[4,16,128,128]{3,2,1,0:T(8,128)S(1)} %copy-done, f32[4,128,128]{2,1,0:T(8,128)S(1)} %collective-permute-done.1.lon_a.refs_2_, f32[4,128,128]{2,1,0:T(8,128)S(1)} %collective-permute-done.2.lon_b.refs_3_, ...), custom_call_target="tpu_custom_call" | custom-call | flops 15728640 | bytes 12582912 | tf_op jit(solution)/shard_map/rest/pallas_call | solution.py:213
  64.9 0.6 edges.5
  65.5 0.1 collective-permute-start.6
  65.6 2.5 %collective-permute-start.7 = (f32[4,128,128]{2,1,0:T(8,128)S(1)}, f32[4,128,128]{2,1,0:T(8,128)S(1)}, u32[]{:S(2)}, u32[]{:S(2)}) collective-permute-start(f32[4,128,128]{2,1,0:T(8,128)S(1)} %get-tuple-element.29), channel_id=1, source_target_pairs={{8,16},{16,8},{9,17},{17,9},{10,18},{18,10},{11,19},{19,11},{12,20... | collective-permute-start | bytes 786440 | tf_op jit(solution)/shard_map/ppermute | solution.py:277
  68.2 2.2 collective-permute-start.8
  70.3 2.1 collective-permute-start.9
  72.4 2.5 %collective-permute-done.8.lev_a.refs_5_ = f32[4,16,128]{2,1,0:T(8,128)S(1)} collective-permute-done((f32[4,16,128]{2,1,0:T(8,128)S(1)}, f32[4,16,128]{2,1,0:T(8,128)S(1)}, u32[]{:S(2)}, u32[]{:S(2)}) %collective-permute-start.8) | collective-permute-done | bytes 32800 | tf_op jit(solution)/shard_map/ppermute | solution.py:277
  74.9 2.1 collective-permute-done.9.lev_b.refs_6_
  77.0 0.0 collective-permute-done.6.lon_a.refs_3_
  77.0 43.6 %collective-permute-done.5.near = f32[16,128,128]{2,1,0:T(8,128)S(1)} collective-permute-done((f32[16,128,128]{2,1,0:T(8,128)S(1)}, f32[16,128,128]{2,1,0:T(8,128)S(1)}, u32[]{:S(2)}, u32[]{:S(2)}) %collective-permute-start.5) | collective-permute-done | bytes 1048608 | tf_op jit(solution)/shard_map/ppermute | solution.py:277
  120.7 1.3 row.5.refs_0_.centre
  122.0 3.6 %collective-permute-start.10 = (f32[16,128,128]{2,1,0:T(8,128)S(1)}, f32[16,128,128]{2,1,0:T(8,128)S(1)}, u32[]{:S(2)}, u32[]{:S(2)}) collective-permute-start(f32[16,128,128]{2,1,0:T(8,128)S(1)} %row.5.refs_0_.centre), channel_id=1, source_target_pairs={{0,32},{32,0},{1,33},{33,1},{2,34},{34,2},{3,35},{35,3},{4,36},{36... | collective-permute-start | bytes 3145736 | tf_op jit(solution)/shard_map/ppermute | solution.py:277
  125.6 2.7 %rest.5.refs_1_.far = f32[3,16,128,128]{3,2,1,0:T(8,128)S(1)} custom-call(s32[6]{0:T(128)S(1)} %stack.41.info, f32[16,128,128]{2,1,0:T(8,128)S(1)} %row.4.refs_0_.centre, f32[3,16,128,128]{3,2,1,0:T(8,128)S(1)} %rest.4.refs_1_.far, f32[4,16,128,128]{3,2,1,0:T(8,128)S(1)} %copy-done, f32[4,128,128]{2,1,0:T(8,128)S(1)} %collective-permute-done.6.lon_a.refs_3_, ...), custom_call_target="tpu_custom_call" | custom-call | flops 15728640 | bytes 12582912 | tf_op jit(solution)/shard_map/rest/pallas_call | solution.py:213
  128.3 0.6 edges.6
  129.0 0.1 collective-permute-start.11
  129.1 1.9 collective-permute-start.12
  131.0 21.4 %collective-permute-start.13 = (f32[4,16,128]{2,1,0:T(8,128)S(1)}, f32[4,16,128]{2,1,0:T(8,128)S(1)}, u32[]{:S(2)}, u32[]{:S(2)}) collective-permute-start(f32[4,16,128]{2,1,0:T(8,128)S(1)} %get-tuple-element.34), channel_id=1, source_target_pairs={{0,1},{2,3},{4,5},{6,7},{1,0},{3,2},{5,4},{7,6},{8,9},{10,11},{12,... | collective-permute-start | bytes 98312 | tf_op jit(solution)/shard_map/ppermute | solution.py:277
  152.5 1.9 collective-permute-start.14
  154.4 2.7 %collective-permute-done.13.lev_a.refs_5_ = f32[4,16,128]{2,1,0:T(8,128)S(1)} collective-permute-done((f32[4,16,128]{2,1,0:T(8,128)S(1)}, f32[4,16,128]{2,1,0:T(8,128)S(1)}, u32[]{:S(2)}, u32[]{:S(2)}) %collective-permute-start.13) | collective-permute-done | bytes 32800 | tf_op jit(solution)/shard_map/ppermute | solution.py:277
  157.0 2.1 collective-permute-done.14.lev_b.refs_6_
  159.2 13.9 %collective-permute-done.10.near = f32[16,128,128]{2,1,0:T(8,128)S(1)} collective-permute-done((f32[16,128,128]{2,1,0:T(8,128)S(1)}, f32[16,128,128]{2,1,0:T(8,128)S(1)}, u32[]{:S(2)}, u32[]{:S(2)}) %collective-permute-start.10) | collective-permute-done | bytes 1048608 | tf_op jit(solution)/shard_map/ppermute | solution.py:277
  173.1 1.3 row.6.refs_0_.centre
  174.3 2.6 %collective-permute-start.15 = (f32[16,128,128]{2,1,0:T(8,128)S(1)}, f32[16,128,128]{2,1,0:T(8,128)S(1)}, u32[]{:S(2)}, u32[]{:S(2)}) collective-permute-start(f32[16,128,128]{2,1,0:T(8,128)S(1)} %row.6.refs_0_.centre), channel_id=1, source_target_pairs={{0,32},{32,0},{1,33},{33,1},{2,34},{34,2},{3,35},{35,3},{4,36},{36... | collective-permute-start | bytes 3145736 | tf_op jit(solution)/shard_map/ppermute | solution.py:277
  176.9 2.8 %rest.6.refs_1_.far = f32[3,16,128,128]{3,2,1,0:T(8,128)S(1)} custom-call(s32[6]{0:T(128)S(1)} %stack.41.info, f32[16,128,128]{2,1,0:T(8,128)S(1)} %row.5.refs_0_.centre, f32[3,16,128,128]{3,2,1,0:T(8,128)S(1)} %rest.5.refs_1_.far, f32[4,16,128,128]{3,2,1,0:T(8,128)S(1)} %copy-done, f32[4,128,128]{2,1,0:T(8,128)S(1)} %collective-permute-done.11.lon_a.refs_3_, ...), custom_call_target="tpu_custom_call" | custom-call | flops 15728640 | bytes 12582912 | tf_op jit(solution)/shard_map/rest/pallas_call | solution.py:213
  179.7 0.6 edges.7
  180.3 0.1 collective-permute-start.16
  180.4 1.9 collective-permute-start.17
  182.3 0.3 collective-permute-start.18
  182.6 3.8 %collective-permute-start.19 = (f32[4,16,128]{2,1,0:T(8,128)S(1)}, f32[4,16,128]{2,1,0:T(8,128)S(1)}, u32[]{:S(2)}, u32[]{:S(2)}) collective-permute-start(f32[4,16,128]{2,1,0:T(8,128)S(1)} %get-tuple-element.39), channel_id=1, source_target_pairs={{1,2},{3,4},{5,6},{2,1},{4,3},{6,5},{9,10},{11,12},{13,14},{10,9},... | collective-permute-start | bytes 98312 | tf_op jit(solution)/shard_map/ppermute | solution.py:277
  186.4 1.2 collective-permute-done.18.refs_5_.lev_a
  187.5 1.8 collective-permute-done.19.refs_6_.lev_b
  189.3 0.0 collective-permute-done.16.refs_3_.lon_a
  189.3 0.3 collective-permute-done.17.refs_4_.lon_b
  189.6 4.4 %rest.7 = (f32[3,16,128,128]{3,2,1,0:T(8,128)S(1)}, f32[2,3,128,128]{3,2,1,0:T(8,128)S(1)}, f32[4,16,128,128]{3,2,1,0:T(8,128)}) custom-call(s32[6]{0:T(128)S(1)} %stack.41.info, f32[16,128,128]{2,1,0:T(8,128)S(1)} %row.6.refs_0_.centre, f32[3,16,128,128]{3,2,1,0:T(8,128)S(1)} %rest.6.refs_1_.far, f32[4,16,128,128]{3,2,1,0:T(8,128)S(1)} %copy-done, ...), custom_call_target="tpu_custom_call" | custom-call | flops 15728640 | bytes 12582912 | tf_op jit(solution)/shard_map/rest/pallas_call | solution.py:213
  194.0 0.1 collective-permute-start.22
  194.1 8.1 %collective-permute-done.15.near = f32[16,128,128]{2,1,0:T(8,128)S(1)} collective-permute-done((f32[16,128,128]{2,1,0:T(8,128)S(1)}, f32[16,128,128]{2,1,0:T(8,128)S(1)}, u32[]{:S(2)}, u32[]{:S(2)}) %collective-permute-start.15) | collective-permute-done | bytes 1048608 | tf_op jit(solution)/shard_map/ppermute | solution.py:277
  202.3 2.3 %row.7 = (f32[16,128,128]{2,1,0:T(8,128)S(1)}, f32[2,128,128]{2,1,0:T(8,128)S(1)}, f32[4,16,128,128]{3,2,1,0:T(8,128)}) custom-call(s32[6]{0:T(128)S(1)} %stack.41.info, f32[16,128,128]{2,1,0:T(8,128)S(1)} %row.6.refs_0_.centre, f32[16,128,128]{2,1,0:T(8,128)S(1)} %collective-permute-done.15.near, ...), custom_call_target="tpu_custom_call", output_to_operand_aliasing={{2}: (9, {})} | custom-call | flops 5242880 | bytes 5242880 | tf_op jit(solution)/shard_map/row/pallas_call | solution.py:139
  204.6 0.1 collective-permute-start.20
  204.7 0.0 collective-permute-done.22
  204.7 0.1 add_multiply_fusion
  204.8 0.1 collective-permute-start.23
  204.9 1.1 collective-permute-done.20
  206.0 2.5 %collective-permute-start.21 = (f32[2,1,128,128]{3,2,1,0:T(8,128)S(1)}, f32[2,1,128,128]{3,2,1,0:T(8,128)S(1)}, u32[]{:S(2)}, u32[]{:S(2)}) collective-permute-start(f32[2,1,128,128]{3,2,1,0:T(8,128)S(1)} %pad_maximum_fusion.1.one), channel_id=1, source_target_pairs={{0,16},{8,24},{16,0},{24,8},{1,17},{9,25},{17,1},{25,9},{2,18},{10... | collective-permute-start | bytes 393224 | tf_op jit(solution)/shard_map/ppermute | solution.py:277
  208.5 9.8 %collective-permute-done.23.two = f32[2,3,128,128]{3,2,1,0:T(8,128)S(1)} collective-permute-done((f32[2,3,128,128]{3,2,1,0:T(8,128)S(1)}, f32[2,3,128,128]{3,2,1,0:T(8,128)S(1)}, u32[]{:S(2)}, u32[]{:S(2)}) %collective-permute-start.23) | collective-permute-done | bytes 393248 | tf_op jit(solution)/shard_map/ppermute | solution.py:277
  218.3 2.4 %scale.2.refs_0_ = f32[4,16,128,128]{3,2,1,0:T(8,128)} custom-call(s32[6]{0:T(128)S(1)} %stack.41.info, f32[3,16,128,128]{3,2,1,0:T(8,128)S(1)} %get-tuple-element.43.field, f32[2,3,128,128]{3,2,1,0:T(8,128)S(1)} %pad_maximum_fusion.one, f32[2,3,128,128]{3,2,1,0:T(8,128)S(1)} %collective-permute-done.23.two), custom_call_target="tpu_custom_call" | custom-call | flops 2359296 | bytes 6291456 | tf_op jit(solution)/shard_map/scale/pallas_call | solution.py:260
  220.7 0.0 collective-permute-done.21.two
  220.8 1.7 scale.3
  (12 shorter events, 0.1 us)
Async XLA Ops:
  1.9 51.6 %collective-permute-start = (f32[16,128,128]{2,1,0:T(8,128)S(1)}, f32[16,128,128]{2,1,0:T(8,128)S(1)}, u32[]{:S(2)}, u32[]{:S(2)}) collective-permute-start(f32[16,128,128]{2,1,0:T(8,128)S(1)} %dynamic-slice_bitcast_fusion.centre), channel_id=1, source_target_pairs={{0,32},{32,0},{1,33},{33,1},{2,34},{34,2},{3,35},{35,3},{4,36},{36... | collective-permute-start | bytes 3145736 | tf_op jit(solution)/shard_map/ppermute | solution.py:277
  7.5 2.2 copy-start.1
  9.7 43.9 %copy-start = (f32[4,16,128,128]{3,2,1,0:T(8,128)S(1)}, f32[4,16,128,128]{3,2,1,0:T(8,128)}, u32[]{:S(2)}) copy-start(f32[4,16,128,128]{3,2,1,0:T(8,128)} %crowding.7) | copy-start | bytes 12582916
  10.3 11.5 %collective-permute-start.1 = (f32[4,128,128]{2,1,0:T(8,128)S(1)}, f32[4,128,128]{2,1,0:T(8,128)S(1)}, u32[]{:S(2)}, u32[]{:S(2)}) collective-permute-start(f32[4,128,128]{2,1,0:T(8,128)S(1)} %get-tuple-element.24), channel_id=1, source_target_pairs={{0,8},{16,24},{8,0},{24,16},{1,9},{17,25},{9,1},{25,17},{2,10},{18... | collective-permute-start | bytes 786440 | tf_op jit(solution)/shard_map/ppermute | solution.py:277
  10.4 11.4 %collective-permute-start.2 = (f32[4,128,128]{2,1,0:T(8,128)S(1)}, f32[4,128,128]{2,1,0:T(8,128)S(1)}, u32[]{:S(2)}, u32[]{:S(2)}) collective-permute-start(f32[4,128,128]{2,1,0:T(8,128)S(1)} %get-tuple-element.25), channel_id=1, source_target_pairs={{8,16},{16,8},{9,17},{17,9},{10,18},{18,10},{11,19},{19,11},{12,20... | collective-permute-start | bytes 786440 | tf_op jit(solution)/shard_map/ppermute | solution.py:277
  13.0 6.8 %collective-permute-start.3 = (f32[4,16,128]{2,1,0:T(8,128)S(1)}, f32[4,16,128]{2,1,0:T(8,128)S(1)}, u32[]{:S(2)}, u32[]{:S(2)}) collective-permute-start(f32[4,16,128]{2,1,0:T(8,128)S(1)} %get-tuple-element.26), channel_id=1, source_target_pairs={{0,1},{2,3},{4,5},{6,7},{1,0},{3,2},{5,4},{7,6},{8,9},{10,11},{12,... | collective-permute-start | bytes 98312 | tf_op jit(solution)/shard_map/ppermute | solution.py:277
  15.1 6.7 %collective-permute-start.4 = (f32[4,16,128]{2,1,0:T(8,128)S(1)}, f32[4,16,128]{2,1,0:T(8,128)S(1)}, u32[]{:S(2)}, u32[]{:S(2)}) collective-permute-start(f32[4,16,128]{2,1,0:T(8,128)S(1)} %get-tuple-element.27), channel_id=1, source_target_pairs={{1,2},{3,4},{5,6},{2,1},{4,3},{6,5},{9,10},{11,12},{13,14},{10,9},... | collective-permute-start | bytes 98312 | tf_op jit(solution)/shard_map/ppermute | solution.py:277
  53.6 2.2 copy-start.2
  55.7 6.4 %copy-start.3 = (f32[4,16,128,128]{3,2,1,0:T(8,128)S(1)}, f32[4,16,128,128]{3,2,1,0:T(8,128)}, u32[]{:S(2)}) copy-start(f32[4,16,128,128]{3,2,1,0:T(8,128)} %refs_0_.3) | copy-start | bytes 12582916
  57.0 63.6 %collective-permute-start.5 = (f32[16,128,128]{2,1,0:T(8,128)S(1)}, f32[16,128,128]{2,1,0:T(8,128)S(1)}, u32[]{:S(2)}, u32[]{:S(2)}) collective-permute-start(f32[16,128,128]{2,1,0:T(8,128)S(1)} %row.4.refs_0_.centre), channel_id=1, source_target_pairs={{0,32},{32,0},{1,33},{33,1},{2,34},{34,2},{3,35},{35,3},{4,36},{36... | collective-permute-start | bytes 3145736 | tf_op jit(solution)/shard_map/ppermute | solution.py:277
  65.5 11.5 %collective-permute-start.6 = (f32[4,128,128]{2,1,0:T(8,128)S(1)}, f32[4,128,128]{2,1,0:T(8,128)S(1)}, u32[]{:S(2)}, u32[]{:S(2)}) collective-permute-start(f32[4,128,128]{2,1,0:T(8,128)S(1)} %get-tuple-element.28), channel_id=1, source_target_pairs={{0,8},{16,24},{8,0},{24,16},{1,9},{17,25},{9,1},{25,17},{2,10},{18... | collective-permute-start | bytes 786440 | tf_op jit(solution)/shard_map/ppermute | solution.py:277
  65.6 11.4 %collective-permute-start.7 = (f32[4,128,128]{2,1,0:T(8,128)S(1)}, f32[4,128,128]{2,1,0:T(8,128)S(1)}, u32[]{:S(2)}, u32[]{:S(2)}) collective-permute-start(f32[4,128,128]{2,1,0:T(8,128)S(1)} %get-tuple-element.29), channel_id=1, source_target_pairs={{8,16},{16,8},{9,17},{17,9},{10,18},{18,10},{11,19},{19,11},{12,20... | collective-permute-start | bytes 786440 | tf_op jit(solution)/shard_map/ppermute | solution.py:277
  68.2 6.8 %collective-permute-start.8 = (f32[4,16,128]{2,1,0:T(8,128)S(1)}, f32[4,16,128]{2,1,0:T(8,128)S(1)}, u32[]{:S(2)}, u32[]{:S(2)}) collective-permute-start(f32[4,16,128]{2,1,0:T(8,128)S(1)} %get-tuple-element.30), channel_id=1, source_target_pairs={{0,1},{2,3},{4,5},{6,7},{1,0},{3,2},{5,4},{7,6},{8,9},{10,11},{12,... | collective-permute-start | bytes 98312 | tf_op jit(solution)/shard_map/ppermute | solution.py:277
  70.3 6.7 %collective-permute-start.9 = (f32[4,16,128]{2,1,0:T(8,128)S(1)}, f32[4,16,128]{2,1,0:T(8,128)S(1)}, u32[]{:S(2)}, u32[]{:S(2)}) collective-permute-start(f32[4,16,128]{2,1,0:T(8,128)S(1)} %get-tuple-element.31), channel_id=1, source_target_pairs={{1,2},{3,4},{5,6},{2,1},{4,3},{6,5},{9,10},{11,12},{13,14},{10,9},... | collective-permute-start | bytes 98312 | tf_op jit(solution)/shard_map/ppermute | solution.py:277
  122.0 51.1 %collective-permute-start.10 = (f32[16,128,128]{2,1,0:T(8,128)S(1)}, f32[16,128,128]{2,1,0:T(8,128)S(1)}, u32[]{:S(2)}, u32[]{:S(2)}) collective-permute-start(f32[16,128,128]{2,1,0:T(8,128)S(1)} %row.5.refs_0_.centre), channel_id=1, source_target_pairs={{0,32},{32,0},{1,33},{33,1},{2,34},{34,2},{3,35},{35,3},{4,36},{36... | collective-permute-start | bytes 3145736 | tf_op jit(solution)/shard_map/ppermute | solution.py:277
  129.0 30.2 %collective-permute-start.11 = (f32[4,128,128]{2,1,0:T(8,128)S(1)}, f32[4,128,128]{2,1,0:T(8,128)S(1)}, u32[]{:S(2)}, u32[]{:S(2)}) collective-permute-start(f32[4,128,128]{2,1,0:T(8,128)S(1)} %get-tuple-element.32), channel_id=1, source_target_pairs={{0,8},{16,24},{8,0},{24,16},{1,9},{17,25},{9,1},{25,17},{2,10},{18... | collective-permute-start | bytes 786440 | tf_op jit(solution)/shard_map/ppermute | solution.py:277
  129.1 30.1 %collective-permute-start.12 = (f32[4,128,128]{2,1,0:T(8,128)S(1)}, f32[4,128,128]{2,1,0:T(8,128)S(1)}, u32[]{:S(2)}, u32[]{:S(2)}) collective-permute-start(f32[4,128,128]{2,1,0:T(8,128)S(1)} %get-tuple-element.33), channel_id=1, source_target_pairs={{8,16},{16,8},{9,17},{17,9},{10,18},{18,10},{11,19},{19,11},{12,20... | collective-permute-start | bytes 786440 | tf_op jit(solution)/shard_map/ppermute | solution.py:277
  131.0 26.0 %collective-permute-start.13 = (f32[4,16,128]{2,1,0:T(8,128)S(1)}, f32[4,16,128]{2,1,0:T(8,128)S(1)}, u32[]{:S(2)}, u32[]{:S(2)}) collective-permute-start(f32[4,16,128]{2,1,0:T(8,128)S(1)} %get-tuple-element.34), channel_id=1, source_target_pairs={{0,1},{2,3},{4,5},{6,7},{1,0},{3,2},{5,4},{7,6},{8,9},{10,11},{12,... | collective-permute-start | bytes 98312 | tf_op jit(solution)/shard_map/ppermute | solution.py:277
  152.5 6.7 %collective-permute-start.14 = (f32[4,16,128]{2,1,0:T(8,128)S(1)}, f32[4,16,128]{2,1,0:T(8,128)S(1)}, u32[]{:S(2)}, u32[]{:S(2)}) collective-permute-start(f32[4,16,128]{2,1,0:T(8,128)S(1)} %get-tuple-element.35), channel_id=1, source_target_pairs={{1,2},{3,4},{5,6},{2,1},{4,3},{6,5},{9,10},{11,12},{13,14},{10,9},... | collective-permute-start | bytes 98312 | tf_op jit(solution)/shard_map/ppermute | solution.py:277
  174.3 27.9 %collective-permute-start.15 = (f32[16,128,128]{2,1,0:T(8,128)S(1)}, f32[16,128,128]{2,1,0:T(8,128)S(1)}, u32[]{:S(2)}, u32[]{:S(2)}) collective-permute-start(f32[16,128,128]{2,1,0:T(8,128)S(1)} %row.6.refs_0_.centre), channel_id=1, source_target_pairs={{0,32},{32,0},{1,33},{33,1},{2,34},{34,2},{3,35},{35,3},{4,36},{36... | collective-permute-start | bytes 3145736 | tf_op jit(solution)/shard_map/ppermute | solution.py:277
  180.3 9.0 %collective-permute-start.16 = (f32[4,128,128]{2,1,0:T(8,128)S(1)}, f32[4,128,128]{2,1,0:T(8,128)S(1)}, u32[]{:S(2)}, u32[]{:S(2)}) collective-permute-start(f32[4,128,128]{2,1,0:T(8,128)S(1)} %get-tuple-element.36), channel_id=1, source_target_pairs={{0,8},{16,24},{8,0},{24,16},{1,9},{17,25},{9,1},{25,17},{2,10},{18... | collective-permute-start | bytes 786440 | tf_op jit(solution)/shard_map/ppermute | solution.py:277
  180.4 9.2 %collective-permute-start.17 = (f32[4,128,128]{2,1,0:T(8,128)S(1)}, f32[4,128,128]{2,1,0:T(8,128)S(1)}, u32[]{:S(2)}, u32[]{:S(2)}) collective-permute-start(f32[4,128,128]{2,1,0:T(8,128)S(1)} %get-tuple-element.37), channel_id=1, source_target_pairs={{8,16},{16,8},{9,17},{17,9},{10,18},{18,10},{11,19},{19,11},{12,20... | collective-permute-start | bytes 786440 | tf_op jit(solution)/shard_map/ppermute | solution.py:277
  182.3 5.2 %collective-permute-start.18 = (f32[4,16,128]{2,1,0:T(8,128)S(1)}, f32[4,16,128]{2,1,0:T(8,128)S(1)}, u32[]{:S(2)}, u32[]{:S(2)}) collective-permute-start(f32[4,16,128]{2,1,0:T(8,128)S(1)} %get-tuple-element.38), channel_id=1, source_target_pairs={{0,1},{2,3},{4,5},{6,7},{1,0},{3,2},{5,4},{7,6},{8,9},{10,11},{12,... | collective-permute-start | bytes 98312 | tf_op jit(solution)/shard_map/ppermute | solution.py:277
  182.6 6.7 %collective-permute-start.19 = (f32[4,16,128]{2,1,0:T(8,128)S(1)}, f32[4,16,128]{2,1,0:T(8,128)S(1)}, u32[]{:S(2)}, u32[]{:S(2)}) collective-permute-start(f32[4,16,128]{2,1,0:T(8,128)S(1)} %get-tuple-element.39), channel_id=1, source_target_pairs={{1,2},{3,4},{5,6},{2,1},{4,3},{6,5},{9,10},{11,12},{13,14},{10,9},... | collective-permute-start | bytes 98312 | tf_op jit(solution)/shard_map/ppermute | solution.py:277
  194.0 10.6 %collective-permute-start.22 = (f32[2,3,128,128]{3,2,1,0:T(8,128)S(1)}, f32[2,3,128,128]{3,2,1,0:T(8,128)S(1)}, u32[]{:S(2)}, u32[]{:S(2)}) collective-permute-start(f32[2,3,128,128]{3,2,1,0:T(8,128)S(1)} %get-tuple-element.44), channel_id=1, source_target_pairs={{0,8},{16,24},{8,0},{24,16},{1,9},{17,25},{9,1},{25,17},{2,10},{18... | collective-permute-start | bytes 1179656 | tf_op jit(solution)/shard_map/ppermute | solution.py:277
  204.6 1.4 collective-permute-start.20
  204.8 13.6 %collective-permute-start.23 = (f32[2,3,128,128]{3,2,1,0:T(8,128)S(1)}, f32[2,3,128,128]{3,2,1,0:T(8,128)S(1)}, u32[]{:S(2)}, u32[]{:S(2)}) collective-permute-start(f32[2,3,128,128]{3,2,1,0:T(8,128)S(1)} %pad_maximum_fusion.one), channel_id=1, source_target_pairs={{0,16},{8,24},{16,0},{24,8},{1,17},{9,25},{17,1},{25,9},{2,18},{10... | collective-permute-start | bytes 1179656 | tf_op jit(solution)/shard_map/ppermute | solution.py:277
  206.0 14.7 %collective-permute-start.21 = (f32[2,1,128,128]{3,2,1,0:T(8,128)S(1)}, f32[2,1,128,128]{3,2,1,0:T(8,128)S(1)}, u32[]{:S(2)}, u32[]{:S(2)}) collective-permute-start(f32[2,1,128,128]{3,2,1,0:T(8,128)S(1)} %pad_maximum_fusion.1.one), channel_id=1, source_target_pairs={{0,16},{8,24},{16,0},{24,8},{1,17},{9,25},{17,1},{25,9},{2,18},{10... | collective-permute-start | bytes 393224 | tf_op jit(solution)/shard_map/ppermute | solution.py:277

commit v3 on v2

v3 whole, which is shorter than its diff:
```python
import functools

import jax
import jax.numpy as jnp
from jax import lax
from jax.experimental import pallas as pl
from jax.experimental.pallas import tpu as pltpu
from jax.sharding import PartitionSpec as P


STEPS = 4
CUTS = ((0, 64, 128),) * 4
MIB = 1 << 20
EVEN_X, EVEN_Z = 4, 5
VMEM = pl.BlockSpec(memory_space=pltpu.VMEM)
SMEM = pl.BlockSpec(memory_space=pltpu.SMEM)
ANY = pl.BlockSpec(memory_space=pl.ANY)


def cost(size, flops, reads):
    return pl.CostEstimate(flops=flops * size, bytes_accessed=4 * reads * size, transcendentals=0)


def cells(a, low_x, high_x, near, far, low_z, high_z, crowding):
    length = a.shape[0]
    z = lax.broadcasted_iota(jnp.int32, a.shape, 0)
    down = jnp.where(z == 0, low_z, pltpu.roll(a, 1, 0))
    up = jnp.where(z == length - 1, high_z, pltpu.roll(a, length - 1, 0))
    spread = low_x + high_x + near + far + down + up - 6.0 * a
    return a + 0.1 * spread + 0.2 * a * (1.0 - a * crowding)


def over_x(n, visit, carry=0):
    carry = visit(0, None, 1, carry)
    carry = lax.fori_loop(1, n - 1, lambda x, c: visit(x, x - 1, x + 1, c), carry)
    return visit(n - 1, n - 2, None, carry)


def line_sums(column, n):
    mean = lax.fori_loop(1, n, lambda x, s: s + column(x), column(0)) / n

    def add(x, s):
        d = column(x) - mean
        return s + d * d

    return mean, lax.fori_loop(0, n, add, jnp.zeros_like(mean))


def sides(info, row, ghosts):
    lon_a, lon_b, lev_a, lev_b = ghosts
    even_x, even_z = info[EVEN_X] == 1, info[EVEN_Z] == 1
    low_x = lambda: jnp.where(even_x, lon_b[row], lon_a[row])
    high_x = lambda: jnp.where(even_x, lon_a[row], lon_b[row])

    def ends_z(x):
        a, b = lev_a[row, pl.ds(x, 1), :], lev_b[row, pl.ds(x, 1), :]
        return jnp.where(even_z, b, a), jnp.where(even_z, a, b)

    return low_x, high_x, ends_z


def edge_kernel(count, mapped, info, *refs):
    first, field, sent = refs[:count], refs[count:-4], refs[-4:]
    lon_a, lon_b, lev_a, lev_b = sent
    rows = [None] * (count > 0)
    if field:
        rows += [info[row] if mapped else row for row in range(4 if mapped else 3)]
    n, length = lev_a.shape[1], lon_a.shape[1]
    at_x, at_z = info[EVEN_X] * (n - 1), info[EVEN_Z] * (length - 1)
    for k, row in enumerate(rows):
        for lon, lev, x_at, z_at in (
            (lon_a, lev_a, at_x, at_z),
            (lon_b, lev_b, n - 1 - at_x, length - 1 - at_z),
        ):
            if row is None:
                begin = 0
                for part in first:
                    depth = part.shape[1]
                    lon[k, begin : begin + depth] = part[x_at]
                    begin += depth
                for x in range(n):
                    low, high = first[0][x, 0:1, :], first[-1][x, depth - 1 : depth, :]
                    lev[k, x : x + 1, :] = jnp.where(z_at == 0, low, high)
            else:
                values = field[0].at[row]
                lon[k] = values[x_at]
                for x in range(n):
                    lev[k, x : x + 1, :] = values[x, pl.ds(z_at, 1), :]


def edges(info, first, field, mapped=False):
    args = [*first, *([] if field is None else [field])]
    n, species = args[0].shape[-3], args[0].shape[-1]
    length = sum(part.shape[1] for part in first) if first else field.shape[2]
    rows = (4 if mapped else 3) * (field is not None) + (len(first) > 0)
    lon = jax.ShapeDtypeStruct((rows, length, species), jnp.float32)
    lev = jax.ShapeDtypeStruct((rows, n, species), jnp.float32)
    return pl.pallas_call(
        functools.partial(edge_kernel, len(first), mapped),
        out_shape=[lon, lon, lev, lev],
        in_specs=[SMEM] + [VMEM] * len(args),
        out_specs=[VMEM] * 4,
        compiler_params=pltpu.CompilerParams(vmem_limit_bytes=16 * MIB),
        cost_estimate=cost(2 * rows * (length + n) * species, 1, 2),
        name="edges",
    )(info, *args)


def row_kernel(spans, mapped, low_open, high_open, final, info, *refs):
    centre, received, field, crowding, lon_a, lon_b, lev_a, lev_b = refs[:8]
    refs = refs[8:]
    below, refs = (None, refs) if low_open else (refs[0], refs[1:])
    above, refs = (None, refs) if high_open else (refs[0], refs[1:])
    n = centre.shape[0]
    begin, end = spans[0][0], spans[-1][1]
    even_x, even_z = info[EVEN_X] == 1, info[EVEN_Z] == 1
    second = info[1] if mapped else 0
    here = info[0]

    def visit(x, before, after, carry):
        a, b = lon_a[0, begin:end], lon_b[0, begin:end]
        low_x = jnp.where(even_x, b, a) if before is None else centre[before]
        high_x = jnp.where(even_x, a, b) if after is None else centre[after]
        a, b = lev_a[0, pl.ds(x, 1), :], lev_b[0, pl.ds(x, 1), :]
        low_z = jnp.where(even_z, b, a) if low_open else below[x, below.shape[1] - 1 :, :]
        high_z = jnp.where(even_z, a, b) if high_open else above[x, 0:1, :]
        near, far = received[x], field[second, x, begin:end]
        value = cells(
            centre[x], low_x, high_x, near, far, low_z, high_z, crowding[here, x, begin:end]
        )
        for (a, b), out in zip(spans, outs):
            out[x] = value[a - begin : b - begin]
        return carry

    outs = refs[: len(spans)]
    over_x(n, visit)
    if final:
        refs[-1][0], refs[-1][1] = line_sums(lambda x: outs[0][x], n)


def row_step(info, p, parts, received, cuts, next_cuts, field, crowding, ghosts, mapped, final):
    n, depth, species = parts[p].shape
    begin, end = cuts[p], cuts[p + 1]
    spans = [(a, b) for a, b in zip(next_cuts[:-1], next_cuts[1:]) if begin <= a and b <= end]
    low_open, high_open = p == 0, p == len(parts) - 1
    out_shape = [jax.ShapeDtypeStruct((n, b - a, species), jnp.float32) for a, b in spans]
    if final:
        out_shape.append(jax.ShapeDtypeStruct((2, depth, species), jnp.float32))
    args = [parts[p], received, field, crowding, *ghosts]
    args += [] if low_open else [parts[p - 1]]
    args += [] if high_open else [parts[p + 1]]
    return pl.pallas_call(
        functools.partial(row_kernel, spans, mapped, low_open, high_open, final),
        in_specs=[SMEM] + [VMEM] * len(args),
        out_specs=[VMEM] * len(out_shape),
        out_shape=out_shape,
        compiler_params=pltpu.CompilerParams(vmem_limit_bytes=20 * MIB),
        cost_estimate=cost(parts[p].size, 20, 5),
    )(info, *args)


def rest_kernel(count, mapped, rows, ghost_from, final, info, *refs):
    first, refs = refs[:count], refs[count:]
    field, crowding, lon_a, lon_b, lev_a, lev_b = refs[:6]
    refs = refs[6:]
    if final:
        out, sums, ended, sem = refs[-4:]
    else:
        out = refs[-1]
    n, length = field.shape[1], field.shape[2]
    copies = []
    for k, row in enumerate(rows):
        at = info[row + 1] if mapped else row
        beyond = info[row + 2] if mapped and row < 2 else row + 1
        crowd_at = info[row + 1]
        low, high, ends_z = sides(info, row - ghost_from, (lon_a, lon_b, lev_a, lev_b))

        def visit(x, before, after, carry):
            low_x = low() if before is None else field[at, before]
            high_x = high() if after is None else field[at, after]
            if mapped:
                near = field[info[row], x]
            elif row:
                near = field[row - 1, x]
            else:
                near = jnp.concatenate([part[x] for part in first], axis=0)
            far = 0.0 if row == 2 else field[beyond, x]
            low_z, high_z = ends_z(x)
            out[k, x] = cells(
                field[at, x], low_x, high_x, near, far, low_z, high_z, crowding[crowd_at, x]
            )
            return carry

        over_x(n, visit)
        if final:
            copies.append(pltpu.make_async_copy(out.at[k], ended.at[info[row + 1]], sem.at[k]))
            copies[-1].start()
            there = slice(k * length, (k + 1) * length)
            sums[0, there], sums[1, there] = line_sums(lambda x: out[k, x], n)
    for copy in copies:
        copy.wait()


def rest_step(info, first, field, crowding, ghosts, mapped, rows=(0, 1, 2), ghost_from=-1, final=False, ended=None):
    _, n, length, species = field.shape
    count = len(rows)
    out_shape = [jax.ShapeDtypeStruct((count, n, length, species), jnp.float32)]
    out_specs, scratch, more = [VMEM], [], {}
    args = [*first, field, crowding, *ghosts]
    in_specs = [SMEM] + [VMEM] * len(args)
    if final:
        out_shape += [
            jax.ShapeDtypeStruct((2, count * length, species), jnp.float32),
            jax.ShapeDtypeStruct((4, n, length, species), jnp.float32),
        ]
        out_specs += [VMEM, ANY]
        scratch = [pltpu.SemaphoreType.DMA((count,))]
        if ended is not None:
            args.append(ended)
            in_specs.append(ANY)
            more = {"input_output_aliases": {len(args): 2}}
    return pl.pallas_call(
        functools.partial(rest_kernel, len(first), mapped, rows, ghost_from, final),
        out_shape=out_shape,
        in_specs=in_specs,
        out_specs=out_specs,
        scratch_shapes=scratch,
        compiler_params=pltpu.CompilerParams(vmem_limit_bytes=24 * MIB),
        cost_estimate=cost(count * n * length * species, 20, 4),
        name="rest",
        **more,
    )(info, *args)


def merged(a, b, n):
    d = a[0] - b[0]
    return jnp.stack([0.5 * (a[0] + b[0]), a[1] + b[1] + (0.5 * n) * d * d])


def line_factors(a, b, n):
    d = a[0] - b[0]
    variance = (a[1] + b[1] + (0.5 * n) * d * d) / (2 * n)
    return 0.5 * (a[0] + b[0]), lax.rsqrt(variance + 0.0001)


def scale_kernel(rows, begins, info, *refs):
    count = len(begins)
    fields, (one, two) = refs[:count], refs[count : count + 2]
    scaled, ended, buffers, sem = refs[-3 - count], refs[-2 - count], refs[-1 - count : -1], refs[-1]
    n = buffers[0].shape[-3]
    jobs = []
    for field, buffer, begin in zip(fields, buffers, begins):
        if begin is None:
            jobs += [(field.at[k], buffer.at[k], info[row], 0, False) for k, row in enumerate(rows)]
        else:
            jobs.append((field, buffer, info[0], begin, True))
    copies, line = [], 0

    def copy(source, target, row, begin):
        there = target.at[row, :, begin : begin + source.shape[1]]
        copies.append(pltpu.make_async_copy(source, there, sem.at[len(copies)]))
        copies[-1].start()

    for field, _, row, begin, place in jobs:
        if place:
            copy(field, ended, row, begin)
    for field, buffer, row, begin, _ in jobs:
        lines = slice(line, line + field.shape[1])
        line += field.shape[1]
        mean, factor = line_factors(*([s[0, lines], s[1, lines]] for s in (one, two)), 2 * n)

        def visit(x, carry):
            buffer[x] = (field[x] - mean) * factor
            return carry

        lax.fori_loop(0, n, visit, 0)
        copy(buffer, scaled, row, begin)
    for c in copies:
        c.wait()


def scale(info, fields, rows, begins, one, two, ended, scaled=None):
    extra = [ended] if scaled is None else [ended, scaled]
    at = 3 + len(fields)
    size = sum(field.size for field in fields)
    return pl.pallas_call(
        functools.partial(scale_kernel, rows, begins),
        out_shape=[jax.ShapeDtypeStruct(ended.shape, jnp.float32)] * 2,
        in_specs=[SMEM] + [VMEM] * (len(fields) + 2) + [ANY] * len(extra),
        out_specs=[ANY, ANY],
        scratch_shapes=[
            *(pltpu.VMEM(field.shape, jnp.float32) for field in fields),
            pltpu.SemaphoreType.DMA((8,)),
        ],
        input_output_aliases={at: 1} if scaled is None else {at: 1, at + 1: 0},
        compiler_params=pltpu.CompilerParams(vmem_limit_bytes=16 * MIB),
        cost_estimate=cost(size, 3, 2),
        name="scale",
    )(info, *fields, one, two, *extra)


def paired(array, axis, pairs):
    return lax.ppermute(array, axis, [*pairs, *((b, a) for a, b in pairs)])


def exchanged(sent):
    lon_a, lon_b, lev_a, lev_b = sent
    return (
        paired(lon_a, "lon", [(0, 1), (2, 3)]),
        paired(lon_b, "lon", [(1, 2)]),
        paired(lev_a, "lev", [(0, 1), (2, 3), (4, 5), (6, 7)]),
        paired(lev_b, "lev", [(1, 2), (3, 4), (5, 6)]),
    )


def halves_of_lines(sums, n):
    half = merged(sums, paired(sums, "lon", [(0, 1), (2, 3)]), n)
    return half, paired(half, "lon", [(0, 2), (1, 3)])


def steps(density, crowding):
    rows, n, _, species = density.shape
    flipped = lax.axis_index("lat") == 0
    order = [jnp.where(flipped, rows - 1 - row, row) for row in range(rows)]

    def swapped(parts):
        return [paired(part, "lat", [(0, 1)]) for part in parts]

    parts = [
        lax.dynamic_slice(density, (order[0], 0, a, 0), (1, n, b - a, species))[0]
        for a, b in zip(CUTS[0][:-1], CUTS[0][1:])
    ]
    arriving = swapped(parts)
    even = [1 - lax.axis_index(axis) % 2 for axis in ("lon", "lev")]
    info = jnp.stack([*order, *even]).astype(jnp.int32)
    rest = None
    for step in range(STEPS):
        start, final = step == 0, step == STEPS - 1
        cuts = CUTS[step]
        next_cuts = cuts if final else CUTS[step + 1]
        field = density if start else rest
        first = [] if start else parts
        sent = edges(info, first, None if final else field, start)
        ghosts = exchanged(sent)
        if final:
            sent = edges(info, [], rest)
            ghosts_rest = exchanged(sent)
            deep, deep_sums, ended = rest_step(
                info, [], rest, crowding, ghosts_rest, False, (1, 2), 0, True
            )
            beside, beside_sums, ended = rest_step(
                info, first, rest, crowding, ghosts_rest, False, (0,), 0, True, ended
            )
        else:
            (rest,) = rest_step(info, first, field, crowding, ghosts, start)
        new = []
        for p in range(len(parts)):
            new += row_step(
                info, p, parts, arriving[p], cuts, next_cuts, field, crowding, ghosts, start, final
            )
        if not final:
            parts = new
            arriving = swapped(parts)
    first, first_sums, last, last_sums = new
    lines = halves_of_lines(deep_sums, n)
    scaled, ended = scale(info, [deep], (2, 3), [None], *lines, ended)
    lines = halves_of_lines(jnp.concatenate([beside_sums, first_sums], axis=1), n)
    scaled, ended = scale(info, [beside, first], (1,), [None, 0], *lines, ended, scaled)
    lines = halves_of_lines(last_sums, n)
    scaled, ended = scale(info, [last], (), [cuts[1]], *lines, ended, scaled)
    return scaled, ended


def solution(mesh):
    placed = P(("trial", "lat"), "lon", "lev", None)
    return jax.shard_map(
        steps,
        mesh=mesh,
        in_specs=(placed, placed),
        out_specs=(placed, placed),
        check_vma=False,
    )
```

time: 223 us -> 218 us (0.978)
  the two profiles are of different devices: /device:TPU:92 before, /device:TPU:66 now
where the time goes in v3:
time: 218 us; the launch traced here: 217 us
  waiting for transfers between devices  110 us (50%)
  starting transfers between devices  69.4 us (32%)
  Pallas kernels  30.7 us (14%)
  local copies, waits for them, and re-layouts  6.05 us (3%)
    ppermute x34, waiting for transfers between devices, paired(): return lax.ppermute(array, axis, [*pairs, *((b, a) for a, b in pairs)])  110 us
    ppermute x34, starting transfers between devices, paired(): return lax.ppermute(array, axis, [*pairs, *((b, a) for a, b in pairs)])  69.4 us
    pallas_call x5, Pallas kernels, rest_step(): pl.pallas_call(functools.partial(rest_kernel, len(first), mapped, rows, g...  13.8 us
    pallas_call x8, Pallas kernels, row_step(): pl.pallas_call(functools.partial(row_kernel, spans, mapped, low_open, hig...  8.21 us
    pallas_call x3, Pallas kernels, scale(): pl.pallas_call(functools.partial(scale_kernel, rows, begins), out_shape=[...  5.62 us
    unnamed x9, local copies, waits for them, and re-layouts  4.68 us
  transfers between devices with their start and end apart: 34, of which 17 were waited for; matrix products, arithmetic and copies ran while one was open for 0% of the time, Pallas kernels for 13%

profile of v3, /device:TPU:66, one launch (start us, length us, event | category | flops | bytes accessed | tf_op | source)
XLA Modules:
  0.0 217.1 jit_solution(1290652647481994147)
XLA Ops:
  0.6 1.3 dynamic-slice_bitcast_fusion
  1.9 5.5 %collective-permute-start.6 = (f32[16,64,128]{2,1,0:T(8,128)S(1)}, f32[16,64,128]{2,1,0:T(8,128)S(1)}, u32[]{:S(2)}, u32[]{:S(2)}) collective-permute-start(f32[16,64,128]{2,1,0:T(8,128)S(1)} %get-tuple-element.70.refs_8_.refs_0_), channel_id=1, source_target_pairs={{0,32},{32,0},{1,33},{33,1},{2,34},{34,2},{3,35},{35,3},{4,36},{36... | collective-permute-start | bytes 1572872 | tf_op jit(solution)/shard_map/ppermute | solution.py:303
  8.1 2.5 %copy-done.1 = f32[4,16,128,128]{3,2,1,0:T(8,128)S(1)} copy-done((f32[4,16,128,128]{3,2,1,0:T(8,128)S(1)}, f32[4,16,128,128]{3,2,1,0:T(8,128)}, u32[]{:S(2)}) %copy-start.1) | copy-done | bytes 4194328
  10.5 0.6 edges.5
  11.3 0.7 collective-permute-start.2
  12.0 0.6 collective-permute-start.3
  12.6 3.4 %collective-permute-done.3.refs_6_.refs_4_ = f32[4,16,128]{2,1,0:T(8,128)S(1)} collective-permute-done((f32[4,16,128]{2,1,0:T(8,128)S(1)}, f32[4,16,128]{2,1,0:T(8,128)S(1)}, u32[]{:S(2)}, u32[]{:S(2)}) %collective-permute-start.3) | collective-permute-done | bytes 32800 | tf_op jit(solution)/shard_map/ppermute | solution.py:303
  16.0 3.4 %collective-permute-start.4 = (f32[4,16,128]{2,1,0:T(8,128)S(1)}, f32[4,16,128]{2,1,0:T(8,128)S(1)}, u32[]{:S(2)}, u32[]{:S(2)}) collective-permute-start(f32[4,16,128]{2,1,0:T(8,128)S(1)} %get-tuple-element.39), channel_id=1, source_target_pairs={{1,2},{3,4},{5,6},{2,1},{4,3},{6,5},{9,10},{11,12},{13,14},{10,9},... | collective-permute-start | bytes 98312 | tf_op jit(solution)/shard_map/ppermute | solution.py:303
  19.4 3.2 %collective-permute-done.4.refs_7_.refs_5_ = f32[4,16,128]{2,1,0:T(8,128)S(1)} collective-permute-done((f32[4,16,128]{2,1,0:T(8,128)S(1)}, f32[4,16,128]{2,1,0:T(8,128)S(1)}, u32[]{:S(2)}, u32[]{:S(2)}) %collective-permute-start.4) | collective-permute-done | bytes 32800 | tf_op jit(solution)/shard_map/ppermute | solution.py:303
  22.7 33.3 %collective-permute-done.6.refs_1_ = f32[16,64,128]{2,1,0:T(8,128)S(1)} collective-permute-done((f32[16,64,128]{2,1,0:T(8,128)S(1)}, f32[16,64,128]{2,1,0:T(8,128)S(1)}, u32[]{:S(2)}, u32[]{:S(2)}) %collective-permute-start.6) | collective-permute-done | bytes 524320 | tf_op jit(solution)/shard_map/ppermute | solution.py:303
  55.9 2.2 %copy-done.2 = f32[4,16,128,128]{3,2,1,0:T(8,128)S(1)} copy-done((f32[4,16,128,128]{3,2,1,0:T(8,128)S(1)}, f32[4,16,128,128]{3,2,1,0:T(8,128)}, u32[]{:S(2)}) %copy-start.2) | copy-done | bytes 4194328
  58.1 1.0 shard_map.42.refs_0_.refs_8_
  59.1 5.3 %collective-permute-start.12 = (f32[16,64,128]{2,1,0:T(8,128)S(1)}, f32[16,64,128]{2,1,0:T(8,128)S(1)}, u32[]{:S(2)}, u32[]{:S(2)}) collective-permute-start(f32[16,64,128]{2,1,0:T(8,128)S(1)} %shard_map.42.refs_0_.refs_8_), channel_id=1, source_target_pairs={{0,32},{32,0},{1,33},{33,1},{2,34},{34,2},{3,35},{35,3},{4,36},{36... | collective-permute-start | bytes 1572872 | tf_op jit(solution)/shard_map/ppermute | solution.py:303
  64.4 2.8 %rest.5.refs_2_ = f32[3,16,128,128]{3,2,1,0:T(8,128)S(1)} custom-call(s32[6]{0:T(128)S(1)} %stack.42.info, f32[4,16,128,128]{3,2,1,0:T(8,128)S(1)} %copy-done.3, f32[4,16,128,128]{3,2,1,0:T(8,128)S(1)} %copy-done, f32[4,128,128]{2,1,0:T(8,128)S(1)} %collective-permute-done.1.refs_4_.refs_2_, f32[4,128,128]{2,1,0:T(8,128)S(1)} %collective-permute-done.2.refs_5_.refs_3_, ...), custom_call_target="tpu_custom_call" | custom-call | flops 15728640 | bytes 12582912 | tf_op jit(solution)/shard_map/rest/pallas_call | solution.py:222
  67.2 19.6 %collective-permute-done.refs_1_ = f32[16,64,128]{2,1,0:T(8,128)S(1)} collective-permute-done((f32[16,64,128]{2,1,0:T(8,128)S(1)}, f32[16,64,128]{2,1,0:T(8,128)S(1)}, u32[]{:S(2)}, u32[]{:S(2)}) %collective-permute-start) | collective-permute-done | bytes 524320 | tf_op jit(solution)/shard_map/ppermute | solution.py:303
  86.8 1.0 shard_map.41.refs_1_.refs_0_.refs_8_
  87.9 2.0 collective-permute-start.5
  89.9 0.6 edges.6
  90.6 0.7 collective-permute-start.8
  91.3 0.6 collective-permute-start.9
  91.9 3.4 %collective-permute-done.9.refs_6_ = f32[4,16,128]{2,1,0:T(8,128)S(1)} collective-permute-done((f32[4,16,128]{2,1,0:T(8,128)S(1)}, f32[4,16,128]{2,1,0:T(8,128)S(1)}, u32[]{:S(2)}, u32[]{:S(2)}) %collective-permute-start.9) | collective-permute-done | bytes 32800 | tf_op jit(solution)/shard_map/ppermute | solution.py:303
  95.3 3.4 %collective-permute-start.10 = (f32[4,16,128]{2,1,0:T(8,128)S(1)}, f32[4,16,128]{2,1,0:T(8,128)S(1)}, u32[]{:S(2)}, u32[]{:S(2)}) collective-permute-start(f32[4,16,128]{2,1,0:T(8,128)S(1)} %get-tuple-element.43), channel_id=1, source_target_pairs={{1,2},{3,4},{5,6},{2,1},{4,3},{6,5},{9,10},{11,12},{13,14},{10,9},... | collective-permute-start | bytes 98312 | tf_op jit(solution)/shard_map/ppermute | solution.py:303
  98.8 3.2 %collective-permute-done.10.refs_7_ = f32[4,16,128]{2,1,0:T(8,128)S(1)} collective-permute-done((f32[4,16,128]{2,1,0:T(8,128)S(1)}, f32[4,16,128]{2,1,0:T(8,128)S(1)}, u32[]{:S(2)}, u32[]{:S(2)}) %collective-permute-start.10) | collective-permute-done | bytes 32800 | tf_op jit(solution)/shard_map/ppermute | solution.py:303
  102.0 7.8 %collective-permute-done.12.refs_1_ = f32[16,64,128]{2,1,0:T(8,128)S(1)} collective-permute-done((f32[16,64,128]{2,1,0:T(8,128)S(1)}, f32[16,64,128]{2,1,0:T(8,128)S(1)}, u32[]{:S(2)}, u32[]{:S(2)}) %collective-permute-start.12) | collective-permute-done | bytes 524320 | tf_op jit(solution)/shard_map/ppermute | solution.py:303
  109.8 1.0 shard_map.44.refs_0_.refs_8_
  110.8 4.9 %collective-permute-start.18 = (f32[16,64,128]{2,1,0:T(8,128)S(1)}, f32[16,64,128]{2,1,0:T(8,128)S(1)}, u32[]{:S(2)}, u32[]{:S(2)}) collective-permute-start(f32[16,64,128]{2,1,0:T(8,128)S(1)} %shard_map.44.refs_0_.refs_8_), channel_id=1, source_target_pairs={{0,32},{32,0},{1,33},{33,1},{2,34},{34,2},{3,35},{35,3},{4,36},{36... | collective-permute-start | bytes 1572872 | tf_op jit(solution)/shard_map/ppermute | solution.py:303
  115.7 2.7 %rest.6.refs_2_ = f32[3,16,128,128]{3,2,1,0:T(8,128)S(1)} custom-call(s32[6]{0:T(128)S(1)} %stack.42.info, f32[16,64,128]{2,1,0:T(8,128)S(1)} %shard_map.42.refs_0_.refs_8_, f32[16,64,128]{2,1,0:T(8,128)S(1)} %shard_map.41.refs_1_.refs_0_.refs_8_, f32[3,16,128,128]{3,2,1,0:T(8,128)S(1)} %rest.5.refs_2_, f32[4,16,128,128]{3,2,1,0:T(8,128)S(1)} %copy-done, ...), custom_call_target="tpu_custom_call" | custom-call | flops 15728640 | bytes 12582912 | tf_op jit(solution)/shard_map/rest/pallas_call | solution.py:222
  118.5 13.0 %collective-permute-done.5.refs_1_ = f32[16,64,128]{2,1,0:T(8,128)S(1)} collective-permute-done((f32[16,64,128]{2,1,0:T(8,128)S(1)}, f32[16,64,128]{2,1,0:T(8,128)S(1)}, u32[]{:S(2)}, u32[]{:S(2)}) %collective-permute-start.5) | collective-permute-done | bytes 524320 | tf_op jit(solution)/shard_map/ppermute | solution.py:303
  131.5 1.0 shard_map.43.refs_1_.refs_0_.refs_8_
  132.4 0.6 edges.7
  133.2 0.7 collective-permute-start.14
  133.9 4.8 %collective-permute-start.11 = (f32[16,64,128]{2,1,0:T(8,128)S(1)}, f32[16,64,128]{2,1,0:T(8,128)S(1)}, u32[]{:S(2)}, u32[]{:S(2)}) collective-permute-start(f32[16,64,128]{2,1,0:T(8,128)S(1)} %shard_map.43.refs_1_.refs_0_.refs_8_), channel_id=1, source_target_pairs={{0,32},{32,0},{1,33},{33,1},{2,34},{34,2},{3,35},{35,3},{4,36},{36... | collective-permute-start | bytes 1572872 | tf_op jit(solution)/shard_map/ppermute | solution.py:303
  139.2 3.6 %collective-permute-done.15.refs_6_ = f32[4,16,128]{2,1,0:T(8,128)S(1)} collective-permute-done((f32[4,16,128]{2,1,0:T(8,128)S(1)}, f32[4,16,128]{2,1,0:T(8,128)S(1)}, u32[]{:S(2)}, u32[]{:S(2)}) %collective-permute-start.15) | collective-permute-done | bytes 32800 | tf_op jit(solution)/shard_map/ppermute | solution.py:303
  142.8 3.5 %collective-permute-start.16 = (f32[4,16,128]{2,1,0:T(8,128)S(1)}, f32[4,16,128]{2,1,0:T(8,128)S(1)}, u32[]{:S(2)}, u32[]{:S(2)}) collective-permute-start(f32[4,16,128]{2,1,0:T(8,128)S(1)} %get-tuple-element.47), channel_id=1, source_target_pairs={{1,2},{3,4},{5,6},{2,1},{4,3},{6,5},{9,10},{11,12},{13,14},{10,9},... | collective-permute-start | bytes 98312 | tf_op jit(solution)/shard_map/ppermute | solution.py:303
  146.3 3.2 %collective-permute-done.16.refs_7_ = f32[4,16,128]{2,1,0:T(8,128)S(1)} collective-permute-done((f32[4,16,128]{2,1,0:T(8,128)S(1)}, f32[4,16,128]{2,1,0:T(8,128)S(1)}, u32[]{:S(2)}, u32[]{:S(2)}) %collective-permute-start.16) | collective-permute-done | bytes 32800 | tf_op jit(solution)/shard_map/ppermute | solution.py:303
  149.5 2.3 %collective-permute-done.18.refs_1_ = f32[16,64,128]{2,1,0:T(8,128)S(1)} collective-permute-done((f32[16,64,128]{2,1,0:T(8,128)S(1)}, f32[16,64,128]{2,1,0:T(8,128)S(1)}, u32[]{:S(2)}, u32[]{:S(2)}) %collective-permute-start.18) | collective-permute-done | bytes 524320 | tf_op jit(solution)/shard_map/ppermute | solution.py:303
  151.7 1.0 shard_map.46.refs_0_.refs_8_
  152.7 2.5 %collective-permute-start.29 = (f32[16,64,128]{2,1,0:T(8,128)S(1)}, f32[16,64,128]{2,1,0:T(8,128)S(1)}, u32[]{:S(2)}, u32[]{:S(2)}) collective-permute-start(f32[16,64,128]{2,1,0:T(8,128)S(1)} %shard_map.46.refs_0_.refs_8_), channel_id=1, source_target_pairs={{0,32},{32,0},{1,33},{33,1},{2,34},{34,2},{3,35},{35,3},{4,36},{36... | collective-permute-start | bytes 1572872 | tf_op jit(solution)/shard_map/ppermute | solution.py:303
  155.2 2.7 %rest.7.refs_2_.refs_0_ = f32[3,16,128,128]{3,2,1,0:T(8,128)S(1)} custom-call(s32[6]{0:T(128)S(1)} %stack.42.info, f32[16,64,128]{2,1,0:T(8,128)S(1)} %shard_map.44.refs_0_.refs_8_, f32[16,64,128]{2,1,0:T(8,128)S(1)} %shard_map.43.refs_1_.refs_0_.refs_8_, f32[3,16,128,128]{3,2,1,0:T(8,128)S(1)} %rest.6.refs_2_, f32[4,16,128,128]{3,2,1,0:T(8,128)S(1)} %copy-done, ...), custom_call_target="tpu_custom_call" | custom-call | flops 15728640 | bytes 12582912 | tf_op jit(solution)/shard_map/rest/pallas_call | solution.py:222
  157.9 0.6 edges.9
  158.6 0.7 collective-permute-start.26
  159.3 0.6 collective-permute-start.27
  159.9 3.3 %collective-permute-done.27.refs_4_.refs_6_ = f32[3,16,128]{2,1,0:T(8,128)S(1)} collective-permute-done((f32[3,16,128]{2,1,0:T(8,128)S(1)}, f32[3,16,128]{2,1,0:T(8,128)S(1)}, u32[]{:S(2)}, u32[]{:S(2)}) %collective-permute-start.27) | collective-permute-done | bytes 24608 | tf_op jit(solution)/shard_map/ppermute | solution.py:303
  163.2 3.4 %collective-permute-start.28 = (f32[3,16,128]{2,1,0:T(8,128)S(1)}, f32[3,16,128]{2,1,0:T(8,128)S(1)}, u32[]{:S(2)}, u32[]{:S(2)}) collective-permute-start(f32[3,16,128]{2,1,0:T(8,128)S(1)} %get-tuple-element.57), channel_id=1, source_target_pairs={{1,2},{3,4},{5,6},{2,1},{4,3},{6,5},{9,10},{11,12},{13,14},{10,9},... | collective-permute-start | bytes 73736 | tf_op jit(solution)/shard_map/ppermute | solution.py:303
  166.7 3.2 %collective-permute-done.28.refs_5_.refs_7_ = f32[3,16,128]{2,1,0:T(8,128)S(1)} collective-permute-done((f32[3,16,128]{2,1,0:T(8,128)S(1)}, f32[3,16,128]{2,1,0:T(8,128)S(1)}, u32[]{:S(2)}, u32[]{:S(2)}) %collective-permute-start.28) | collective-permute-done | bytes 24608 | tf_op jit(solution)/shard_map/ppermute | solution.py:303
  169.8 3.3 %rest.8 = (f32[2,16,128,128]{3,2,1,0:T(8,128)S(1)}, f32[2,256,128]{2,1,0:T(8,128)S(1)}, f32[4,16,128,128]{3,2,1,0:T(8,128)}) custom-call(s32[6]{0:T(128)S(1)} %stack.42.info, f32[3,16,128,128]{3,2,1,0:T(8,128)S(1)} %rest.7.refs_2_.refs_0_, f32[4,16,128,128]{3,2,1,0:T(8,128)S(1)} %copy-done, f32[3,128,128]{2,1,0:T(8,128)S(1)} %collective-permute-done.25.refs_2_.refs_4_, ...), custom_call_target="tpu_custom_call" | custom-call | flops 10485760 | bytes 8388608 | tf_op jit(solution)/shard_map/rest/pallas_call | solution.py:222
  173.2 3.7 %collective-permute-start.32 = (f32[2,256,128]{2,1,0:T(8,128)S(1)}, f32[2,256,128]{2,1,0:T(8,128)S(1)}, u32[]{:S(2)}, u32[]{:S(2)}) collective-permute-start(f32[2,256,128]{2,1,0:T(8,128)S(1)} %get-tuple-element.64), channel_id=1, source_target_pairs={{0,8},{16,24},{8,0},{24,16},{1,9},{17,25},{9,1},{25,17},{2,10},{18... | collective-permute-start | bytes 786440 | tf_op jit(solution)/shard_map/ppermute | solution.py:303
  176.9 1.0 shard_map.45.refs_1_.refs_0_.refs_8_
  178.5 4.9 %collective-permute-start.22 = (f32[1,16,128]{2,1,0:T(8,128)S(1)}, f32[1,16,128]{2,1,0:T(8,128)S(1)}, u32[]{:S(2)}, u32[]{:S(2)}) collective-permute-start(f32[1,16,128]{2,1,0:T(8,128)S(1)} %get-tuple-element.51), channel_id=1, source_target_pairs={{1,2},{3,4},{5,6},{2,1},{4,3},{6,5},{9,10},{11,12},{13,14},{10,9},... | collective-permute-start | bytes 24584 | tf_op jit(solution)/shard_map/ppermute | solution.py:303
  183.5 3.6 %collective-permute-start.17 = (f32[16,64,128]{2,1,0:T(8,128)S(1)}, f32[16,64,128]{2,1,0:T(8,128)S(1)}, u32[]{:S(2)}, u32[]{:S(2)}) collective-permute-start(f32[16,64,128]{2,1,0:T(8,128)S(1)} %shard_map.45.refs_1_.refs_0_.refs_8_), channel_id=1, source_target_pairs={{0,32},{32,0},{1,33},{33,1},{2,34},{34,2},{3,35},{35,3},{4,36},{36... | collective-permute-start | bytes 1572872 | tf_op jit(solution)/shard_map/ppermute | solution.py:303
  187.1 2.3 %rest.9 = (f32[1,16,128,128]{3,2,1,0:T(8,128)S(1)}, f32[2,128,128]{2,1,0:T(8,128)S(1)}, f32[4,16,128,128]{3,2,1,0:T(8,128)}) custom-call(s32[6]{0:T(128)S(1)} %stack.42.info, f32[16,64,128]{2,1,0:T(8,128)S(1)} %shard_map.46.refs_0_.refs_8_, f32[16,64,128]{2,1,0:T(8,128)S(1)} %shard_map.45.refs_1_.refs_0_.refs_8_, ...), custom_call_target="tpu_custom_call", output_to_operand_aliasing={{2}: (9, {})} | custom-call | flops 5242880 | bytes 4194304 | tf_op jit(solution)/shard_map/rest/pallas_call | solution.py:222
  189.4 0.7 collective-permute-start.20
  190.7 1.2 shard_map.48
  191.9 6.7 %collective-permute-start.30 = (f32[2,192,128]{2,1,0:T(8,128)S(1)}, f32[2,192,128]{2,1,0:T(8,128)S(1)}, u32[]{:S(2)}, u32[]{:S(2)}) collective-permute-start(f32[2,192,128]{2,1,0:T(8,128)S(1)} %constant_dynamic-update-slice_fusion), channel_id=1, source_target_pairs={{0,8},{16,24},{8,0},{24,16},{1,9},{17,25},{9,1},{25,17},{2,10},{18... | collective-permute-start | bytes 589832 | tf_op jit(solution)/shard_map/ppermute | solution.py:303
  198.7 0.9 collective-permute-start.33
  199.5 1.2 collective-permute-done.17.refs_1_
  200.8 1.2 shard_map.47
  202.1 2.3 %collective-permute-start.31 = (f32[2,192,128]{2,1,0:T(8,128)S(1)}, f32[2,192,128]{2,1,0:T(8,128)S(1)}, u32[]{:S(2)}, u32[]{:S(2)}) collective-permute-start(f32[2,192,128]{2,1,0:T(8,128)S(1)} %pad_maximum_fusion.1.refs_2_), channel_id=1, source_target_pairs={{0,16},{8,24},{16,0},{24,8},{1,17},{9,25},{17,1},{25,9},{2,18},{10... | collective-permute-start | bytes 589832 | tf_op jit(solution)/shard_map/ppermute | solution.py:303
  204.4 1.5 collective-permute-start.24
  205.8 3.6 %collective-permute-done.33.refs_2_ = f32[2,256,128]{2,1,0:T(8,128)S(1)} collective-permute-done((f32[2,256,128]{2,1,0:T(8,128)S(1)}, f32[2,256,128]{2,1,0:T(8,128)S(1)}, u32[]{:S(2)}, u32[]{:S(2)}) %collective-permute-start.33) | collective-permute-done | bytes 262176 | tf_op jit(solution)/shard_map/ppermute | solution.py:303
  209.4 2.1 scale.3
  211.5 1.9 collective-permute-done.31.refs_3_
  213.4 1.9 scale.4
  215.4 1.6 scale.5
  (43 shorter events, 3.1 us)
Async XLA Ops:
  1.9 54.0 %collective-permute-start.6 = (f32[16,64,128]{2,1,0:T(8,128)S(1)}, f32[16,64,128]{2,1,0:T(8,128)S(1)}, u32[]{:S(2)}, u32[]{:S(2)}) collective-permute-start(f32[16,64,128]{2,1,0:T(8,128)S(1)} %get-tuple-element.70.refs_8_.refs_0_), channel_id=1, source_target_pairs={{0,32},{32,0},{1,33},{33,1},{2,34},{34,2},{3,35},{35,3},{4,36},{36... | collective-permute-start | bytes 1572872 | tf_op jit(solution)/shard_map/ppermute | solution.py:303
  7.5 48.4 %copy-start = (f32[4,16,128,128]{3,2,1,0:T(8,128)S(1)}, f32[4,16,128,128]{3,2,1,0:T(8,128)}, u32[]{:S(2)}) copy-start(f32[4,16,128,128]{3,2,1,0:T(8,128)} %refs_3_.21) | copy-start | bytes 12582916
  7.5 79.3 %collective-permute-start = (f32[16,64,128]{2,1,0:T(8,128)S(1)}, f32[16,64,128]{2,1,0:T(8,128)S(1)}, u32[]{:S(2)}, u32[]{:S(2)}) collective-permute-start(f32[16,64,128]{2,1,0:T(8,128)S(1)} %get-tuple-element.71.refs_0_.refs_8_), channel_id=1, source_target_pairs={{0,32},{32,0},{1,33},{33,1},{2,34},{34,2},{3,35},{35,3},{4,36},{36... | collective-permute-start | bytes 1572872 | tf_op jit(solution)/shard_map/ppermute | solution.py:303
  8.1 2.5 %copy-start.1 = (f32[4,16,128,128]{3,2,1,0:T(8,128)S(1)}, f32[4,16,128,128]{3,2,1,0:T(8,128)}, u32[]{:S(2)}) copy-start(f32[4,16,128,128]{3,2,1,0:T(8,128)} %refs_2_.3) | copy-start | bytes 12582916
  11.2 11.5 %collective-permute-start.1 = (f32[4,128,128]{2,1,0:T(8,128)S(1)}, f32[4,128,128]{2,1,0:T(8,128)S(1)}, u32[]{:S(2)}, u32[]{:S(2)}) collective-permute-start(f32[4,128,128]{2,1,0:T(8,128)S(1)} %get-tuple-element.36), channel_id=1, source_target_pairs={{0,8},{16,24},{8,0},{24,16},{1,9},{17,25},{9,1},{25,17},{2,10},{18... | collective-permute-start | bytes 786440 | tf_op jit(solution)/shard_map/ppermute | solution.py:303
  11.3 11.4 %collective-permute-start.2 = (f32[4,128,128]{2,1,0:T(8,128)S(1)}, f32[4,128,128]{2,1,0:T(8,128)S(1)}, u32[]{:S(2)}, u32[]{:S(2)}) collective-permute-start(f32[4,128,128]{2,1,0:T(8,128)S(1)} %get-tuple-element.37), channel_id=1, source_target_pairs={{8,16},{16,8},{9,17},{17,9},{10,18},{18,10},{11,19},{19,11},{12,20... | collective-permute-start | bytes 786440 | tf_op jit(solution)/shard_map/ppermute | solution.py:303
  12.0 4.0 %collective-permute-start.3 = (f32[4,16,128]{2,1,0:T(8,128)S(1)}, f32[4,16,128]{2,1,0:T(8,128)S(1)}, u32[]{:S(2)}, u32[]{:S(2)}) collective-permute-start(f32[4,16,128]{2,1,0:T(8,128)S(1)} %get-tuple-element.38), channel_id=1, source_target_pairs={{0,1},{2,3},{4,5},{6,7},{1,0},{3,2},{5,4},{7,6},{8,9},{10,11},{12,... | collective-permute-start | bytes 98312 | tf_op jit(solution)/shard_map/ppermute | solution.py:303
  16.0 6.7 %collective-permute-start.4 = (f32[4,16,128]{2,1,0:T(8,128)S(1)}, f32[4,16,128]{2,1,0:T(8,128)S(1)}, u32[]{:S(2)}, u32[]{:S(2)}) collective-permute-start(f32[4,16,128]{2,1,0:T(8,128)S(1)} %get-tuple-element.39), channel_id=1, source_target_pairs={{1,2},{3,4},{5,6},{2,1},{4,3},{6,5},{9,10},{11,12},{13,14},{10,9},... | collective-permute-start | bytes 98312 | tf_op jit(solution)/shard_map/ppermute | solution.py:303
  55.9 2.2 %copy-start.2 = (f32[4,16,128,128]{3,2,1,0:T(8,128)S(1)}, f32[4,16,128,128]{3,2,1,0:T(8,128)}, u32[]{:S(2)}) copy-start(f32[4,16,128,128]{3,2,1,0:T(8,128)} %refs_2_.3) | copy-start | bytes 12582916
  58.1 6.3 %copy-start.3 = (f32[4,16,128,128]{3,2,1,0:T(8,128)S(1)}, f32[4,16,128,128]{3,2,1,0:T(8,128)}, u32[]{:S(2)}) copy-start(f32[4,16,128,128]{3,2,1,0:T(8,128)} %refs_2_.3) | copy-start | bytes 12582916
  59.1 50.7 %collective-permute-start.12 = (f32[16,64,128]{2,1,0:T(8,128)S(1)}, f32[16,64,128]{2,1,0:T(8,128)S(1)}, u32[]{:S(2)}, u32[]{:S(2)}) collective-permute-start(f32[16,64,128]{2,1,0:T(8,128)S(1)} %shard_map.42.refs_0_.refs_8_), channel_id=1, source_target_pairs={{0,32},{32,0},{1,33},{33,1},{2,34},{34,2},{3,35},{35,3},{4,36},{36... | collective-permute-start | bytes 1572872 | tf_op jit(solution)/shard_map/ppermute | solution.py:303
  87.9 43.6 %collective-permute-start.5 = (f32[16,64,128]{2,1,0:T(8,128)S(1)}, f32[16,64,128]{2,1,0:T(8,128)S(1)}, u32[]{:S(2)}, u32[]{:S(2)}) collective-permute-start(f32[16,64,128]{2,1,0:T(8,128)S(1)} %shard_map.41.refs_1_.refs_0_.refs_8_), channel_id=1, source_target_pairs={{0,32},{32,0},{1,33},{33,1},{2,34},{34,2},{3,35},{35,3},{4,36},{36... | collective-permute-start | bytes 1572872 | tf_op jit(solution)/shard_map/ppermute | solution.py:303
  90.5 11.5 %collective-permute-start.7 = (f32[4,128,128]{2,1,0:T(8,128)S(1)}, f32[4,128,128]{2,1,0:T(8,128)S(1)}, u32[]{:S(2)}, u32[]{:S(2)}) collective-permute-start(f32[4,128,128]{2,1,0:T(8,128)S(1)} %get-tuple-element.40), channel_id=1, source_target_pairs={{0,8},{16,24},{8,0},{24,16},{1,9},{17,25},{9,1},{25,17},{2,10},{18... | collective-permute-start | bytes 786440 | tf_op jit(solution)/shard_map/ppermute | solution.py:303
  90.6 11.4 %collective-permute-start.8 = (f32[4,128,128]{2,1,0:T(8,128)S(1)}, f32[4,128,128]{2,1,0:T(8,128)S(1)}, u32[]{:S(2)}, u32[]{:S(2)}) collective-permute-start(f32[4,128,128]{2,1,0:T(8,128)S(1)} %get-tuple-element.41), channel_id=1, source_target_pairs={{8,16},{16,8},{9,17},{17,9},{10,18},{18,10},{11,19},{19,11},{12,20... | collective-permute-start | bytes 786440 | tf_op jit(solution)/shard_map/ppermute | solution.py:303
  91.3 4.0 %collective-permute-start.9 = (f32[4,16,128]{2,1,0:T(8,128)S(1)}, f32[4,16,128]{2,1,0:T(8,128)S(1)}, u32[]{:S(2)}, u32[]{:S(2)}) collective-permute-start(f32[4,16,128]{2,1,0:T(8,128)S(1)} %get-tuple-element.42), channel_id=1, source_target_pairs={{0,1},{2,3},{4,5},{6,7},{1,0},{3,2},{5,4},{7,6},{8,9},{10,11},{12,... | collective-permute-start | bytes 98312 | tf_op jit(solution)/shard_map/ppermute | solution.py:303
  95.3 6.7 %collective-permute-start.10 = (f32[4,16,128]{2,1,0:T(8,128)S(1)}, f32[4,16,128]{2,1,0:T(8,128)S(1)}, u32[]{:S(2)}, u32[]{:S(2)}) collective-permute-start(f32[4,16,128]{2,1,0:T(8,128)S(1)} %get-tuple-element.43), channel_id=1, source_target_pairs={{1,2},{3,4},{5,6},{2,1},{4,3},{6,5},{9,10},{11,12},{13,14},{10,9},... | collective-permute-start | bytes 98312 | tf_op jit(solution)/shard_map/ppermute | solution.py:303
  110.8 40.9 %collective-permute-start.18 = (f32[16,64,128]{2,1,0:T(8,128)S(1)}, f32[16,64,128]{2,1,0:T(8,128)S(1)}, u32[]{:S(2)}, u32[]{:S(2)}) collective-permute-start(f32[16,64,128]{2,1,0:T(8,128)S(1)} %shard_map.44.refs_0_.refs_8_), channel_id=1, source_target_pairs={{0,32},{32,0},{1,33},{33,1},{2,34},{34,2},{3,35},{35,3},{4,36},{36... | collective-permute-start | bytes 1572872 | tf_op jit(solution)/shard_map/ppermute | solution.py:303
  133.1 16.4 %collective-permute-start.13 = (f32[4,128,128]{2,1,0:T(8,128)S(1)}, f32[4,128,128]{2,1,0:T(8,128)S(1)}, u32[]{:S(2)}, u32[]{:S(2)}) collective-permute-start(f32[4,128,128]{2,1,0:T(8,128)S(1)} %get-tuple-element.44), channel_id=1, source_target_pairs={{0,8},{16,24},{8,0},{24,16},{1,9},{17,25},{9,1},{25,17},{2,10},{18... | collective-permute-start | bytes 786440 | tf_op jit(solution)/shard_map/ppermute | solution.py:303
  133.2 16.3 %collective-permute-start.14 = (f32[4,128,128]{2,1,0:T(8,128)S(1)}, f32[4,128,128]{2,1,0:T(8,128)S(1)}, u32[]{:S(2)}, u32[]{:S(2)}) collective-permute-start(f32[4,128,128]{2,1,0:T(8,128)S(1)} %get-tuple-element.45), channel_id=1, source_target_pairs={{8,16},{16,8},{9,17},{17,9},{10,18},{18,10},{11,19},{19,11},{12,20... | collective-permute-start | bytes 786440 | tf_op jit(solution)/shard_map/ppermute | solution.py:303
  133.9 43.0 %collective-permute-start.11 = (f32[16,64,128]{2,1,0:T(8,128)S(1)}, f32[16,64,128]{2,1,0:T(8,128)S(1)}, u32[]{:S(2)}, u32[]{:S(2)}) collective-permute-start(f32[16,64,128]{2,1,0:T(8,128)S(1)} %shard_map.43.refs_1_.refs_0_.refs_8_), channel_id=1, source_target_pairs={{0,32},{32,0},{1,33},{33,1},{2,34},{34,2},{3,35},{35,3},{4,36},{36... | collective-permute-start | bytes 1572872 | tf_op jit(solution)/shard_map/ppermute | solution.py:303
  138.6 4.1 %collective-permute-start.15 = (f32[4,16,128]{2,1,0:T(8,128)S(1)}, f32[4,16,128]{2,1,0:T(8,128)S(1)}, u32[]{:S(2)}, u32[]{:S(2)}) collective-permute-start(f32[4,16,128]{2,1,0:T(8,128)S(1)} %get-tuple-element.46), channel_id=1, source_target_pairs={{0,1},{2,3},{4,5},{6,7},{1,0},{3,2},{5,4},{7,6},{8,9},{10,11},{12,... | collective-permute-start | bytes 98312 | tf_op jit(solution)/shard_map/ppermute | solution.py:303
  142.8 6.7 %collective-permute-start.16 = (f32[4,16,128]{2,1,0:T(8,128)S(1)}, f32[4,16,128]{2,1,0:T(8,128)S(1)}, u32[]{:S(2)}, u32[]{:S(2)}) collective-permute-start(f32[4,16,128]{2,1,0:T(8,128)S(1)} %get-tuple-element.47), channel_id=1, source_target_pairs={{1,2},{3,4},{5,6},{2,1},{4,3},{6,5},{9,10},{11,12},{13,14},{10,9},... | collective-permute-start | bytes 98312 | tf_op jit(solution)/shard_map/ppermute | solution.py:303
  152.7 38.0 %collective-permute-start.29 = (f32[16,64,128]{2,1,0:T(8,128)S(1)}, f32[16,64,128]{2,1,0:T(8,128)S(1)}, u32[]{:S(2)}, u32[]{:S(2)}) collective-permute-start(f32[16,64,128]{2,1,0:T(8,128)S(1)} %shard_map.46.refs_0_.refs_8_), channel_id=1, source_target_pairs={{0,32},{32,0},{1,33},{33,1},{2,34},{34,2},{3,35},{35,3},{4,36},{36... | collective-permute-start | bytes 1572872 | tf_op jit(solution)/shard_map/ppermute | solution.py:303
  158.5 11.3 %collective-permute-start.25 = (f32[3,128,128]{2,1,0:T(8,128)S(1)}, f32[3,128,128]{2,1,0:T(8,128)S(1)}, u32[]{:S(2)}, u32[]{:S(2)}) collective-permute-start(f32[3,128,128]{2,1,0:T(8,128)S(1)} %get-tuple-element.54), channel_id=1, source_target_pairs={{0,8},{16,24},{8,0},{24,16},{1,9},{17,25},{9,1},{25,17},{2,10},{18... | collective-permute-start | bytes 589832 | tf_op jit(solution)/shard_map/ppermute | solution.py:303
  158.6 11.2 %collective-permute-start.26 = (f32[3,128,128]{2,1,0:T(8,128)S(1)}, f32[3,128,128]{2,1,0:T(8,128)S(1)}, u32[]{:S(2)}, u32[]{:S(2)}) collective-permute-start(f32[3,128,128]{2,1,0:T(8,128)S(1)} %get-tuple-element.55), channel_id=1, source_target_pairs={{8,16},{16,8},{9,17},{17,9},{10,18},{18,10},{11,19},{19,11},{12,20... | collective-permute-start | bytes 589832 | tf_op jit(solution)/shard_map/ppermute | solution.py:303
  159.3 3.9 %collective-permute-start.27 = (f32[3,16,128]{2,1,0:T(8,128)S(1)}, f32[3,16,128]{2,1,0:T(8,128)S(1)}, u32[]{:S(2)}, u32[]{:S(2)}) collective-permute-start(f32[3,16,128]{2,1,0:T(8,128)S(1)} %get-tuple-element.56), channel_id=1, source_target_pairs={{0,1},{2,3},{4,5},{6,7},{1,0},{3,2},{5,4},{7,6},{8,9},{10,11},{12,... | collective-permute-start | bytes 73736 | tf_op jit(solution)/shard_map/ppermute | solution.py:303
  163.2 6.6 %collective-permute-start.28 = (f32[3,16,128]{2,1,0:T(8,128)S(1)}, f32[3,16,128]{2,1,0:T(8,128)S(1)}, u32[]{:S(2)}, u32[]{:S(2)}) collective-permute-start(f32[3,16,128]{2,1,0:T(8,128)S(1)} %get-tuple-element.57), channel_id=1, source_target_pairs={{1,2},{3,4},{5,6},{2,1},{4,3},{6,5},{9,10},{11,12},{13,14},{10,9},... | collective-permute-start | bytes 73736 | tf_op jit(solution)/shard_map/ppermute | solution.py:303
  173.2 25.4 %collective-permute-start.32 = (f32[2,256,128]{2,1,0:T(8,128)S(1)}, f32[2,256,128]{2,1,0:T(8,128)S(1)}, u32[]{:S(2)}, u32[]{:S(2)}) collective-permute-start(f32[2,256,128]{2,1,0:T(8,128)S(1)} %get-tuple-element.64), channel_id=1, source_target_pairs={{0,8},{16,24},{8,0},{24,16},{1,9},{17,25},{9,1},{25,17},{2,10},{18... | collective-permute-start | bytes 786440 | tf_op jit(solution)/shard_map/ppermute | solution.py:303
  178.4 10.9 %collective-permute-start.21 = (f32[1,16,128]{2,1,0:T(8,128)S(1)}, f32[1,16,128]{2,1,0:T(8,128)S(1)}, u32[]{:S(2)}, u32[]{:S(2)}) collective-permute-start(f32[1,16,128]{2,1,0:T(8,128)S(1)} %get-tuple-element.50), channel_id=1, source_target_pairs={{0,1},{2,3},{4,5},{6,7},{1,0},{3,2},{5,4},{7,6},{8,9},{10,11},{12,... | collective-permute-start | bytes 24584 | tf_op jit(solution)/shard_map/ppermute | solution.py:303
  178.5 10.9 %collective-permute-start.22 = (f32[1,16,128]{2,1,0:T(8,128)S(1)}, f32[1,16,128]{2,1,0:T(8,128)S(1)}, u32[]{:S(2)}, u32[]{:S(2)}) collective-permute-start(f32[1,16,128]{2,1,0:T(8,128)S(1)} %get-tuple-element.51), channel_id=1, source_target_pairs={{1,2},{3,4},{5,6},{2,1},{4,3},{6,5},{9,10},{11,12},{13,14},{10,9},... | collective-permute-start | bytes 24584 | tf_op jit(solution)/shard_map/ppermute | solution.py:303
  183.5 17.3 %collective-permute-start.17 = (f32[16,64,128]{2,1,0:T(8,128)S(1)}, f32[16,64,128]{2,1,0:T(8,128)S(1)}, u32[]{:S(2)}, u32[]{:S(2)}) collective-permute-start(f32[16,64,128]{2,1,0:T(8,128)S(1)} %shard_map.45.refs_1_.refs_0_.refs_8_), channel_id=1, source_target_pairs={{0,32},{32,0},{1,33},{33,1},{2,34},{34,2},{3,35},{35,3},{4,36},{36... | collective-permute-start | bytes 1572872 | tf_op jit(solution)/shard_map/ppermute | solution.py:303
  189.3 1.3 collective-permute-start.19
  189.4 1.2 collective-permute-start.20
  191.9 10.2 %collective-permute-start.30 = (f32[2,192,128]{2,1,0:T(8,128)S(1)}, f32[2,192,128]{2,1,0:T(8,128)S(1)}, u32[]{:S(2)}, u32[]{:S(2)}) collective-permute-start(f32[2,192,128]{2,1,0:T(8,128)S(1)} %constant_dynamic-update-slice_fusion), channel_id=1, source_target_pairs={{0,8},{16,24},{8,0},{24,16},{1,9},{17,25},{9,1},{25,17},{2,10},{18... | collective-permute-start | bytes 589832 | tf_op jit(solution)/shard_map/ppermute | solution.py:303
  198.7 10.8 %collective-permute-start.33 = (f32[2,256,128]{2,1,0:T(8,128)S(1)}, f32[2,256,128]{2,1,0:T(8,128)S(1)}, u32[]{:S(2)}, u32[]{:S(2)}) collective-permute-start(f32[2,256,128]{2,1,0:T(8,128)S(1)} %pad_maximum_fusion.refs_1_), channel_id=1, source_target_pairs={{0,16},{8,24},{16,0},{24,8},{1,17},{9,25},{17,1},{25,9},{2,18},{10... | collective-permute-start | bytes 786440 | tf_op jit(solution)/shard_map/ppermute | solution.py:303
  201.9 2.4 %collective-permute-start.23 = (f32[2,64,128]{2,1,0:T(8,128)S(1)}, f32[2,64,128]{2,1,0:T(8,128)S(1)}, u32[]{:S(2)}, u32[]{:S(2)}) collective-permute-start(f32[2,64,128]{2,1,0:T(8,128)S(1)} %get-tuple-element.53), channel_id=1, source_target_pairs={{0,8},{16,24},{8,0},{24,16},{1,9},{17,25},{9,1},{25,17},{2,10},{18... | collective-permute-start | bytes 196616 | tf_op jit(solution)/shard_map/ppermute | solution.py:303
  202.1 11.3 %collective-permute-start.31 = (f32[2,192,128]{2,1,0:T(8,128)S(1)}, f32[2,192,128]{2,1,0:T(8,128)S(1)}, u32[]{:S(2)}, u32[]{:S(2)}) collective-permute-start(f32[2,192,128]{2,1,0:T(8,128)S(1)} %pad_maximum_fusion.1.refs_2_), channel_id=1, source_target_pairs={{0,16},{8,24},{16,0},{24,8},{1,17},{9,25},{17,1},{25,9},{2,18},{10... | collective-permute-start | bytes 589832 | tf_op jit(solution)/shard_map/ppermute | solution.py:303
  204.4 11.0 %collective-permute-start.24 = (f32[2,64,128]{2,1,0:T(8,128)S(1)}, f32[2,64,128]{2,1,0:T(8,128)S(1)}, u32[]{:S(2)}, u32[]{:S(2)}) collective-permute-start(f32[2,64,128]{2,1,0:T(8,128)S(1)} %pad_maximum_fusion.2.refs_1_), channel_id=1, source_target_pairs={{0,16},{8,24},{16,0},{24,8},{1,17},{9,25},{17,1},{25,9},{2,18},{10... | collective-permute-start | bytes 196616 | tf_op jit(solution)/shard_map/ppermute | solution.py:303

commit v4 on v3

--- a/solution.py
+++ b/solution.py
@@ -9,7 +9,7 @@
 
 
 STEPS = 4
-CUTS = ((0, 64, 128),) * 4
+CUTS = (0, 64, 128)
 MIB = 1 << 20
 EVEN_X, EVEN_Z = 4, 5
 VMEM = pl.BlockSpec(memory_space=pltpu.VMEM)
@@ -106,13 +106,13 @@
     )(info, *args)
 
 
-def row_kernel(spans, mapped, low_open, high_open, final, info, *refs):
+def row_kernel(begin, mapped, low_open, high_open, final, info, *refs):
     centre, received, field, crowding, lon_a, lon_b, lev_a, lev_b = refs[:8]
     refs = refs[8:]
     below, refs = (None, refs) if low_open else (refs[0], refs[1:])
     above, refs = (None, refs) if high_open else (refs[0], refs[1:])
-    n = centre.shape[0]
-    begin, end = spans[0][0], spans[-1][1]
+    n, depth = centre.shape[0], centre.shape[1]
+    end = begin + depth
     even_x, even_z = info[EVEN_X] == 1, info[EVEN_Z] == 1
     second = info[1] if mapped else 0
     here = info[0]
@@ -125,32 +125,28 @@
         low_z = jnp.where(even_z, b, a) if low_open else below[x, below.shape[1] - 1 :, :]
         high_z = jnp.where(even_z, a, b) if high_open else above[x, 0:1, :]
         near, far = received[x], field[second, x, begin:end]
-        value = cells(
+        out[x] = cells(
             centre[x], low_x, high_x, near, far, low_z, high_z, crowding[here, x, begin:end]
         )
-        for (a, b), out in zip(spans, outs):
-            out[x] = value[a - begin : b - begin]
         return carry
 
-    outs = refs[: len(spans)]
+    out = refs[0]
     over_x(n, visit)
     if final:
-        refs[-1][0], refs[-1][1] = line_sums(lambda x: outs[0][x], n)
-
-
-def row_step(info, p, parts, received, cuts, next_cuts, field, crowding, ghosts, mapped, final):
+        refs[1][0], refs[1][1] = line_sums(lambda x: out[x], n)
+
+
+def row_step(info, p, parts, received, cuts, field, crowding, ghosts, mapped, final):
     n, depth, species = parts[p].shape
-    begin, end = cuts[p], cuts[p + 1]
-    spans = [(a, b) for a, b in zip(next_cuts[:-1], next_cuts[1:]) if begin <= a and b <= end]
     low_open, high_open = p == 0, p == len(parts) - 1
-    out_shape = [jax.ShapeDtypeStruct((n, b - a, species), jnp.float32) for a, b in spans]
+    out_shape = [jax.ShapeDtypeStruct((n, depth, species), jnp.float32)]
     if final:
         out_shape.append(jax.ShapeDtypeStruct((2, depth, species), jnp.float32))
     args = [parts[p], received, field, crowding, *ghosts]
     args += [] if low_open else [parts[p - 1]]
     args += [] if high_open else [parts[p + 1]]
     return pl.pallas_call(
-        functools.partial(row_kernel, spans, mapped, low_open, high_open, final),
+        functools.partial(row_kernel, cuts[p], mapped, low_open, high_open, final),
         in_specs=[SMEM] + [VMEM] * len(args),
         out_specs=[VMEM] * len(out_shape),
         out_shape=out_shape,
@@ -328,35 +324,41 @@
 
     parts = [
         lax.dynamic_slice(density, (order[0], 0, a, 0), (1, n, b - a, species))[0]
-        for a, b in zip(CUTS[0][:-1], CUTS[0][1:])
+        for a, b in zip(CUTS[:-1], CUTS[1:])
     ]
     arriving = swapped(parts)
     even = [1 - lax.axis_index(axis) % 2 for axis in ("lon", "lev")]
     info = jnp.stack([*order, *even]).astype(jnp.int32)
-    rest = None
+    cuts, last_step = CUTS, STEPS - 1
+    sent = edges(info, [], density, True)
+    row_ghosts = exchanged(sent)
+    (ahead,) = rest_step(info, [], density, crowding, row_ghosts, True)
+    sent = edges(info, [], ahead)
+    ghosts, ghost_from = exchanged(sent), 0
+    field = density
     for step in range(STEPS):
-        start, final = step == 0, step == STEPS - 1
-        cuts = CUTS[step]
-        next_cuts = cuts if final else CUTS[step + 1]
-        field = density if start else rest
-        first = [] if start else parts
-        sent = edges(info, first, None if final else field, start)
-        ghosts = exchanged(sent)
+        start, final = step == 0, step == last_step
+        if not start:
+            field = ahead
         if final:
-            sent = edges(info, [], rest)
-            ghosts_rest = exchanged(sent)
+            sent = edges(info, parts, None)
+            row_ghosts = exchanged(sent)
+            beside, beside_sums, ended = rest_step(
+                info, parts, field, crowding, ghosts, False, (0,), ghost_from, True, ended
+            )
+        elif not start:
+            (ahead,) = rest_step(info, parts, field, crowding, ghosts, False, ghost_from=ghost_from)
+            sent = edges(info, parts, ahead)
+            row_ghosts = ghosts = exchanged(sent)
+            ghost_from = -1
+        if step == last_step - 1:
             deep, deep_sums, ended = rest_step(
-                info, [], rest, crowding, ghosts_rest, False, (1, 2), 0, True
+                info, [], ahead, crowding, ghosts, False, (1, 2), ghost_from, True
             )
-            beside, beside_sums, ended = rest_step(
-                info, first, rest, crowding, ghosts_rest, False, (0,), 0, True, ended
-            )
-        else:
-            (rest,) = rest_step(info, first, field, crowding, ghosts, start)
         new = []
         for p in range(len(parts)):
             new += row_step(
-                info, p, parts, arriving[p], cuts, next_cuts, field, crowding, ghosts, start, final
+                info, p, parts, arriving[p], cuts, field, crowding, row_ghosts, start, final
             )
         if not final:
             parts = new

time: 218 us -> 209 us (0.959)
  the two profiles are of different devices: /device:TPU:66 before, /device:TPU:88 now
where the time goes in v4:
time: 209 us; the launch traced here: 208 us
  starting transfers between devices  98.9 us (47%)
  waiting for transfers between devices  71.8 us (34%)
  Pallas kernels  30.8 us (15%)
  local copies, waits for them, and re-layouts  5.77 us (3%)
    ppermute x34, starting transfers between devices, paired(): return lax.ppermute(array, axis, [*pairs, *((b, a) for a, b in pairs)])  98.9 us
    ppermute x34, waiting for transfers between devices, paired(): return lax.ppermute(array, axis, [*pairs, *((b, a) for a, b in pairs)])  71.8 us
    pallas_call x5, Pallas kernels, rest_step(): pl.pallas_call(functools.partial(rest_kernel, len(first), mapped, rows, g...  13.8 us
    pallas_call x8, Pallas kernels, row_step(): pl.pallas_call(functools.partial(row_kernel, cuts[p], mapped, low_open, h...  8.23 us
    pallas_call x3, Pallas kernels, scale(): pl.pallas_call(functools.partial(scale_kernel, rows, begins), out_shape=[...  5.62 us
    unnamed x9, local copies, waits for them, and re-layouts  4.4 us
  transfers between devices with their start and end apart: 34, of which 13 were waited for; matrix products, arithmetic and copies ran while one was open for 0% of the time, Pallas kernels for 14%

profile of v4, /device:TPU:88, one launch (start us, length us, event | category | flops | bytes accessed | tf_op | source)
XLA Modules:
  0.0 208.4 jit_solution(12145240531463196481)
XLA Ops:
  0.6 1.3 dynamic-slice_bitcast_fusion
  1.9 5.5 %collective-permute-start.6 = (f32[16,64,128]{2,1,0:T(8,128)S(1)}, f32[16,64,128]{2,1,0:T(8,128)S(1)}, u32[]{:S(2)}, u32[]{:S(2)}) collective-permute-start(f32[16,64,128]{2,1,0:T(8,128)S(1)} %get-tuple-element.70.refs_8_.refs_0_), channel_id=1, source_target_pairs={{0,32},{32,0},{1,33},{33,1},{2,34},{34,2},{3,35},{35,3},{4,36},{36... | collective-permute-start | bytes 1572872 | tf_op jit(solution)/shard_map/ppermute | solution.py:299
  8.0 2.2 %copy-done.1 = f32[4,16,128,128]{3,2,1,0:T(8,128)S(1)} copy-done((f32[4,16,128,128]{3,2,1,0:T(8,128)S(1)}, f32[4,16,128,128]{3,2,1,0:T(8,128)}, u32[]{:S(2)}) %copy-start.1) | copy-done | bytes 4194328
  10.2 0.6 edges.5
  11.0 0.8 collective-permute-start.2
  11.8 1.6 collective-permute-start.3
  13.4 2.4 %collective-permute-done.3.refs_6_.refs_4_ = f32[4,16,128]{2,1,0:T(8,128)S(1)} collective-permute-done((f32[4,16,128]{2,1,0:T(8,128)S(1)}, f32[4,16,128]{2,1,0:T(8,128)S(1)}, u32[]{:S(2)}, u32[]{:S(2)}) %collective-permute-start.3) | collective-permute-done | bytes 32800 | tf_op jit(solution)/shard_map/ppermute | solution.py:299
  15.8 3.6 %collective-permute-start.4 = (f32[4,16,128]{2,1,0:T(8,128)S(1)}, f32[4,16,128]{2,1,0:T(8,128)S(1)}, u32[]{:S(2)}, u32[]{:S(2)}) collective-permute-start(f32[4,16,128]{2,1,0:T(8,128)S(1)} %get-tuple-element.39), channel_id=1, source_target_pairs={{1,2},{3,4},{5,6},{2,1},{4,3},{6,5},{9,10},{11,12},{13,14},{10,9},... | collective-permute-start | bytes 98312 | tf_op jit(solution)/shard_map/ppermute | solution.py:299
  19.4 3.1 %collective-permute-done.4.refs_7_.refs_5_ = f32[4,16,128]{2,1,0:T(8,128)S(1)} collective-permute-done((f32[4,16,128]{2,1,0:T(8,128)S(1)}, f32[4,16,128]{2,1,0:T(8,128)S(1)}, u32[]{:S(2)}, u32[]{:S(2)}) %collective-permute-start.4) | collective-permute-done | bytes 32800 | tf_op jit(solution)/shard_map/ppermute | solution.py:299
  22.5 33.4 %collective-permute-done.6.refs_1_ = f32[16,64,128]{2,1,0:T(8,128)S(1)} collective-permute-done((f32[16,64,128]{2,1,0:T(8,128)S(1)}, f32[16,64,128]{2,1,0:T(8,128)S(1)}, u32[]{:S(2)}, u32[]{:S(2)}) %collective-permute-start.6) | collective-permute-done | bytes 524320 | tf_op jit(solution)/shard_map/ppermute | solution.py:299
  55.9 2.2 %copy-done.2 = f32[4,16,128,128]{3,2,1,0:T(8,128)S(1)} copy-done((f32[4,16,128,128]{3,2,1,0:T(8,128)S(1)}, f32[4,16,128,128]{3,2,1,0:T(8,128)}, u32[]{:S(2)}) %copy-start.2) | copy-done | bytes 4194328
  58.1 1.0 shard_map.42.refs_0_.refs_8_
  59.1 5.3 %collective-permute-start.16 = (f32[16,64,128]{2,1,0:T(8,128)S(1)}, f32[16,64,128]{2,1,0:T(8,128)S(1)}, u32[]{:S(2)}, u32[]{:S(2)}) collective-permute-start(f32[16,64,128]{2,1,0:T(8,128)S(1)} %shard_map.42.refs_0_.refs_8_), channel_id=1, source_target_pairs={{0,32},{32,0},{1,33},{33,1},{2,34},{34,2},{3,35},{35,3},{4,36},{36... | collective-permute-start | bytes 1572872 | tf_op jit(solution)/shard_map/ppermute | solution.py:299
  64.4 2.8 %rest.5.refs_0_.refs_2_ = f32[3,16,128,128]{3,2,1,0:T(8,128)S(1)} custom-call(s32[6]{0:T(128)S(1)} %stack.42.info, f32[4,16,128,128]{3,2,1,0:T(8,128)S(1)} %copy-done.3, f32[4,16,128,128]{3,2,1,0:T(8,128)S(1)} %copy-done, f32[4,128,128]{2,1,0:T(8,128)S(1)} %collective-permute-done.1.refs_4_.refs_2_, ...), custom_call_target="tpu_custom_call" | custom-call | flops 15728640 | bytes 12582912 | tf_op jit(solution)/shard_map/rest/pallas_call | solution.py:218
  67.2 0.6 edges.6
  67.9 0.7 collective-permute-start.8
  68.6 1.6 collective-permute-start.9
  70.2 7.2 %collective-permute-done.refs_1_ = f32[16,64,128]{2,1,0:T(8,128)S(1)} collective-permute-done((f32[16,64,128]{2,1,0:T(8,128)S(1)}, f32[16,64,128]{2,1,0:T(8,128)S(1)}, u32[]{:S(2)}, u32[]{:S(2)}) %collective-permute-start) | collective-permute-done | bytes 524320 | tf_op jit(solution)/shard_map/ppermute | solution.py:299
  77.3 3.7 %collective-permute-start.10 = (f32[3,16,128]{2,1,0:T(8,128)S(1)}, f32[3,16,128]{2,1,0:T(8,128)S(1)}, u32[]{:S(2)}, u32[]{:S(2)}) collective-permute-start(f32[3,16,128]{2,1,0:T(8,128)S(1)} %get-tuple-element.43), channel_id=1, source_target_pairs={{1,2},{3,4},{5,6},{2,1},{4,3},{6,5},{9,10},{11,12},{13,14},{10,9},... | collective-permute-start | bytes 73736 | tf_op jit(solution)/shard_map/ppermute | solution.py:299
  81.0 1.0 shard_map.41.refs_1_.refs_0_.refs_8_
  82.0 5.2 %collective-permute-start.5 = (f32[16,64,128]{2,1,0:T(8,128)S(1)}, f32[16,64,128]{2,1,0:T(8,128)S(1)}, u32[]{:S(2)}, u32[]{:S(2)}) collective-permute-start(f32[16,64,128]{2,1,0:T(8,128)S(1)} %shard_map.41.refs_1_.refs_0_.refs_8_), channel_id=1, source_target_pairs={{0,32},{32,0},{1,33},{33,1},{2,34},{34,2},{3,35},{35,3},{4,36},{36... | collective-permute-start | bytes 1572872 | tf_op jit(solution)/shard_map/ppermute | solution.py:299
  87.2 2.7 %rest.6.refs_2_ = f32[3,16,128,128]{3,2,1,0:T(8,128)S(1)} custom-call(s32[6]{0:T(128)S(1)} %stack.42.info, f32[16,64,128]{2,1,0:T(8,128)S(1)} %shard_map.42.refs_0_.refs_8_, f32[16,64,128]{2,1,0:T(8,128)S(1)} %shard_map.41.refs_1_.refs_0_.refs_8_, f32[3,16,128,128]{3,2,1,0:T(8,128)S(1)} %rest.5.refs_0_.refs_2_, f32[4,16,128,128]{3,2,1,0:T(8,128)S(1)} %copy-done, ...), custom_call_target="tpu_custom_call" | custom-call | flops 15728640 | bytes 12582912 | tf_op jit(solution)/shard_map/rest/pallas_call | solution.py:218
  90.0 0.6 edges.7
  90.7 0.7 collective-permute-start.12
  91.4 4.9 %collective-permute-start.13 = (f32[4,16,128]{2,1,0:T(8,128)S(1)}, f32[4,16,128]{2,1,0:T(8,128)S(1)}, u32[]{:S(2)}, u32[]{:S(2)}) collective-permute-start(f32[4,16,128]{2,1,0:T(8,128)S(1)} %get-tuple-element.46), channel_id=1, source_target_pairs={{0,1},{2,3},{4,5},{6,7},{1,0},{3,2},{5,4},{7,6},{8,9},{10,11},{12,... | collective-permute-start | bytes 98312 | tf_op jit(solution)/shard_map/ppermute | solution.py:299
  96.3 1.9 collective-permute-done.13.refs_6_
  98.2 1.9 collective-permute-start.14
  100.1 5.1 %collective-permute-done.14.refs_7_ = f32[4,16,128]{2,1,0:T(8,128)S(1)} collective-permute-done((f32[4,16,128]{2,1,0:T(8,128)S(1)}, f32[4,16,128]{2,1,0:T(8,128)S(1)}, u32[]{:S(2)}, u32[]{:S(2)}) %collective-permute-start.14) | collective-permute-done | bytes 32800 | tf_op jit(solution)/shard_map/ppermute | solution.py:299
  105.2 1.0 shard_map.44.refs_0_.refs_8_
  106.2 3.7 %collective-permute-start.22 = (f32[16,64,128]{2,1,0:T(8,128)S(1)}, f32[16,64,128]{2,1,0:T(8,128)S(1)}, u32[]{:S(2)}, u32[]{:S(2)}) collective-permute-start(f32[16,64,128]{2,1,0:T(8,128)S(1)} %shard_map.44.refs_0_.refs_8_), channel_id=1, source_target_pairs={{0,32},{32,0},{1,33},{33,1},{2,34},{34,2},{3,35},{35,3},{4,36},{36... | collective-permute-start | bytes 1572872 | tf_op jit(solution)/shard_map/ppermute | solution.py:299
  110.0 1.0 shard_map.43.refs_1_.refs_0_.refs_8_
  111.0 2.7 %rest.7.refs_2_.refs_0_ = f32[3,16,128,128]{3,2,1,0:T(8,128)S(1)} custom-call(s32[6]{0:T(128)S(1)} %stack.42.info, f32[16,64,128]{2,1,0:T(8,128)S(1)} %shard_map.44.refs_0_.refs_8_, f32[16,64,128]{2,1,0:T(8,128)S(1)} %shard_map.43.refs_1_.refs_0_.refs_8_, f32[3,16,128,128]{3,2,1,0:T(8,128)S(1)} %rest.6.refs_2_, f32[4,16,128,128]{3,2,1,0:T(8,128)S(1)} %copy-done, ...), custom_call_target="tpu_custom_call" | custom-call | flops 15728640 | bytes 12582912 | tf_op jit(solution)/shard_map/rest/pallas_call | solution.py:218
  113.7 0.6 edges.8
  114.3 4.2 %collective-permute-start.17 = (f32[4,128,128]{2,1,0:T(8,128)S(1)}, f32[4,128,128]{2,1,0:T(8,128)S(1)}, u32[]{:S(2)}, u32[]{:S(2)}) collective-permute-start(f32[4,128,128]{2,1,0:T(8,128)S(1)} %get-tuple-element.48), channel_id=1, source_target_pairs={{0,8},{16,24},{8,0},{24,16},{1,9},{17,25},{9,1},{25,17},{2,10},{18... | collective-permute-start | bytes 786440 | tf_op jit(solution)/shard_map/ppermute | solution.py:299
  118.6 0.7 collective-permute-start.18
  119.2 2.2 %collective-permute-start.15 = (f32[16,64,128]{2,1,0:T(8,128)S(1)}, f32[16,64,128]{2,1,0:T(8,128)S(1)}, u32[]{:S(2)}, u32[]{:S(2)}) collective-permute-start(f32[16,64,128]{2,1,0:T(8,128)S(1)} %shard_map.43.refs_1_.refs_0_.refs_8_), channel_id=1, source_target_pairs={{0,32},{32,0},{1,33},{33,1},{2,34},{34,2},{3,35},{35,3},{4,36},{36... | collective-permute-start | bytes 1572872 | tf_op jit(solution)/shard_map/ppermute | solution.py:299
  121.4 21.4 %collective-permute-start.19 = (f32[4,16,128]{2,1,0:T(8,128)S(1)}, f32[4,16,128]{2,1,0:T(8,128)S(1)}, u32[]{:S(2)}, u32[]{:S(2)}) collective-permute-start(f32[4,16,128]{2,1,0:T(8,128)S(1)} %get-tuple-element.50), channel_id=1, source_target_pairs={{0,1},{2,3},{4,5},{6,7},{1,0},{3,2},{5,4},{7,6},{8,9},{10,11},{12,... | collective-permute-start | bytes 98312 | tf_op jit(solution)/shard_map/ppermute | solution.py:299
  142.8 2.2 %collective-permute-done.19.refs_6_.refs_4_ = f32[4,16,128]{2,1,0:T(8,128)S(1)} collective-permute-done((f32[4,16,128]{2,1,0:T(8,128)S(1)}, f32[4,16,128]{2,1,0:T(8,128)S(1)}, u32[]{:S(2)}, u32[]{:S(2)}) %collective-permute-start.19) | collective-permute-done | bytes 32800 | tf_op jit(solution)/shard_map/ppermute | solution.py:299
  145.1 1.9 collective-permute-start.20
  147.0 4.8 %collective-permute-done.20.refs_7_.refs_5_ = f32[4,16,128]{2,1,0:T(8,128)S(1)} collective-permute-done((f32[4,16,128]{2,1,0:T(8,128)S(1)}, f32[4,16,128]{2,1,0:T(8,128)S(1)}, u32[]{:S(2)}, u32[]{:S(2)}) %collective-permute-start.20) | collective-permute-done | bytes 32800 | tf_op jit(solution)/shard_map/ppermute | solution.py:299
  151.8 1.0 shard_map.46.refs_0_.refs_8_
  152.8 1.1 collective-permute-start.29
  153.8 3.3 %rest.8 = (f32[2,16,128,128]{3,2,1,0:T(8,128)S(1)}, f32[2,256,128]{2,1,0:T(8,128)S(1)}, f32[4,16,128,128]{3,2,1,0:T(8,128)}) custom-call(s32[6]{0:T(128)S(1)} %stack.42.info, f32[3,16,128,128]{3,2,1,0:T(8,128)S(1)} %rest.7.refs_2_.refs_0_, f32[4,16,128,128]{3,2,1,0:T(8,128)S(1)} %copy-done, f32[4,128,128]{2,1,0:T(8,128)S(1)} %collective-permute-done.17.refs_4_.refs_2_, ...), custom_call_target="tpu_custom_call" | custom-call | flops 10485760 | bytes 8388608 | tf_op jit(solution)/shard_map/rest/pallas_call | solution.py:218
  157.1 3.5 %collective-permute-start.32 = (f32[2,256,128]{2,1,0:T(8,128)S(1)}, f32[2,256,128]{2,1,0:T(8,128)S(1)}, u32[]{:S(2)}, u32[]{:S(2)}) collective-permute-start(f32[2,256,128]{2,1,0:T(8,128)S(1)} %get-tuple-element.64), channel_id=1, source_target_pairs={{0,8},{16,24},{8,0},{24,16},{1,9},{17,25},{9,1},{25,17},{2,10},{18... | collective-permute-start | bytes 786440 | tf_op jit(solution)/shard_map/ppermute | solution.py:299
  160.6 3.2 %collective-permute-done.15.refs_1_ = f32[16,64,128]{2,1,0:T(8,128)S(1)} collective-permute-done((f32[16,64,128]{2,1,0:T(8,128)S(1)}, f32[16,64,128]{2,1,0:T(8,128)S(1)}, u32[]{:S(2)}, u32[]{:S(2)}) %collective-permute-start.15) | collective-permute-done | bytes 524320 | tf_op jit(solution)/shard_map/ppermute | solution.py:299
  163.8 1.0 shard_map.45.refs_1_.refs_0_.refs_8_
  164.7 0.6 edges.9
  165.3 4.6 %collective-permute-start.25 = (f32[1,16,128]{2,1,0:T(8,128)S(1)}, f32[1,16,128]{2,1,0:T(8,128)S(1)}, u32[]{:S(2)}, u32[]{:S(2)}) collective-permute-start(f32[1,16,128]{2,1,0:T(8,128)S(1)} %get-tuple-element.54), channel_id=1, source_target_pairs={{0,1},{2,3},{4,5},{6,7},{1,0},{3,2},{5,4},{7,6},{8,9},{10,11},{12,... | collective-permute-start | bytes 24584 | tf_op jit(solution)/shard_map/ppermute | solution.py:299
  169.9 4.5 %collective-permute-start.26 = (f32[1,16,128]{2,1,0:T(8,128)S(1)}, f32[1,16,128]{2,1,0:T(8,128)S(1)}, u32[]{:S(2)}, u32[]{:S(2)}) collective-permute-start(f32[1,16,128]{2,1,0:T(8,128)S(1)} %get-tuple-element.55), channel_id=1, source_target_pairs={{1,2},{3,4},{5,6},{2,1},{4,3},{6,5},{9,10},{11,12},{13,14},{10,9},... | collective-permute-start | bytes 24584 | tf_op jit(solution)/shard_map/ppermute | solution.py:299
  174.5 2.8 %collective-permute-start.21 = (f32[16,64,128]{2,1,0:T(8,128)S(1)}, f32[16,64,128]{2,1,0:T(8,128)S(1)}, u32[]{:S(2)}, u32[]{:S(2)}) collective-permute-start(f32[16,64,128]{2,1,0:T(8,128)S(1)} %shard_map.45.refs_1_.refs_0_.refs_8_), channel_id=1, source_target_pairs={{0,32},{32,0},{1,33},{33,1},{2,34},{34,2},{3,35},{35,3},{4,36},{36... | collective-permute-start | bytes 1572872 | tf_op jit(solution)/shard_map/ppermute | solution.py:299
  177.2 2.3 %rest.9 = (f32[1,16,128,128]{3,2,1,0:T(8,128)S(1)}, f32[2,128,128]{2,1,0:T(8,128)S(1)}, f32[4,16,128,128]{3,2,1,0:T(8,128)}) custom-call(s32[6]{0:T(128)S(1)} %stack.42.info, f32[16,64,128]{2,1,0:T(8,128)S(1)} %shard_map.46.refs_0_.refs_8_, f32[16,64,128]{2,1,0:T(8,128)S(1)} %shard_map.45.refs_1_.refs_0_.refs_8_, ...), custom_call_target="tpu_custom_call", output_to_operand_aliasing={{2}: (9, {})} | custom-call | flops 5242880 | bytes 4194304 | tf_op jit(solution)/shard_map/rest/pallas_call | solution.py:218
  179.5 0.9 collective-permute-start.23
  180.4 0.7 collective-permute-start.24
  181.3 1.2 shard_map.48
  182.5 6.6 %collective-permute-start.30 = (f32[2,192,128]{2,1,0:T(8,128)S(1)}, f32[2,192,128]{2,1,0:T(8,128)S(1)}, u32[]{:S(2)}, u32[]{:S(2)}) collective-permute-start(f32[2,192,128]{2,1,0:T(8,128)S(1)} %constant_dynamic-update-slice_fusion), channel_id=1, source_target_pairs={{0,8},{16,24},{8,0},{24,16},{1,9},{17,25},{9,1},{25,17},{2,10},{18... | collective-permute-start | bytes 589832 | tf_op jit(solution)/shard_map/ppermute | solution.py:299
  189.1 1.1 collective-permute-start.33
  190.3 3.6 %collective-permute-done.21.refs_1_ = f32[16,64,128]{2,1,0:T(8,128)S(1)} collective-permute-done((f32[16,64,128]{2,1,0:T(8,128)S(1)}, f32[16,64,128]{2,1,0:T(8,128)S(1)}, u32[]{:S(2)}, u32[]{:S(2)}) %collective-permute-start.21) | collective-permute-done | bytes 524320 | tf_op jit(solution)/shard_map/ppermute | solution.py:299
  193.9 1.2 shard_map.47
  195.4 1.0 collective-permute-done.27
  196.5 2.6 %collective-permute-start.28 = (f32[2,64,128]{2,1,0:T(8,128)S(1)}, f32[2,64,128]{2,1,0:T(8,128)S(1)}, u32[]{:S(2)}, u32[]{:S(2)}) collective-permute-start(f32[2,64,128]{2,1,0:T(8,128)S(1)} %pad_maximum_fusion.2.refs_1_), channel_id=1, source_target_pairs={{0,16},{8,24},{16,0},{24,8},{1,17},{9,25},{17,1},{25,9},{2,18},{10... | collective-permute-start | bytes 196616 | tf_op jit(solution)/shard_map/ppermute | solution.py:299
  199.1 2.1 %scale.3 = (f32[4,16,128,128]{3,2,1,0:T(8,128)}, f32[4,16,128,128]{3,2,1,0:T(8,128)}) custom-call(s32[6]{0:T(128)S(1)} %stack.42.info, f32[2,16,128,128]{3,2,1,0:T(8,128)S(1)} %get-tuple-element.63.refs_0_, f32[2,256,128]{2,1,0:T(8,128)S(1)} %pad_maximum_fusion.refs_1_, ...), custom_call_target="tpu_custom_call", output_to_operand_aliasing={{1}: (4, {})} | custom-call | flops 1572864 | bytes 4194304 | tf_op jit(solution)/shard_map/scale/pallas_call | solution.py:282
  201.2 3.5 %collective-permute-done.31.refs_3_ = f32[2,192,128]{2,1,0:T(8,128)S(1)} collective-permute-done((f32[2,192,128]{2,1,0:T(8,128)S(1)}, f32[2,192,128]{2,1,0:T(8,128)S(1)}, u32[]{:S(2)}, u32[]{:S(2)}) %collective-permute-start.31) | collective-permute-done | bytes 196640 | tf_op jit(solution)/shard_map/ppermute | solution.py:299
  204.7 1.9 scale.4
  206.7 1.6 scale.5
  (43 shorter events, 1.6 us)
Async XLA Ops:
  1.9 54.0 %collective-permute-start.6 = (f32[16,64,128]{2,1,0:T(8,128)S(1)}, f32[16,64,128]{2,1,0:T(8,128)S(1)}, u32[]{:S(2)}, u32[]{:S(2)}) collective-permute-start(f32[16,64,128]{2,1,0:T(8,128)S(1)} %get-tuple-element.70.refs_8_.refs_0_), channel_id=1, source_target_pairs={{0,32},{32,0},{1,33},{33,1},{2,34},{34,2},{3,35},{35,3},{4,36},{36... | collective-permute-start | bytes 1572872 | tf_op jit(solution)/shard_map/ppermute | solution.py:299
  7.4 69.9 %collective-permute-start = (f32[16,64,128]{2,1,0:T(8,128)S(1)}, f32[16,64,128]{2,1,0:T(8,128)S(1)}, u32[]{:S(2)}, u32[]{:S(2)}) collective-permute-start(f32[16,64,128]{2,1,0:T(8,128)S(1)} %get-tuple-element.71.refs_0_.refs_8_), channel_id=1, source_target_pairs={{0,32},{32,0},{1,33},{33,1},{2,34},{34,2},{3,35},{35,3},{4,36},{36... | collective-permute-start | bytes 1572872 | tf_op jit(solution)/shard_map/ppermute | solution.py:299
  8.0 2.2 %copy-start.1 = (f32[4,16,128,128]{3,2,1,0:T(8,128)S(1)}, f32[4,16,128,128]{3,2,1,0:T(8,128)}, u32[]{:S(2)}) copy-start(f32[4,16,128,128]{3,2,1,0:T(8,128)} %refs_2_.3) | copy-start | bytes 12582916
  10.2 45.7 %copy-start = (f32[4,16,128,128]{3,2,1,0:T(8,128)S(1)}, f32[4,16,128,128]{3,2,1,0:T(8,128)}, u32[]{:S(2)}) copy-start(f32[4,16,128,128]{3,2,1,0:T(8,128)} %refs_3_.21) | copy-start | bytes 12582916
  10.9 11.6 %collective-permute-start.1 = (f32[4,128,128]{2,1,0:T(8,128)S(1)}, f32[4,128,128]{2,1,0:T(8,128)S(1)}, u32[]{:S(2)}, u32[]{:S(2)}) collective-permute-start(f32[4,128,128]{2,1,0:T(8,128)S(1)} %get-tuple-element.36), channel_id=1, source_target_pairs={{0,8},{16,24},{8,0},{24,16},{1,9},{17,25},{9,1},{25,17},{2,10},{18... | collective-permute-start | bytes 786440 | tf_op jit(solution)/shard_map/ppermute | solution.py:299
  11.0 11.5 %collective-permute-start.2 = (f32[4,128,128]{2,1,0:T(8,128)S(1)}, f32[4,128,128]{2,1,0:T(8,128)S(1)}, u32[]{:S(2)}, u32[]{:S(2)}) collective-permute-start(f32[4,128,128]{2,1,0:T(8,128)S(1)} %get-tuple-element.37), channel_id=1, source_target_pairs={{8,16},{16,8},{9,17},{17,9},{10,18},{18,10},{11,19},{19,11},{12,20... | collective-permute-start | bytes 786440 | tf_op jit(solution)/shard_map/ppermute | solution.py:299
  11.8 4.0 %collective-permute-start.3 = (f32[4,16,128]{2,1,0:T(8,128)S(1)}, f32[4,16,128]{2,1,0:T(8,128)S(1)}, u32[]{:S(2)}, u32[]{:S(2)}) collective-permute-start(f32[4,16,128]{2,1,0:T(8,128)S(1)} %get-tuple-element.38), channel_id=1, source_target_pairs={{0,1},{2,3},{4,5},{6,7},{1,0},{3,2},{5,4},{7,6},{8,9},{10,11},{12,... | collective-permute-start | bytes 98312 | tf_op jit(solution)/shard_map/ppermute | solution.py:299
  15.8 6.7 %collective-permute-start.4 = (f32[4,16,128]{2,1,0:T(8,128)S(1)}, f32[4,16,128]{2,1,0:T(8,128)S(1)}, u32[]{:S(2)}, u32[]{:S(2)}) collective-permute-start(f32[4,16,128]{2,1,0:T(8,128)S(1)} %get-tuple-element.39), channel_id=1, source_target_pairs={{1,2},{3,4},{5,6},{2,1},{4,3},{6,5},{9,10},{11,12},{13,14},{10,9},... | collective-permute-start | bytes 98312 | tf_op jit(solution)/shard_map/ppermute | solution.py:299
  55.9 2.2 %copy-start.2 = (f32[4,16,128,128]{3,2,1,0:T(8,128)S(1)}, f32[4,16,128,128]{3,2,1,0:T(8,128)}, u32[]{:S(2)}) copy-start(f32[4,16,128,128]{3,2,1,0:T(8,128)} %refs_2_.3) | copy-start | bytes 12582916
  58.1 6.3 %copy-start.3 = (f32[4,16,128,128]{3,2,1,0:T(8,128)S(1)}, f32[4,16,128,128]{3,2,1,0:T(8,128)}, u32[]{:S(2)}) copy-start(f32[4,16,128,128]{3,2,1,0:T(8,128)} %refs_2_.3) | copy-start | bytes 12582916
  59.1 46.2 %collective-permute-start.16 = (f32[16,64,128]{2,1,0:T(8,128)S(1)}, f32[16,64,128]{2,1,0:T(8,128)S(1)}, u32[]{:S(2)}, u32[]{:S(2)}) collective-permute-start(f32[16,64,128]{2,1,0:T(8,128)S(1)} %shard_map.42.refs_0_.refs_8_), channel_id=1, source_target_pairs={{0,32},{32,0},{1,33},{33,1},{2,34},{34,2},{3,35},{35,3},{4,36},{36... | collective-permute-start | bytes 1572872 | tf_op jit(solution)/shard_map/ppermute | solution.py:299
  67.8 19.4 %collective-permute-start.7 = (f32[3,128,128]{2,1,0:T(8,128)S(1)}, f32[3,128,128]{2,1,0:T(8,128)S(1)}, u32[]{:S(2)}, u32[]{:S(2)}) collective-permute-start(f32[3,128,128]{2,1,0:T(8,128)S(1)} %get-tuple-element.40), channel_id=1, source_target_pairs={{0,8},{16,24},{8,0},{24,16},{1,9},{17,25},{9,1},{25,17},{2,10},{18... | collective-permute-start | bytes 589832 | tf_op jit(solution)/shard_map/ppermute | solution.py:299
  67.9 19.3 %collective-permute-start.8 = (f32[3,128,128]{2,1,0:T(8,128)S(1)}, f32[3,128,128]{2,1,0:T(8,128)S(1)}, u32[]{:S(2)}, u32[]{:S(2)}) collective-permute-start(f32[3,128,128]{2,1,0:T(8,128)S(1)} %get-tuple-element.41), channel_id=1, source_target_pairs={{8,16},{16,8},{9,17},{17,9},{10,18},{18,10},{11,19},{19,11},{12,20... | collective-permute-start | bytes 589832 | tf_op jit(solution)/shard_map/ppermute | solution.py:299
  68.6 13.4 %collective-permute-start.9 = (f32[3,16,128]{2,1,0:T(8,128)S(1)}, f32[3,16,128]{2,1,0:T(8,128)S(1)}, u32[]{:S(2)}, u32[]{:S(2)}) collective-permute-start(f32[3,16,128]{2,1,0:T(8,128)S(1)} %get-tuple-element.42), channel_id=1, source_target_pairs={{0,1},{2,3},{4,5},{6,7},{1,0},{3,2},{5,4},{7,6},{8,9},{10,11},{12,... | collective-permute-start | bytes 73736 | tf_op jit(solution)/shard_map/ppermute | solution.py:299
  77.3 9.9 %collective-permute-start.10 = (f32[3,16,128]{2,1,0:T(8,128)S(1)}, f32[3,16,128]{2,1,0:T(8,128)S(1)}, u32[]{:S(2)}, u32[]{:S(2)}) collective-permute-start(f32[3,16,128]{2,1,0:T(8,128)S(1)} %get-tuple-element.43), channel_id=1, source_target_pairs={{1,2},{3,4},{5,6},{2,1},{4,3},{6,5},{9,10},{11,12},{13,14},{10,9},... | collective-permute-start | bytes 73736 | tf_op jit(solution)/shard_map/ppermute | solution.py:299
  82.0 27.9 %collective-permute-start.5 = (f32[16,64,128]{2,1,0:T(8,128)S(1)}, f32[16,64,128]{2,1,0:T(8,128)S(1)}, u32[]{:S(2)}, u32[]{:S(2)}) collective-permute-start(f32[16,64,128]{2,1,0:T(8,128)S(1)} %shard_map.41.refs_1_.refs_0_.refs_8_), channel_id=1, source_target_pairs={{0,32},{32,0},{1,33},{33,1},{2,34},{34,2},{3,35},{35,3},{4,36},{36... | collective-permute-start | bytes 1572872 | tf_op jit(solution)/shard_map/ppermute | solution.py:299
  90.6 14.6 %collective-permute-start.11 = (f32[4,128,128]{2,1,0:T(8,128)S(1)}, f32[4,128,128]{2,1,0:T(8,128)S(1)}, u32[]{:S(2)}, u32[]{:S(2)}) collective-permute-start(f32[4,128,128]{2,1,0:T(8,128)S(1)} %get-tuple-element.44), channel_id=1, source_target_pairs={{0,8},{16,24},{8,0},{24,16},{1,9},{17,25},{9,1},{25,17},{2,10},{18... | collective-permute-start | bytes 786440 | tf_op jit(solution)/shard_map/ppermute | solution.py:299
  90.7 14.5 %collective-permute-start.12 = (f32[4,128,128]{2,1,0:T(8,128)S(1)}, f32[4,128,128]{2,1,0:T(8,128)S(1)}, u32[]{:S(2)}, u32[]{:S(2)}) collective-permute-start(f32[4,128,128]{2,1,0:T(8,128)S(1)} %get-tuple-element.45), channel_id=1, source_target_pairs={{8,16},{16,8},{9,17},{17,9},{10,18},{18,10},{11,19},{19,11},{12,20... | collective-permute-start | bytes 786440 | tf_op jit(solution)/shard_map/ppermute | solution.py:299
  91.4 6.8 %collective-permute-start.13 = (f32[4,16,128]{2,1,0:T(8,128)S(1)}, f32[4,16,128]{2,1,0:T(8,128)S(1)}, u32[]{:S(2)}, u32[]{:S(2)}) collective-permute-start(f32[4,16,128]{2,1,0:T(8,128)S(1)} %get-tuple-element.46), channel_id=1, source_target_pairs={{0,1},{2,3},{4,5},{6,7},{1,0},{3,2},{5,4},{7,6},{8,9},{10,11},{12,... | collective-permute-start | bytes 98312 | tf_op jit(solution)/shard_map/ppermute | solution.py:299
  98.2 7.0 %collective-permute-start.14 = (f32[4,16,128]{2,1,0:T(8,128)S(1)}, f32[4,16,128]{2,1,0:T(8,128)S(1)}, u32[]{:S(2)}, u32[]{:S(2)}) collective-permute-start(f32[4,16,128]{2,1,0:T(8,128)S(1)} %get-tuple-element.47), channel_id=1, source_target_pairs={{1,2},{3,4},{5,6},{2,1},{4,3},{6,5},{9,10},{11,12},{13,14},{10,9},... | collective-permute-start | bytes 98312 | tf_op jit(solution)/shard_map/ppermute | solution.py:299
  106.2 45.5 %collective-permute-start.22 = (f32[16,64,128]{2,1,0:T(8,128)S(1)}, f32[16,64,128]{2,1,0:T(8,128)S(1)}, u32[]{:S(2)}, u32[]{:S(2)}) collective-permute-start(f32[16,64,128]{2,1,0:T(8,128)S(1)} %shard_map.44.refs_0_.refs_8_), channel_id=1, source_target_pairs={{0,32},{32,0},{1,33},{33,1},{2,34},{34,2},{3,35},{35,3},{4,36},{36... | collective-permute-start | bytes 1572872 | tf_op jit(solution)/shard_map/ppermute | solution.py:299
  114.3 37.4 %collective-permute-start.17 = (f32[4,128,128]{2,1,0:T(8,128)S(1)}, f32[4,128,128]{2,1,0:T(8,128)S(1)}, u32[]{:S(2)}, u32[]{:S(2)}) collective-permute-start(f32[4,128,128]{2,1,0:T(8,128)S(1)} %get-tuple-element.48), channel_id=1, source_target_pairs={{0,8},{16,24},{8,0},{24,16},{1,9},{17,25},{9,1},{25,17},{2,10},{18... | collective-permute-start | bytes 786440 | tf_op jit(solution)/shard_map/ppermute | solution.py:299
  118.6 33.2 %collective-permute-start.18 = (f32[4,128,128]{2,1,0:T(8,128)S(1)}, f32[4,128,128]{2,1,0:T(8,128)S(1)}, u32[]{:S(2)}, u32[]{:S(2)}) collective-permute-start(f32[4,128,128]{2,1,0:T(8,128)S(1)} %get-tuple-element.49), channel_id=1, source_target_pairs={{8,16},{16,8},{9,17},{17,9},{10,18},{18,10},{11,19},{19,11},{12,20... | collective-permute-start | bytes 786440 | tf_op jit(solution)/shard_map/ppermute | solution.py:299
  119.2 44.5 %collective-permute-start.15 = (f32[16,64,128]{2,1,0:T(8,128)S(1)}, f32[16,64,128]{2,1,0:T(8,128)S(1)}, u32[]{:S(2)}, u32[]{:S(2)}) collective-permute-start(f32[16,64,128]{2,1,0:T(8,128)S(1)} %shard_map.43.refs_1_.refs_0_.refs_8_), channel_id=1, source_target_pairs={{0,32},{32,0},{1,33},{33,1},{2,34},{34,2},{3,35},{35,3},{4,36},{36... | collective-permute-start | bytes 1572872 | tf_op jit(solution)/shard_map/ppermute | solution.py:299
  121.4 23.7 %collective-permute-start.19 = (f32[4,16,128]{2,1,0:T(8,128)S(1)}, f32[4,16,128]{2,1,0:T(8,128)S(1)}, u32[]{:S(2)}, u32[]{:S(2)}) collective-permute-start(f32[4,16,128]{2,1,0:T(8,128)S(1)} %get-tuple-element.50), channel_id=1, source_target_pairs={{0,1},{2,3},{4,5},{6,7},{1,0},{3,2},{5,4},{7,6},{8,9},{10,11},{12,... | collective-permute-start | bytes 98312 | tf_op jit(solution)/shard_map/ppermute | solution.py:299
  145.1 6.7 %collective-permute-start.20 = (f32[4,16,128]{2,1,0:T(8,128)S(1)}, f32[4,16,128]{2,1,0:T(8,128)S(1)}, u32[]{:S(2)}, u32[]{:S(2)}) collective-permute-start(f32[4,16,128]{2,1,0:T(8,128)S(1)} %get-tuple-element.51), channel_id=1, source_target_pairs={{1,2},{3,4},{5,6},{2,1},{4,3},{6,5},{9,10},{11,12},{13,14},{10,9},... | collective-permute-start | bytes 98312 | tf_op jit(solution)/shard_map/ppermute | solution.py:299
  152.8 28.5 %collective-permute-start.29 = (f32[16,64,128]{2,1,0:T(8,128)S(1)}, f32[16,64,128]{2,1,0:T(8,128)S(1)}, u32[]{:S(2)}, u32[]{:S(2)}) collective-permute-start(f32[16,64,128]{2,1,0:T(8,128)S(1)} %shard_map.46.refs_0_.refs_8_), channel_id=1, source_target_pairs={{0,32},{32,0},{1,33},{33,1},{2,34},{34,2},{3,35},{35,3},{4,36},{36... | collective-permute-start | bytes 1572872 | tf_op jit(solution)/shard_map/ppermute | solution.py:299
  157.1 31.9 %collective-permute-start.32 = (f32[2,256,128]{2,1,0:T(8,128)S(1)}, f32[2,256,128]{2,1,0:T(8,128)S(1)}, u32[]{:S(2)}, u32[]{:S(2)}) collective-permute-start(f32[2,256,128]{2,1,0:T(8,128)S(1)} %get-tuple-element.64), channel_id=1, source_target_pairs={{0,8},{16,24},{8,0},{24,16},{1,9},{17,25},{9,1},{25,17},{2,10},{18... | collective-permute-start | bytes 786440 | tf_op jit(solution)/shard_map/ppermute | solution.py:299
  165.3 14.2 %collective-permute-start.25 = (f32[1,16,128]{2,1,0:T(8,128)S(1)}, f32[1,16,128]{2,1,0:T(8,128)S(1)}, u32[]{:S(2)}, u32[]{:S(2)}) collective-permute-start(f32[1,16,128]{2,1,0:T(8,128)S(1)} %get-tuple-element.54), channel_id=1, source_target_pairs={{0,1},{2,3},{4,5},{6,7},{1,0},{3,2},{5,4},{7,6},{8,9},{10,11},{12,... | collective-permute-start | bytes 24584 | tf_op jit(solution)/shard_map/ppermute | solution.py:299
  169.9 10.4 %collective-permute-start.26 = (f32[1,16,128]{2,1,0:T(8,128)S(1)}, f32[1,16,128]{2,1,0:T(8,128)S(1)}, u32[]{:S(2)}, u32[]{:S(2)}) collective-permute-start(f32[1,16,128]{2,1,0:T(8,128)S(1)} %get-tuple-element.55), channel_id=1, source_target_pairs={{1,2},{3,4},{5,6},{2,1},{4,3},{6,5},{9,10},{11,12},{13,14},{10,9},... | collective-permute-start | bytes 24584 | tf_op jit(solution)/shard_map/ppermute | solution.py:299
  174.5 19.5 %collective-permute-start.21 = (f32[16,64,128]{2,1,0:T(8,128)S(1)}, f32[16,64,128]{2,1,0:T(8,128)S(1)}, u32[]{:S(2)}, u32[]{:S(2)}) collective-permute-start(f32[16,64,128]{2,1,0:T(8,128)S(1)} %shard_map.45.refs_1_.refs_0_.refs_8_), channel_id=1, source_target_pairs={{0,32},{32,0},{1,33},{33,1},{2,34},{34,2},{3,35},{35,3},{4,36},{36... | collective-permute-start | bytes 1572872 | tf_op jit(solution)/shard_map/ppermute | solution.py:299
  179.5 1.8 collective-permute-start.23
  180.4 0.9 collective-permute-start.24
  182.5 12.8 %collective-permute-start.30 = (f32[2,192,128]{2,1,0:T(8,128)S(1)}, f32[2,192,128]{2,1,0:T(8,128)S(1)}, u32[]{:S(2)}, u32[]{:S(2)}) collective-permute-start(f32[2,192,128]{2,1,0:T(8,128)S(1)} %constant_dynamic-update-slice_fusion), channel_id=1, source_target_pairs={{0,8},{16,24},{8,0},{24,16},{1,9},{17,25},{9,1},{25,17},{2,10},{18... | collective-permute-start | bytes 589832 | tf_op jit(solution)/shard_map/ppermute | solution.py:299
  189.1 10.0 %collective-permute-start.33 = (f32[2,256,128]{2,1,0:T(8,128)S(1)}, f32[2,256,128]{2,1,0:T(8,128)S(1)}, u32[]{:S(2)}, u32[]{:S(2)}) collective-permute-start(f32[2,256,128]{2,1,0:T(8,128)S(1)} %pad_maximum_fusion.refs_1_), channel_id=1, source_target_pairs={{0,16},{8,24},{16,0},{24,8},{1,17},{9,25},{17,1},{25,9},{2,18},{10... | collective-permute-start | bytes 786440 | tf_op jit(solution)/shard_map/ppermute | solution.py:299
  195.1 1.3 collective-permute-start.27
  195.3 9.4 %collective-permute-start.31 = (f32[2,192,128]{2,1,0:T(8,128)S(1)}, f32[2,192,128]{2,1,0:T(8,128)S(1)}, u32[]{:S(2)}, u32[]{:S(2)}) collective-permute-start(f32[2,192,128]{2,1,0:T(8,128)S(1)} %pad_maximum_fusion.1.refs_2_), channel_id=1, source_target_pairs={{0,16},{8,24},{16,0},{24,8},{1,17},{9,25},{17,1},{25,9},{2,18},{10... | collective-permute-start | bytes 589832 | tf_op jit(solution)/shard_map/ppermute | solution.py:299
  196.5 10.2 %collective-permute-start.28 = (f32[2,64,128]{2,1,0:T(8,128)S(1)}, f32[2,64,128]{2,1,0:T(8,128)S(1)}, u32[]{:S(2)}, u32[]{:S(2)}) collective-permute-start(f32[2,64,128]{2,1,0:T(8,128)S(1)} %pad_maximum_fusion.2.refs_1_), channel_id=1, source_target_pairs={{0,16},{8,24},{16,0},{24,8},{1,17},{9,25},{17,1},{25,9},{2,18},{10... | collective-permute-start | bytes 196616 | tf_op jit(solution)/shard_map/ppermute | solution.py:299

commit v5 on v4

--- a/solution.py
+++ b/solution.py
@@ -36,8 +36,8 @@
     return visit(n - 1, n - 2, None, carry)
 
 
-def line_sums(column, n):
-    mean = lax.fori_loop(1, n, lambda x, s: s + column(x), column(0)) / n
+def line_sums(total, column, n):
+    mean = total / n
 
     def add(x, s):
         d = column(x) - mean
@@ -125,15 +125,16 @@
         low_z = jnp.where(even_z, b, a) if low_open else below[x, below.shape[1] - 1 :, :]
         high_z = jnp.where(even_z, a, b) if high_open else above[x, 0:1, :]
         near, far = received[x], field[second, x, begin:end]
-        out[x] = cells(
+        value = cells(
             centre[x], low_x, high_x, near, far, low_z, high_z, crowding[here, x, begin:end]
         )
-        return carry
+        out[x] = value
+        return carry + value if final else carry
 
     out = refs[0]
-    over_x(n, visit)
+    total = over_x(n, visit, jnp.zeros(centre.shape[1:], jnp.float32) if final else 0)
     if final:
-        refs[1][0], refs[1][1] = line_sums(lambda x: out[x], n)
+        refs[1][0], refs[1][1] = line_sums(total, lambda x: out[x], n)
 
 
 def row_step(info, p, parts, received, cuts, field, crowding, ghosts, mapped, final):
@@ -155,14 +156,12 @@
     )(info, *args)
 
 
-def rest_kernel(count, mapped, rows, ghost_from, final, info, *refs):
+def rest_kernel(count, mapped, rows, ghost_from, final, place, info, *refs):
     first, refs = refs[:count], refs[count:]
     field, crowding, lon_a, lon_b, lev_a, lev_b = refs[:6]
     refs = refs[6:]
-    if final:
-        out, sums, ended, sem = refs[-4:]
-    else:
-        out = refs[-1]
+    out, refs = refs[0], refs[1:]
+    sums, refs = (refs[0], refs[1:]) if final else (None, refs)
     n, length = field.shape[1], field.shape[2]
     copies = []
     for k, row in enumerate(rows):
@@ -182,49 +181,46 @@
                 near = jnp.concatenate([part[x] for part in first], axis=0)
             far = 0.0 if row == 2 else field[beyond, x]
             low_z, high_z = ends_z(x)
-            out[k, x] = cells(
+            value = cells(
                 field[at, x], low_x, high_x, near, far, low_z, high_z, crowding[crowd_at, x]
             )
-            return carry
-
-        over_x(n, visit)
-        if final:
+            out[k, x] = value
+            return carry + value if final else carry
+
+        total = over_x(n, visit, jnp.zeros(field.shape[2:], jnp.float32) if final else 0)
+        if place:
+            ended, sem = refs
             copies.append(pltpu.make_async_copy(out.at[k], ended.at[info[row + 1]], sem.at[k]))
             copies[-1].start()
+        if final:
             there = slice(k * length, (k + 1) * length)
-            sums[0, there], sums[1, there] = line_sums(lambda x: out[k, x], n)
+            sums[0, there], sums[1, there] = line_sums(total, lambda x: out[k, x], n)
     for copy in copies:
         copy.wait()
 
 
-def rest_step(info, first, field, crowding, ghosts, mapped, rows=(0, 1, 2), ghost_from=-1, final=False, ended=None):
+def rest_step(info, first, field, crowding, ghosts, mapped, rows=(0, 1, 2), ghost_from=-1, final=False, place=False):
     _, n, length, species = field.shape
     count = len(rows)
     out_shape = [jax.ShapeDtypeStruct((count, n, length, species), jnp.float32)]
-    out_specs, scratch, more = [VMEM], [], {}
+    out_specs, scratch = [VMEM], []
     args = [*first, field, crowding, *ghosts]
-    in_specs = [SMEM] + [VMEM] * len(args)
     if final:
-        out_shape += [
-            jax.ShapeDtypeStruct((2, count * length, species), jnp.float32),
-            jax.ShapeDtypeStruct((4, n, length, species), jnp.float32),
-        ]
-        out_specs += [VMEM, ANY]
+        out_shape.append(jax.ShapeDtypeStruct((2, count * length, species), jnp.float32))
+        out_specs.append(VMEM)
+    if place:
+        out_shape.append(jax.ShapeDtypeStruct((4, n, length, species), jnp.float32))
+        out_specs.append(ANY)
         scratch = [pltpu.SemaphoreType.DMA((count,))]
-        if ended is not None:
-            args.append(ended)
-            in_specs.append(ANY)
-            more = {"input_output_aliases": {len(args): 2}}
     return pl.pallas_call(
-        functools.partial(rest_kernel, len(first), mapped, rows, ghost_from, final),
+        functools.partial(rest_kernel, len(first), mapped, rows, ghost_from, final, place),
         out_shape=out_shape,
-        in_specs=in_specs,
+        in_specs=[SMEM] + [VMEM] * len(args),
         out_specs=out_specs,
         scratch_shapes=scratch,
         compiler_params=pltpu.CompilerParams(vmem_limit_bytes=24 * MIB),
         cost_estimate=cost(count * n * length * species, 20, 4),
         name="rest",
-        **more,
     )(info, *args)
 
 
@@ -239,17 +235,18 @@
     return 0.5 * (a[0] + b[0]), lax.rsqrt(variance + 0.0001)
 
 
-def scale_kernel(rows, begins, info, *refs):
+def scale_kernel(rows, begins, places, info, *refs):
     count = len(begins)
-    fields, (one, two) = refs[:count], refs[count : count + 2]
+    fields, (one, two), refs = refs[:count], refs[count : count + 2], refs[count + 2 :]
+    placed, refs = refs[: len(places)], refs[len(places) :]
     scaled, ended, buffers, sem = refs[-3 - count], refs[-2 - count], refs[-1 - count : -1], refs[-1]
     n = buffers[0].shape[-3]
     jobs = []
     for field, buffer, begin in zip(fields, buffers, begins):
         if begin is None:
-            jobs += [(field.at[k], buffer.at[k], info[row], 0, False) for k, row in enumerate(rows)]
+            jobs += [(field.at[k], buffer.at[k], info[row], 0) for k, row in enumerate(rows)]
         else:
-            jobs.append((field, buffer, info[0], begin, True))
+            jobs.append((field, buffer, info[0], begin))
     copies, line = [], 0
 
     def copy(source, target, row, begin):
@@ -257,10 +254,9 @@
         copies.append(pltpu.make_async_copy(source, there, sem.at[len(copies)]))
         copies[-1].start()
 
-    for field, _, row, begin, place in jobs:
-        if place:
-            copy(field, ended, row, begin)
-    for field, buffer, row, begin, _ in jobs:
+    for source, (row, begin) in zip(placed, places):
+        copy(source if row == 0 else source.at[0], ended, info[row], begin)
+    for field, buffer, row, begin in jobs:
         lines = slice(line, line + field.shape[1])
         line += field.shape[1]
         mean, factor = line_factors(*([s[0, lines], s[1, lines]] for s in (one, two)), 2 * n)
@@ -275,14 +271,14 @@
         c.wait()
 
 
-def scale(info, fields, rows, begins, one, two, ended, scaled=None):
+def scale(info, fields, rows, begins, one, two, placed, places, ended, scaled=None):
     extra = [ended] if scaled is None else [ended, scaled]
-    at = 3 + len(fields)
+    at = 3 + len(fields) + len(placed)
     size = sum(field.size for field in fields)
     return pl.pallas_call(
-        functools.partial(scale_kernel, rows, begins),
+        functools.partial(scale_kernel, rows, begins, places),
         out_shape=[jax.ShapeDtypeStruct(ended.shape, jnp.float32)] * 2,
-        in_specs=[SMEM] + [VMEM] * (len(fields) + 2) + [ANY] * len(extra),
+        in_specs=[SMEM] + [VMEM] * (len(fields) + 2 + len(placed)) + [ANY] * len(extra),
         out_specs=[ANY, ANY],
         scratch_shapes=[
             *(pltpu.VMEM(field.shape, jnp.float32) for field in fields),
@@ -292,7 +288,7 @@
         compiler_params=pltpu.CompilerParams(vmem_limit_bytes=16 * MIB),
         cost_estimate=cost(size, 3, 2),
         name="scale",
-    )(info, *fields, one, two, *extra)
+    )(info, *fields, one, two, *placed, *extra)
 
 
 def paired(array, axis, pairs):
@@ -343,8 +339,8 @@
         if final:
             sent = edges(info, parts, None)
             row_ghosts = exchanged(sent)
-            beside, beside_sums, ended = rest_step(
-                info, parts, field, crowding, ghosts, False, (0,), ghost_from, True, ended
+            beside, beside_sums = rest_step(
+                info, parts, field, crowding, ghosts, False, (0,), ghost_from, True
             )
         elif not start:
             (ahead,) = rest_step(info, parts, field, crowding, ghosts, False, ghost_from=ghost_from)
@@ -353,7 +349,7 @@
             ghost_from = -1
         if step == last_step - 1:
             deep, deep_sums, ended = rest_step(
-                info, [], ahead, crowding, ghosts, False, (1, 2), ghost_from, True
+                info, [], ahead, crowding, ghosts, False, (1, 2), ghost_from, True, True
             )
         new = []
         for p in range(len(parts)):
@@ -365,11 +361,21 @@
             arriving = swapped(parts)
     first, first_sums, last, last_sums = new
     lines = halves_of_lines(deep_sums, n)
-    scaled, ended = scale(info, [deep], (2, 3), [None], *lines, ended)
+    scaled, ended = scale(info, [deep], (2, 3), [None], *lines, [], [], ended)
     lines = halves_of_lines(jnp.concatenate([beside_sums, first_sums], axis=1), n)
-    scaled, ended = scale(info, [beside, first], (1,), [None, 0], *lines, ended, scaled)
+    scaled, ended = scale(
+        info,
+        [beside, first],
+        (1,),
+        [None, 0],
+        *lines,
+        [beside, first, last],
+        [(1, 0), (0, 0), (0, cuts[1])],
+        ended,
+        scaled,
+    )
     lines = halves_of_lines(last_sums, n)
-    scaled, ended = scale(info, [last], (), [cuts[1]], *lines, ended, scaled)
+    scaled, ended = scale(info, [last], (), [cuts[1]], *lines, [], [], ended, scaled)
     return scaled, ended
 
 

time: 209 us -> 209 us (level)
  no operation moved by 1% of the time
where the time goes in v5:
time: 209 us
  starting transfers between devices  98.9 us (47%)
  waiting for transfers between devices  72.5 us (35%)
  Pallas kernels  30.5 us (15%)
  local copies, waits for them, and re-layouts  5.77 us (3%)
    ppermute x34, starting transfers between devices, paired(): return lax.ppermute(array, axis, [*pairs, *((b, a) for a, b in pairs)])  98.9 us
    ppermute x34, waiting for transfers between devices, paired(): return lax.ppermute(array, axis, [*pairs, *((b, a) for a, b in pairs)])  72.5 us
    pallas_call x5, Pallas kernels, rest_step(): pl.pallas_call(functools.partial(rest_kernel, len(first), mapped, rows, g...  13.1 us
    pallas_call x8, Pallas kernels, row_step(): pl.pallas_call(functools.partial(row_kernel, cuts[p], mapped, low_open, h...  8.15 us
    pallas_call x3, Pallas kernels, scale(): pl.pallas_call(functools.partial(scale_kernel, rows, begins, places), out...  6.08 us
    unnamed x9, local copies, waits for them, and re-layouts  4.4 us
  transfers between devices with their start and end apart: 34, of which 13 were waited for; matrix products, arithmetic and copies ran while one was open for 0% of the time, Pallas kernels for 14%

profile of v5, /device:TPU:88, one launch (start us, length us, event | category | flops | bytes accessed | tf_op | source)
XLA Modules:
  0.0 208.8 jit_solution(6847801762385224943)
XLA Ops:
  0.6 1.3 dynamic-slice_bitcast_fusion
  1.9 5.5 %collective-permute-start.6 = (f32[16,64,128]{2,1,0:T(8,128)S(1)}, f32[16,64,128]{2,1,0:T(8,128)S(1)}, u32[]{:S(2)}, u32[]{:S(2)}) collective-permute-start(f32[16,64,128]{2,1,0:T(8,128)S(1)} %get-tuple-element.68.refs_8_.refs_0_), channel_id=1, source_target_pairs={{0,32},{32,0},{1,33},{33,1},{2,34},{34,2},{3,35},{35,3},{4,36},{36... | collective-permute-start | bytes 1572872 | tf_op jit(solution)/shard_map/ppermute | solution.py:295
  8.0 2.2 %copy-done.1 = f32[4,16,128,128]{3,2,1,0:T(8,128)S(1)} copy-done((f32[4,16,128,128]{3,2,1,0:T(8,128)S(1)}, f32[4,16,128,128]{3,2,1,0:T(8,128)}, u32[]{:S(2)}) %copy-start.1) | copy-done | bytes 4194328
  10.2 0.6 edges.5
  11.0 0.8 collective-permute-start.2
  11.8 1.6 collective-permute-start.3
  13.4 2.4 %collective-permute-done.3.refs_6_.refs_4_ = f32[4,16,128]{2,1,0:T(8,128)S(1)} collective-permute-done((f32[4,16,128]{2,1,0:T(8,128)S(1)}, f32[4,16,128]{2,1,0:T(8,128)S(1)}, u32[]{:S(2)}, u32[]{:S(2)}) %collective-permute-start.3) | collective-permute-done | bytes 32800 | tf_op jit(solution)/shard_map/ppermute | solution.py:295
  15.8 3.6 %collective-permute-start.4 = (f32[4,16,128]{2,1,0:T(8,128)S(1)}, f32[4,16,128]{2,1,0:T(8,128)S(1)}, u32[]{:S(2)}, u32[]{:S(2)}) collective-permute-start(f32[4,16,128]{2,1,0:T(8,128)S(1)} %get-tuple-element.38), channel_id=1, source_target_pairs={{1,2},{3,4},{5,6},{2,1},{4,3},{6,5},{9,10},{11,12},{13,14},{10,9},... | collective-permute-start | bytes 98312 | tf_op jit(solution)/shard_map/ppermute | solution.py:295
  19.4 3.1 %collective-permute-done.4.refs_7_.refs_5_ = f32[4,16,128]{2,1,0:T(8,128)S(1)} collective-permute-done((f32[4,16,128]{2,1,0:T(8,128)S(1)}, f32[4,16,128]{2,1,0:T(8,128)S(1)}, u32[]{:S(2)}, u32[]{:S(2)}) %collective-permute-start.4) | collective-permute-done | bytes 32800 | tf_op jit(solution)/shard_map/ppermute | solution.py:295
  22.5 33.4 %collective-permute-done.6.refs_1_ = f32[16,64,128]{2,1,0:T(8,128)S(1)} collective-permute-done((f32[16,64,128]{2,1,0:T(8,128)S(1)}, f32[16,64,128]{2,1,0:T(8,128)S(1)}, u32[]{:S(2)}, u32[]{:S(2)}) %collective-permute-start.6) | collective-permute-done | bytes 524320 | tf_op jit(solution)/shard_map/ppermute | solution.py:295
  55.9 2.2 %copy-done.2 = f32[4,16,128,128]{3,2,1,0:T(8,128)S(1)} copy-done((f32[4,16,128,128]{3,2,1,0:T(8,128)S(1)}, f32[4,16,128,128]{3,2,1,0:T(8,128)}, u32[]{:S(2)}) %copy-start.2) | copy-done | bytes 4194328
  58.1 1.0 shard_map.42.refs_0_.refs_8_
  59.1 5.3 %collective-permute-start.16 = (f32[16,64,128]{2,1,0:T(8,128)S(1)}, f32[16,64,128]{2,1,0:T(8,128)S(1)}, u32[]{:S(2)}, u32[]{:S(2)}) collective-permute-start(f32[16,64,128]{2,1,0:T(8,128)S(1)} %shard_map.42.refs_0_.refs_8_), channel_id=1, source_target_pairs={{0,32},{32,0},{1,33},{33,1},{2,34},{34,2},{3,35},{35,3},{4,36},{36... | collective-permute-start | bytes 1572872 | tf_op jit(solution)/shard_map/ppermute | solution.py:295
  64.4 2.8 %rest.5.refs_0_.refs_2_ = f32[3,16,128,128]{3,2,1,0:T(8,128)S(1)} custom-call(s32[6]{0:T(128)S(1)} %stack.42.info, f32[4,16,128,128]{3,2,1,0:T(8,128)S(1)} %copy-done.3, f32[4,16,128,128]{3,2,1,0:T(8,128)S(1)} %copy-done, f32[4,128,128]{2,1,0:T(8,128)S(1)} %collective-permute-done.1.refs_4_.refs_2_, ...), custom_call_target="tpu_custom_call" | custom-call | flops 15728640 | bytes 12582912 | tf_op jit(solution)/shard_map/rest/pallas_call | solution.py:215
  67.2 0.6 edges.6
  67.9 0.7 collective-permute-start.8
  68.6 1.6 collective-permute-start.9
  70.2 7.2 %collective-permute-done.refs_1_ = f32[16,64,128]{2,1,0:T(8,128)S(1)} collective-permute-done((f32[16,64,128]{2,1,0:T(8,128)S(1)}, f32[16,64,128]{2,1,0:T(8,128)S(1)}, u32[]{:S(2)}, u32[]{:S(2)}) %collective-permute-start) | collective-permute-done | bytes 524320 | tf_op jit(solution)/shard_map/ppermute | solution.py:295
  77.3 3.7 %collective-permute-start.10 = (f32[3,16,128]{2,1,0:T(8,128)S(1)}, f32[3,16,128]{2,1,0:T(8,128)S(1)}, u32[]{:S(2)}, u32[]{:S(2)}) collective-permute-start(f32[3,16,128]{2,1,0:T(8,128)S(1)} %get-tuple-element.42), channel_id=1, source_target_pairs={{1,2},{3,4},{5,6},{2,1},{4,3},{6,5},{9,10},{11,12},{13,14},{10,9},... | collective-permute-start | bytes 73736 | tf_op jit(solution)/shard_map/ppermute | solution.py:295
  81.0 1.0 shard_map.41.refs_1_.refs_0_.refs_8_
  82.0 5.2 %collective-permute-start.5 = (f32[16,64,128]{2,1,0:T(8,128)S(1)}, f32[16,64,128]{2,1,0:T(8,128)S(1)}, u32[]{:S(2)}, u32[]{:S(2)}) collective-permute-start(f32[16,64,128]{2,1,0:T(8,128)S(1)} %shard_map.41.refs_1_.refs_0_.refs_8_), channel_id=1, source_target_pairs={{0,32},{32,0},{1,33},{33,1},{2,34},{34,2},{3,35},{35,3},{4,36},{36... | collective-permute-start | bytes 1572872 | tf_op jit(solution)/shard_map/ppermute | solution.py:295
  87.2 2.7 %rest.6.refs_2_ = f32[3,16,128,128]{3,2,1,0:T(8,128)S(1)} custom-call(s32[6]{0:T(128)S(1)} %stack.42.info, f32[16,64,128]{2,1,0:T(8,128)S(1)} %shard_map.42.refs_0_.refs_8_, f32[16,64,128]{2,1,0:T(8,128)S(1)} %shard_map.41.refs_1_.refs_0_.refs_8_, f32[3,16,128,128]{3,2,1,0:T(8,128)S(1)} %rest.5.refs_0_.refs_2_, f32[4,16,128,128]{3,2,1,0:T(8,128)S(1)} %copy-done, ...), custom_call_target="tpu_custom_call" | custom-call | flops 15728640 | bytes 12582912 | tf_op jit(solution)/shard_map/rest/pallas_call | solution.py:215
  90.0 0.6 edges.7
  90.7 0.7 collective-permute-start.12
  91.4 4.9 %collective-permute-start.13 = (f32[4,16,128]{2,1,0:T(8,128)S(1)}, f32[4,16,128]{2,1,0:T(8,128)S(1)}, u32[]{:S(2)}, u32[]{:S(2)}) collective-permute-start(f32[4,16,128]{2,1,0:T(8,128)S(1)} %get-tuple-element.45), channel_id=1, source_target_pairs={{0,1},{2,3},{4,5},{6,7},{1,0},{3,2},{5,4},{7,6},{8,9},{10,11},{12,... | collective-permute-start | bytes 98312 | tf_op jit(solution)/shard_map/ppermute | solution.py:295
  96.3 1.9 collective-permute-done.13.refs_6_
  98.2 1.9 collective-permute-start.14
  100.1 5.1 %collective-permute-done.14.refs_7_ = f32[4,16,128]{2,1,0:T(8,128)S(1)} collective-permute-done((f32[4,16,128]{2,1,0:T(8,128)S(1)}, f32[4,16,128]{2,1,0:T(8,128)S(1)}, u32[]{:S(2)}, u32[]{:S(2)}) %collective-permute-start.14) | collective-permute-done | bytes 32800 | tf_op jit(solution)/shard_map/ppermute | solution.py:295
  105.2 1.0 shard_map.44.refs_0_.refs_8_
  106.2 3.7 %collective-permute-start.22 = (f32[16,64,128]{2,1,0:T(8,128)S(1)}, f32[16,64,128]{2,1,0:T(8,128)S(1)}, u32[]{:S(2)}, u32[]{:S(2)}) collective-permute-start(f32[16,64,128]{2,1,0:T(8,128)S(1)} %shard_map.44.refs_0_.refs_8_), channel_id=1, source_target_pairs={{0,32},{32,0},{1,33},{33,1},{2,34},{34,2},{3,35},{35,3},{4,36},{36... | collective-permute-start | bytes 1572872 | tf_op jit(solution)/shard_map/ppermute | solution.py:295
  110.0 1.0 shard_map.43.refs_1_.refs_0_.refs_8_
  111.0 2.7 %rest.7.refs_2_.refs_0_ = f32[3,16,128,128]{3,2,1,0:T(8,128)S(1)} custom-call(s32[6]{0:T(128)S(1)} %stack.42.info, f32[16,64,128]{2,1,0:T(8,128)S(1)} %shard_map.44.refs_0_.refs_8_, f32[16,64,128]{2,1,0:T(8,128)S(1)} %shard_map.43.refs_1_.refs_0_.refs_8_, f32[3,16,128,128]{3,2,1,0:T(8,128)S(1)} %rest.6.refs_2_, f32[4,16,128,128]{3,2,1,0:T(8,128)S(1)} %copy-done, ...), custom_call_target="tpu_custom_call" | custom-call | flops 15728640 | bytes 12582912 | tf_op jit(solution)/shard_map/rest/pallas_call | solution.py:215
  113.7 0.6 edges.8
  114.3 4.2 %collective-permute-start.17 = (f32[4,128,128]{2,1,0:T(8,128)S(1)}, f32[4,128,128]{2,1,0:T(8,128)S(1)}, u32[]{:S(2)}, u32[]{:S(2)}) collective-permute-start(f32[4,128,128]{2,1,0:T(8,128)S(1)} %get-tuple-element.47), channel_id=1, source_target_pairs={{0,8},{16,24},{8,0},{24,16},{1,9},{17,25},{9,1},{25,17},{2,10},{18... | collective-permute-start | bytes 786440 | tf_op jit(solution)/shard_map/ppermute | solution.py:295
  118.6 0.7 collective-permute-start.18
  119.2 2.2 %collective-permute-start.15 = (f32[16,64,128]{2,1,0:T(8,128)S(1)}, f32[16,64,128]{2,1,0:T(8,128)S(1)}, u32[]{:S(2)}, u32[]{:S(2)}) collective-permute-start(f32[16,64,128]{2,1,0:T(8,128)S(1)} %shard_map.43.refs_1_.refs_0_.refs_8_), channel_id=1, source_target_pairs={{0,32},{32,0},{1,33},{33,1},{2,34},{34,2},{3,35},{35,3},{4,36},{36... | collective-permute-start | bytes 1572872 | tf_op jit(solution)/shard_map/ppermute | solution.py:295
  121.4 21.4 %collective-permute-start.19 = (f32[4,16,128]{2,1,0:T(8,128)S(1)}, f32[4,16,128]{2,1,0:T(8,128)S(1)}, u32[]{:S(2)}, u32[]{:S(2)}) collective-permute-start(f32[4,16,128]{2,1,0:T(8,128)S(1)} %get-tuple-element.49), channel_id=1, source_target_pairs={{0,1},{2,3},{4,5},{6,7},{1,0},{3,2},{5,4},{7,6},{8,9},{10,11},{12,... | collective-permute-start | bytes 98312 | tf_op jit(solution)/shard_map/ppermute | solution.py:295
  142.8 2.2 %collective-permute-done.19.refs_6_.refs_4_ = f32[4,16,128]{2,1,0:T(8,128)S(1)} collective-permute-done((f32[4,16,128]{2,1,0:T(8,128)S(1)}, f32[4,16,128]{2,1,0:T(8,128)S(1)}, u32[]{:S(2)}, u32[]{:S(2)}) %collective-permute-start.19) | collective-permute-done | bytes 32800 | tf_op jit(solution)/shard_map/ppermute | solution.py:295
  145.1 1.9 collective-permute-start.20
  147.0 4.8 %collective-permute-done.20.refs_7_.refs_5_ = f32[4,16,128]{2,1,0:T(8,128)S(1)} collective-permute-done((f32[4,16,128]{2,1,0:T(8,128)S(1)}, f32[4,16,128]{2,1,0:T(8,128)S(1)}, u32[]{:S(2)}, u32[]{:S(2)}) %collective-permute-start.20) | collective-permute-done | bytes 32800 | tf_op jit(solution)/shard_map/ppermute | solution.py:295
  151.8 1.0 shard_map.46.refs_0_.refs_8_
  152.8 1.1 collective-permute-start.29
  153.8 3.3 %rest.9 = (f32[2,16,128,128]{3,2,1,0:T(8,128)S(1)}, f32[2,256,128]{2,1,0:T(8,128)S(1)}, f32[4,16,128,128]{3,2,1,0:T(8,128)}) custom-call(s32[6]{0:T(128)S(1)} %stack.42.info, f32[3,16,128,128]{3,2,1,0:T(8,128)S(1)} %rest.7.refs_2_.refs_0_, f32[4,16,128,128]{3,2,1,0:T(8,128)S(1)} %copy-done, f32[4,128,128]{2,1,0:T(8,128)S(1)} %collective-permute-done.17.refs_4_.refs_2_, ...), custom_call_target="tpu_custom_call" | custom-call | flops 10485760 | bytes 8388608 | tf_op jit(solution)/shard_map/rest/pallas_call | solution.py:215
  157.2 3.5 %collective-permute-start.32 = (f32[2,256,128]{2,1,0:T(8,128)S(1)}, f32[2,256,128]{2,1,0:T(8,128)S(1)}, u32[]{:S(2)}, u32[]{:S(2)}) collective-permute-start(f32[2,256,128]{2,1,0:T(8,128)S(1)} %get-tuple-element.62), channel_id=1, source_target_pairs={{0,8},{16,24},{8,0},{24,16},{1,9},{17,25},{9,1},{25,17},{2,10},{18... | collective-permute-start | bytes 786440 | tf_op jit(solution)/shard_map/ppermute | solution.py:295
  160.6 3.1 %collective-permute-done.15.refs_1_ = f32[16,64,128]{2,1,0:T(8,128)S(1)} collective-permute-done((f32[16,64,128]{2,1,0:T(8,128)S(1)}, f32[16,64,128]{2,1,0:T(8,128)S(1)}, u32[]{:S(2)}, u32[]{:S(2)}) %collective-permute-start.15) | collective-permute-done | bytes 524320 | tf_op jit(solution)/shard_map/ppermute | solution.py:295
  163.8 1.0 shard_map.45.refs_1_.refs_0_.refs_8_
  164.7 0.6 edges.9
  165.3 4.6 %collective-permute-start.25 = (f32[1,16,128]{2,1,0:T(8,128)S(1)}, f32[1,16,128]{2,1,0:T(8,128)S(1)}, u32[]{:S(2)}, u32[]{:S(2)}) collective-permute-start(f32[1,16,128]{2,1,0:T(8,128)S(1)} %get-tuple-element.53), channel_id=1, source_target_pairs={{0,1},{2,3},{4,5},{6,7},{1,0},{3,2},{5,4},{7,6},{8,9},{10,11},{12,... | collective-permute-start | bytes 24584 | tf_op jit(solution)/shard_map/ppermute | solution.py:295
  169.9 4.5 %collective-permute-start.26 = (f32[1,16,128]{2,1,0:T(8,128)S(1)}, f32[1,16,128]{2,1,0:T(8,128)S(1)}, u32[]{:S(2)}, u32[]{:S(2)}) collective-permute-start(f32[1,16,128]{2,1,0:T(8,128)S(1)} %get-tuple-element.54), channel_id=1, source_target_pairs={{1,2},{3,4},{5,6},{2,1},{4,3},{6,5},{9,10},{11,12},{13,14},{10,9},... | collective-permute-start | bytes 24584 | tf_op jit(solution)/shard_map/ppermute | solution.py:295
  174.5 2.8 %collective-permute-start.21 = (f32[16,64,128]{2,1,0:T(8,128)S(1)}, f32[16,64,128]{2,1,0:T(8,128)S(1)}, u32[]{:S(2)}, u32[]{:S(2)}) collective-permute-start(f32[16,64,128]{2,1,0:T(8,128)S(1)} %shard_map.45.refs_1_.refs_0_.refs_8_), channel_id=1, source_target_pairs={{0,32},{32,0},{1,33},{33,1},{2,34},{34,2},{3,35},{35,3},{4,36},{36... | collective-permute-start | bytes 1572872 | tf_op jit(solution)/shard_map/ppermute | solution.py:295
  177.2 1.6 rest.8
  178.8 0.9 collective-permute-start.23
  179.6 0.7 collective-permute-start.24
  180.6 1.1 shard_map.48
  181.7 6.6 %collective-permute-start.30 = (f32[2,192,128]{2,1,0:T(8,128)S(1)}, f32[2,192,128]{2,1,0:T(8,128)S(1)}, u32[]{:S(2)}, u32[]{:S(2)}) collective-permute-start(f32[2,192,128]{2,1,0:T(8,128)S(1)} %constant_dynamic-update-slice_fusion), channel_id=1, source_target_pairs={{0,8},{16,24},{8,0},{24,16},{1,9},{17,25},{9,1},{25,17},{2,10},{18... | collective-permute-start | bytes 589832 | tf_op jit(solution)/shard_map/ppermute | solution.py:295
  188.4 1.1 collective-permute-start.33
  189.5 4.4 %collective-permute-done.21.refs_1_ = f32[16,64,128]{2,1,0:T(8,128)S(1)} collective-permute-done((f32[16,64,128]{2,1,0:T(8,128)S(1)}, f32[16,64,128]{2,1,0:T(8,128)S(1)}, u32[]{:S(2)}, u32[]{:S(2)}) %collective-permute-start.21) | collective-permute-done | bytes 524320 | tf_op jit(solution)/shard_map/ppermute | solution.py:295
  193.9 1.1 shard_map.47
  195.4 1.0 collective-permute-done.27
  196.4 2.6 %collective-permute-start.28 = (f32[2,64,128]{2,1,0:T(8,128)S(1)}, f32[2,64,128]{2,1,0:T(8,128)S(1)}, u32[]{:S(2)}, u32[]{:S(2)}) collective-permute-start(f32[2,64,128]{2,1,0:T(8,128)S(1)} %pad_maximum_fusion.2.refs_1_), channel_id=1, source_target_pairs={{0,16},{8,24},{16,0},{24,8},{1,17},{9,25},{17,1},{25,9},{2,18},{10... | collective-permute-start | bytes 196616 | tf_op jit(solution)/shard_map/ppermute | solution.py:295
  199.0 2.1 %scale.3 = (f32[4,16,128,128]{3,2,1,0:T(8,128)}, f32[4,16,128,128]{3,2,1,0:T(8,128)}) custom-call(s32[6]{0:T(128)S(1)} %stack.42.info, f32[2,16,128,128]{3,2,1,0:T(8,128)S(1)} %get-tuple-element.61.refs_0_, f32[2,256,128]{2,1,0:T(8,128)S(1)} %pad_maximum_fusion.refs_1_, ...), custom_call_target="tpu_custom_call", output_to_operand_aliasing={{1}: (4, {})} | custom-call | flops 1572864 | bytes 4194304 | tf_op jit(solution)/shard_map/scale/pallas_call | solution.py:278
  201.2 3.5 %collective-permute-done.31.refs_3_ = f32[2,192,128]{2,1,0:T(8,128)S(1)} collective-permute-done((f32[2,192,128]{2,1,0:T(8,128)S(1)}, f32[2,192,128]{2,1,0:T(8,128)S(1)}, u32[]{:S(2)}, u32[]{:S(2)}) %collective-permute-start.31) | collective-permute-done | bytes 196640 | tf_op jit(solution)/shard_map/ppermute | solution.py:295
  204.7 2.4 %scale.4 = (f32[4,16,128,128]{3,2,1,0:T(8,128)}, f32[4,16,128,128]{3,2,1,0:T(8,128)}) custom-call(s32[6]{0:T(128)S(1)} %stack.42.info, f32[1,16,128,128]{3,2,1,0:T(8,128)S(1)} %get-tuple-element.57.refs_0_.refs_4_, f32[16,64,128]{2,1,0:T(8,128)S(1)} %get-tuple-element.58.refs_1_.refs_5_, ...), custom_call_target="tpu_custom_call", output_to_operand_aliasing={{1}: (8, {}), {0}: (9, {})} | custom-call | flops 1179648 | bytes 3145728 | tf_op jit(solution)/shard_map/scale/pallas_call | solution.py:278
  207.1 1.5 scale.5
  (43 shorter events, 1.6 us)
Async XLA Ops:
  1.9 54.0 %collective-permute-start.6 = (f32[16,64,128]{2,1,0:T(8,128)S(1)}, f32[16,64,128]{2,1,0:T(8,128)S(1)}, u32[]{:S(2)}, u32[]{:S(2)}) collective-permute-start(f32[16,64,128]{2,1,0:T(8,128)S(1)} %get-tuple-element.68.refs_8_.refs_0_), channel_id=1, source_target_pairs={{0,32},{32,0},{1,33},{33,1},{2,34},{34,2},{3,35},{35,3},{4,36},{36... | collective-permute-start | bytes 1572872 | tf_op jit(solution)/shard_map/ppermute | solution.py:295
  7.4 69.9 %collective-permute-start = (f32[16,64,128]{2,1,0:T(8,128)S(1)}, f32[16,64,128]{2,1,0:T(8,128)S(1)}, u32[]{:S(2)}, u32[]{:S(2)}) collective-permute-start(f32[16,64,128]{2,1,0:T(8,128)S(1)} %get-tuple-element.69.refs_0_.refs_8_), channel_id=1, source_target_pairs={{0,32},{32,0},{1,33},{33,1},{2,34},{34,2},{3,35},{35,3},{4,36},{36... | collective-permute-start | bytes 1572872 | tf_op jit(solution)/shard_map/ppermute | solution.py:295
  8.0 2.2 %copy-start.1 = (f32[4,16,128,128]{3,2,1,0:T(8,128)S(1)}, f32[4,16,128,128]{3,2,1,0:T(8,128)}, u32[]{:S(2)}) copy-start(f32[4,16,128,128]{3,2,1,0:T(8,128)} %refs_2_.3) | copy-start | bytes 12582916
  10.2 45.7 %copy-start = (f32[4,16,128,128]{3,2,1,0:T(8,128)S(1)}, f32[4,16,128,128]{3,2,1,0:T(8,128)}, u32[]{:S(2)}) copy-start(f32[4,16,128,128]{3,2,1,0:T(8,128)} %refs_1_.3) | copy-start | bytes 12582916
  10.9 11.6 %collective-permute-start.1 = (f32[4,128,128]{2,1,0:T(8,128)S(1)}, f32[4,128,128]{2,1,0:T(8,128)S(1)}, u32[]{:S(2)}, u32[]{:S(2)}) collective-permute-start(f32[4,128,128]{2,1,0:T(8,128)S(1)} %get-tuple-element.35), channel_id=1, source_target_pairs={{0,8},{16,24},{8,0},{24,16},{1,9},{17,25},{9,1},{25,17},{2,10},{18... | collective-permute-start | bytes 786440 | tf_op jit(solution)/shard_map/ppermute | solution.py:295
  11.0 11.5 %collective-permute-start.2 = (f32[4,128,128]{2,1,0:T(8,128)S(1)}, f32[4,128,128]{2,1,0:T(8,128)S(1)}, u32[]{:S(2)}, u32[]{:S(2)}) collective-permute-start(f32[4,128,128]{2,1,0:T(8,128)S(1)} %get-tuple-element.36), channel_id=1, source_target_pairs={{8,16},{16,8},{9,17},{17,9},{10,18},{18,10},{11,19},{19,11},{12,20... | collective-permute-start | bytes 786440 | tf_op jit(solution)/shard_map/ppermute | solution.py:295
  11.8 4.0 %collective-permute-start.3 = (f32[4,16,128]{2,1,0:T(8,128)S(1)}, f32[4,16,128]{2,1,0:T(8,128)S(1)}, u32[]{:S(2)}, u32[]{:S(2)}) collective-permute-start(f32[4,16,128]{2,1,0:T(8,128)S(1)} %get-tuple-element.37), channel_id=1, source_target_pairs={{0,1},{2,3},{4,5},{6,7},{1,0},{3,2},{5,4},{7,6},{8,9},{10,11},{12,... | collective-permute-start | bytes 98312 | tf_op jit(solution)/shard_map/ppermute | solution.py:295
  15.8 6.7 %collective-permute-start.4 = (f32[4,16,128]{2,1,0:T(8,128)S(1)}, f32[4,16,128]{2,1,0:T(8,128)S(1)}, u32[]{:S(2)}, u32[]{:S(2)}) collective-permute-start(f32[4,16,128]{2,1,0:T(8,128)S(1)} %get-tuple-element.38), channel_id=1, source_target_pairs={{1,2},{3,4},{5,6},{2,1},{4,3},{6,5},{9,10},{11,12},{13,14},{10,9},... | collective-permute-start | bytes 98312 | tf_op jit(solution)/shard_map/ppermute | solution.py:295
  55.9 2.2 %copy-start.2 = (f32[4,16,128,128]{3,2,1,0:T(8,128)S(1)}, f32[4,16,128,128]{3,2,1,0:T(8,128)}, u32[]{:S(2)}) copy-start(f32[4,16,128,128]{3,2,1,0:T(8,128)} %refs_2_.3) | copy-start | bytes 12582916
  58.1 6.3 %copy-start.3 = (f32[4,16,128,128]{3,2,1,0:T(8,128)S(1)}, f32[4,16,128,128]{3,2,1,0:T(8,128)}, u32[]{:S(2)}) copy-start(f32[4,16,128,128]{3,2,1,0:T(8,128)} %refs_2_.3) | copy-start | bytes 12582916
  59.1 46.2 %collective-permute-start.16 = (f32[16,64,128]{2,1,0:T(8,128)S(1)}, f32[16,64,128]{2,1,0:T(8,128)S(1)}, u32[]{:S(2)}, u32[]{:S(2)}) collective-permute-start(f32[16,64,128]{2,1,0:T(8,128)S(1)} %shard_map.42.refs_0_.refs_8_), channel_id=1, source_target_pairs={{0,32},{32,0},{1,33},{33,1},{2,34},{34,2},{3,35},{35,3},{4,36},{36... | collective-permute-start | bytes 1572872 | tf_op jit(solution)/shard_map/ppermute | solution.py:295
  67.8 19.4 %collective-permute-start.7 = (f32[3,128,128]{2,1,0:T(8,128)S(1)}, f32[3,128,128]{2,1,0:T(8,128)S(1)}, u32[]{:S(2)}, u32[]{:S(2)}) collective-permute-start(f32[3,128,128]{2,1,0:T(8,128)S(1)} %get-tuple-element.39), channel_id=1, source_target_pairs={{0,8},{16,24},{8,0},{24,16},{1,9},{17,25},{9,1},{25,17},{2,10},{18... | collective-permute-start | bytes 589832 | tf_op jit(solution)/shard_map/ppermute | solution.py:295
  67.9 19.3 %collective-permute-start.8 = (f32[3,128,128]{2,1,0:T(8,128)S(1)}, f32[3,128,128]{2,1,0:T(8,128)S(1)}, u32[]{:S(2)}, u32[]{:S(2)}) collective-permute-start(f32[3,128,128]{2,1,0:T(8,128)S(1)} %get-tuple-element.40), channel_id=1, source_target_pairs={{8,16},{16,8},{9,17},{17,9},{10,18},{18,10},{11,19},{19,11},{12,20... | collective-permute-start | bytes 589832 | tf_op jit(solution)/shard_map/ppermute | solution.py:295
  68.6 13.4 %collective-permute-start.9 = (f32[3,16,128]{2,1,0:T(8,128)S(1)}, f32[3,16,128]{2,1,0:T(8,128)S(1)}, u32[]{:S(2)}, u32[]{:S(2)}) collective-permute-start(f32[3,16,128]{2,1,0:T(8,128)S(1)} %get-tuple-element.41), channel_id=1, source_target_pairs={{0,1},{2,3},{4,5},{6,7},{1,0},{3,2},{5,4},{7,6},{8,9},{10,11},{12,... | collective-permute-start | bytes 73736 | tf_op jit(solution)/shard_map/ppermute | solution.py:295
  77.3 9.9 %collective-permute-start.10 = (f32[3,16,128]{2,1,0:T(8,128)S(1)}, f32[3,16,128]{2,1,0:T(8,128)S(1)}, u32[]{:S(2)}, u32[]{:S(2)}) collective-permute-start(f32[3,16,128]{2,1,0:T(8,128)S(1)} %get-tuple-element.42), channel_id=1, source_target_pairs={{1,2},{3,4},{5,6},{2,1},{4,3},{6,5},{9,10},{11,12},{13,14},{10,9},... | collective-permute-start | bytes 73736 | tf_op jit(solution)/shard_map/ppermute | solution.py:295
  82.0 27.9 %collective-permute-start.5 = (f32[16,64,128]{2,1,0:T(8,128)S(1)}, f32[16,64,128]{2,1,0:T(8,128)S(1)}, u32[]{:S(2)}, u32[]{:S(2)}) collective-permute-start(f32[16,64,128]{2,1,0:T(8,128)S(1)} %shard_map.41.refs_1_.refs_0_.refs_8_), channel_id=1, source_target_pairs={{0,32},{32,0},{1,33},{33,1},{2,34},{34,2},{3,35},{35,3},{4,36},{36... | collective-permute-start | bytes 1572872 | tf_op jit(solution)/shard_map/ppermute | solution.py:295
  90.6 14.6 %collective-permute-start.11 = (f32[4,128,128]{2,1,0:T(8,128)S(1)}, f32[4,128,128]{2,1,0:T(8,128)S(1)}, u32[]{:S(2)}, u32[]{:S(2)}) collective-permute-start(f32[4,128,128]{2,1,0:T(8,128)S(1)} %get-tuple-element.43), channel_id=1, source_target_pairs={{0,8},{16,24},{8,0},{24,16},{1,9},{17,25},{9,1},{25,17},{2,10},{18... | collective-permute-start | bytes 786440 | tf_op jit(solution)/shard_map/ppermute | solution.py:295
  90.7 14.5 %collective-permute-start.12 = (f32[4,128,128]{2,1,0:T(8,128)S(1)}, f32[4,128,128]{2,1,0:T(8,128)S(1)}, u32[]{:S(2)}, u32[]{:S(2)}) collective-permute-start(f32[4,128,128]{2,1,0:T(8,128)S(1)} %get-tuple-element.44), channel_id=1, source_target_pairs={{8,16},{16,8},{9,17},{17,9},{10,18},{18,10},{11,19},{19,11},{12,20... | collective-permute-start | bytes 786440 | tf_op jit(solution)/shard_map/ppermute | solution.py:295
  91.4 6.8 %collective-permute-start.13 = (f32[4,16,128]{2,1,0:T(8,128)S(1)}, f32[4,16,128]{2,1,0:T(8,128)S(1)}, u32[]{:S(2)}, u32[]{:S(2)}) collective-permute-start(f32[4,16,128]{2,1,0:T(8,128)S(1)} %get-tuple-element.45), channel_id=1, source_target_pairs={{0,1},{2,3},{4,5},{6,7},{1,0},{3,2},{5,4},{7,6},{8,9},{10,11},{12,... | collective-permute-start | bytes 98312 | tf_op jit(solution)/shard_map/ppermute | solution.py:295
  98.2 7.0 %collective-permute-start.14 = (f32[4,16,128]{2,1,0:T(8,128)S(1)}, f32[4,16,128]{2,1,0:T(8,128)S(1)}, u32[]{:S(2)}, u32[]{:S(2)}) collective-permute-start(f32[4,16,128]{2,1,0:T(8,128)S(1)} %get-tuple-element.46), channel_id=1, source_target_pairs={{1,2},{3,4},{5,6},{2,1},{4,3},{6,5},{9,10},{11,12},{13,14},{10,9},... | collective-permute-start | bytes 98312 | tf_op jit(solution)/shard_map/ppermute | solution.py:295
  106.2 45.5 %collective-permute-start.22 = (f32[16,64,128]{2,1,0:T(8,128)S(1)}, f32[16,64,128]{2,1,0:T(8,128)S(1)}, u32[]{:S(2)}, u32[]{:S(2)}) collective-permute-start(f32[16,64,128]{2,1,0:T(8,128)S(1)} %shard_map.44.refs_0_.refs_8_), channel_id=1, source_target_pairs={{0,32},{32,0},{1,33},{33,1},{2,34},{34,2},{3,35},{35,3},{4,36},{36... | collective-permute-start | bytes 1572872 | tf_op jit(solution)/shard_map/ppermute | solution.py:295
  114.3 37.4 %collective-permute-start.17 = (f32[4,128,128]{2,1,0:T(8,128)S(1)}, f32[4,128,128]{2,1,0:T(8,128)S(1)}, u32[]{:S(2)}, u32[]{:S(2)}) collective-permute-start(f32[4,128,128]{2,1,0:T(8,128)S(1)} %get-tuple-element.47), channel_id=1, source_target_pairs={{0,8},{16,24},{8,0},{24,16},{1,9},{17,25},{9,1},{25,17},{2,10},{18... | collective-permute-start | bytes 786440 | tf_op jit(solution)/shard_map/ppermute | solution.py:295
  118.6 33.2 %collective-permute-start.18 = (f32[4,128,128]{2,1,0:T(8,128)S(1)}, f32[4,128,128]{2,1,0:T(8,128)S(1)}, u32[]{:S(2)}, u32[]{:S(2)}) collective-permute-start(f32[4,128,128]{2,1,0:T(8,128)S(1)} %get-tuple-element.48), channel_id=1, source_target_pairs={{8,16},{16,8},{9,17},{17,9},{10,18},{18,10},{11,19},{19,11},{12,20... | collective-permute-start | bytes 786440 | tf_op jit(solution)/shard_map/ppermute | solution.py:295
  119.2 44.5 %collective-permute-start.15 = (f32[16,64,128]{2,1,0:T(8,128)S(1)}, f32[16,64,128]{2,1,0:T(8,128)S(1)}, u32[]{:S(2)}, u32[]{:S(2)}) collective-permute-start(f32[16,64,128]{2,1,0:T(8,128)S(1)} %shard_map.43.refs_1_.refs_0_.refs_8_), channel_id=1, source_target_pairs={{0,32},{32,0},{1,33},{33,1},{2,34},{34,2},{3,35},{35,3},{4,36},{36... | collective-permute-start | bytes 1572872 | tf_op jit(solution)/shard_map/ppermute | solution.py:295
  121.4 23.7 %collective-permute-start.19 = (f32[4,16,128]{2,1,0:T(8,128)S(1)}, f32[4,16,128]{2,1,0:T(8,128)S(1)}, u32[]{:S(2)}, u32[]{:S(2)}) collective-permute-start(f32[4,16,128]{2,1,0:T(8,128)S(1)} %get-tuple-element.49), channel_id=1, source_target_pairs={{0,1},{2,3},{4,5},{6,7},{1,0},{3,2},{5,4},{7,6},{8,9},{10,11},{12,... | collective-permute-start | bytes 98312 | tf_op jit(solution)/shard_map/ppermute | solution.py:295
  145.1 6.7 %collective-permute-start.20 = (f32[4,16,128]{2,1,0:T(8,128)S(1)}, f32[4,16,128]{2,1,0:T(8,128)S(1)}, u32[]{:S(2)}, u32[]{:S(2)}) collective-permute-start(f32[4,16,128]{2,1,0:T(8,128)S(1)} %get-tuple-element.50), channel_id=1, source_target_pairs={{1,2},{3,4},{5,6},{2,1},{4,3},{6,5},{9,10},{11,12},{13,14},{10,9},... | collective-permute-start | bytes 98312 | tf_op jit(solution)/shard_map/ppermute | solution.py:295
  152.8 27.8 %collective-permute-start.29 = (f32[16,64,128]{2,1,0:T(8,128)S(1)}, f32[16,64,128]{2,1,0:T(8,128)S(1)}, u32[]{:S(2)}, u32[]{:S(2)}) collective-permute-start(f32[16,64,128]{2,1,0:T(8,128)S(1)} %shard_map.46.refs_0_.refs_8_), channel_id=1, source_target_pairs={{0,32},{32,0},{1,33},{33,1},{2,34},{34,2},{3,35},{35,3},{4,36},{36... | collective-permute-start | bytes 1572872 | tf_op jit(solution)/shard_map/ppermute | solution.py:295
  157.2 31.1 %collective-permute-start.32 = (f32[2,256,128]{2,1,0:T(8,128)S(1)}, f32[2,256,128]{2,1,0:T(8,128)S(1)}, u32[]{:S(2)}, u32[]{:S(2)}) collective-permute-start(f32[2,256,128]{2,1,0:T(8,128)S(1)} %get-tuple-element.62), channel_id=1, source_target_pairs={{0,8},{16,24},{8,0},{24,16},{1,9},{17,25},{9,1},{25,17},{2,10},{18... | collective-permute-start | bytes 786440 | tf_op jit(solution)/shard_map/ppermute | solution.py:295
  165.3 13.5 %collective-permute-start.25 = (f32[1,16,128]{2,1,0:T(8,128)S(1)}, f32[1,16,128]{2,1,0:T(8,128)S(1)}, u32[]{:S(2)}, u32[]{:S(2)}) collective-permute-start(f32[1,16,128]{2,1,0:T(8,128)S(1)} %get-tuple-element.53), channel_id=1, source_target_pairs={{0,1},{2,3},{4,5},{6,7},{1,0},{3,2},{5,4},{7,6},{8,9},{10,11},{12,... | collective-permute-start | bytes 24584 | tf_op jit(solution)/shard_map/ppermute | solution.py:295
  169.9 9.7 %collective-permute-start.26 = (f32[1,16,128]{2,1,0:T(8,128)S(1)}, f32[1,16,128]{2,1,0:T(8,128)S(1)}, u32[]{:S(2)}, u32[]{:S(2)}) collective-permute-start(f32[1,16,128]{2,1,0:T(8,128)S(1)} %get-tuple-element.54), channel_id=1, source_target_pairs={{1,2},{3,4},{5,6},{2,1},{4,3},{6,5},{9,10},{11,12},{13,14},{10,9},... | collective-permute-start | bytes 24584 | tf_op jit(solution)/shard_map/ppermute | solution.py:295
  174.5 19.5 %collective-permute-start.21 = (f32[16,64,128]{2,1,0:T(8,128)S(1)}, f32[16,64,128]{2,1,0:T(8,128)S(1)}, u32[]{:S(2)}, u32[]{:S(2)}) collective-permute-start(f32[16,64,128]{2,1,0:T(8,128)S(1)} %shard_map.45.refs_1_.refs_0_.refs_8_), channel_id=1, source_target_pairs={{0,32},{32,0},{1,33},{33,1},{2,34},{34,2},{3,35},{35,3},{4,36},{36... | collective-permute-start | bytes 1572872 | tf_op jit(solution)/shard_map/ppermute | solution.py:295
  178.8 1.8 collective-permute-start.23
  179.6 0.9 collective-permute-start.24
  181.7 13.5 %collective-permute-start.30 = (f32[2,192,128]{2,1,0:T(8,128)S(1)}, f32[2,192,128]{2,1,0:T(8,128)S(1)}, u32[]{:S(2)}, u32[]{:S(2)}) collective-permute-start(f32[2,192,128]{2,1,0:T(8,128)S(1)} %constant_dynamic-update-slice_fusion), channel_id=1, source_target_pairs={{0,8},{16,24},{8,0},{24,16},{1,9},{17,25},{9,1},{25,17},{2,10},{18... | collective-permute-start | bytes 589832 | tf_op jit(solution)/shard_map/ppermute | solution.py:295
  188.4 10.7 %collective-permute-start.33 = (f32[2,256,128]{2,1,0:T(8,128)S(1)}, f32[2,256,128]{2,1,0:T(8,128)S(1)}, u32[]{:S(2)}, u32[]{:S(2)}) collective-permute-start(f32[2,256,128]{2,1,0:T(8,128)S(1)} %pad_maximum_fusion.refs_1_), channel_id=1, source_target_pairs={{0,16},{8,24},{16,0},{24,8},{1,17},{9,25},{17,1},{25,9},{2,18},{10... | collective-permute-start | bytes 786440 | tf_op jit(solution)/shard_map/ppermute | solution.py:295
  195.0 1.3 collective-permute-start.27
  195.3 9.4 %collective-permute-start.31 = (f32[2,192,128]{2,1,0:T(8,128)S(1)}, f32[2,192,128]{2,1,0:T(8,128)S(1)}, u32[]{:S(2)}, u32[]{:S(2)}) collective-permute-start(f32[2,192,128]{2,1,0:T(8,128)S(1)} %pad_maximum_fusion.1.refs_2_), channel_id=1, source_target_pairs={{0,16},{8,24},{16,0},{24,8},{1,17},{9,25},{17,1},{25,9},{2,18},{10... | collective-permute-start | bytes 589832 | tf_op jit(solution)/shard_map/ppermute | solution.py:295
  196.4 10.7 %collective-permute-start.28 = (f32[2,64,128]{2,1,0:T(8,128)S(1)}, f32[2,64,128]{2,1,0:T(8,128)S(1)}, u32[]{:S(2)}, u32[]{:S(2)}) collective-permute-start(f32[2,64,128]{2,1,0:T(8,128)S(1)} %pad_maximum_fusion.2.refs_1_), channel_id=1, source_target_pairs={{0,16},{8,24},{16,0},{24,8},{1,17},{9,25},{17,1},{25,9},{2,18},{10... | collective-permute-start | bytes 196616 | tf_op jit(solution)/shard_map/ppermute | solution.py:295
